TPU v7x, 128 devices: a whole 4x4x4 slice. The times are simulated.
128 devices in a mesh: gx: 16 (over y, x), gy: 8 (over z, core).
Axes of the slice: x: 4, y: 4, z: 4, core: 2. Of those that a mesh axis runs over, the one named last changes fastest.
Arguments:
- point_feats: bfloat16 [1048576, 128], P(('gx', 'gy')), may hold values from -6 to 6
- point_tile: int32 [1048576, 1], P(('gx', 'gy')), may hold values from 0 to 127; in each aligned block of 8192 rows (0 to 8191, 8192 to 16383, ...) at most 80 rows name the same one
- point_cell: int32 [1048576], P(('gx', 'gy')), may hold values from 0 to 4095
- point_count: int32 [128], P(('gx', 'gy')), may hold values from 6144 to 8192, as said below
- conv_weight: bfloat16 [3, 3, 128, 128], replicated, may hold values from -0.1875 to 0.1875
- conv_bias: float32 [128], replicated, may hold values from -3 to 3
Outputs:
- bev_map: bfloat16 [256, 2048, 128], P('gx', 'gy')
- conv_out: bfloat16 [256, 2048, 128], P('gx', 'gy')
Inputs may be any that keep to these rules, and one draw needn't show every extreme that they name: `point_tile`: among the 8192 rows of one device no tile is named by more than 80 rows, a bound that some block reaches. `point_count`: only slots below a device's count are live; some device has all 8192 slots live.
All inputs are finite; a program needn't handle non-finite values.
Results may differ from a plain program's by a relative error of at most 0.0045.
Values may be sent and summed in bfloat16 or wider, within the bound.
No kernel may reach another device: no remote copies, remote signals or barrier semaphores. Data moves between devices by JAX's collectives and lax.ppermute only.
A program may use at most 64 MiB of HBM per device.

v0:
```python
import jax
import jax.numpy as jnp
from jax import lax
from jax.sharding import PartitionSpec as P

COLS_DEV = 256
ROWS_DEV = 16


def with_halo(cells, sides, width):
    for axis, dim in sides:
        count = lax.axis_size(axis)
        ends = count - 1
        head = lax.slice_in_dim(cells, 0, width, axis=dim)
        tail = lax.slice_in_dim(cells, cells.shape[dim] - width, cells.shape[dim], axis=dim)
        cells = jnp.concatenate(
            [
                lax.ppermute(tail, axis, [(i, (i + 1) % count) for i in range(ends)]),
                cells,
                lax.ppermute(head, axis, [((i + 1) % count, i) for i in range(ends)]),
            ],
            axis=dim,
        )
    return cells


def shards(point_feats, point_tile, point_cell, point_count, conv_weight, conv_bias):
    size_gx = lax.axis_size("gx")
    size_gy = lax.axis_size("gy")
    devices = size_gx * size_gy
    points = point_feats.shape[0]
    channels = point_feats.shape[1]
    capacity = 5 * points // (4 * devices)
    slots = devices * capacity
    target = point_tile[:, 0]
    live = jnp.arange(points, dtype=jnp.int32) < point_count[0]
    hits = (target[:, None] == jnp.arange(devices, dtype=jnp.int32)[None, :]) & live[:, None]
    blk = min(128, points)
    nblk = points // blk
    inner_idx = jnp.arange(blk, dtype=jnp.int32)
    lower = (inner_idx[:, None] >= inner_idx[None, :]).astype(jnp.bfloat16)
    hit_blocks = hits.astype(jnp.bfloat16).reshape(nblk, blk, devices)
    inner = jnp.einsum("ij,bjd->bid", lower, hit_blocks, preferred_element_type=jnp.float32)
    totals = inner[:, -1, :]
    before = jnp.cumsum(totals, axis=0) - totals
    ranks = (inner + before[:, None, :]).reshape(points, devices)
    place = jnp.sum(jnp.where(hits, ranks, 0.0), axis=1).astype(jnp.int32) - 1
    position = jnp.where(live, target * capacity + place, slots)
    slot_ids = jnp.arange(slots, dtype=jnp.int32)

    def pick(found, item):
        pos_block, first = item
        matches = pos_block[:, None] == slot_ids[None, :]
        owners = (first + inner_idx + 1)[:, None]
        return (found + jnp.sum(jnp.where(matches, owners, 0), axis=0), None)

    starts = jnp.arange(nblk, dtype=jnp.int32) * blk
    source, unused = lax.scan(
        pick, jnp.zeros((slots,), jnp.int32), (position.reshape(nblk, blk), starts)
    )
    filled = source > 0
    source_row = jnp.maximum(source - 1, 0)
    send_feats = jnp.where(
        filled[:, None], jnp.take(point_feats, source_row, axis=0), jnp.zeros((), jnp.bfloat16)
    )
    send_cells = jnp.where(filled, jnp.take(point_cell, source_row, axis=0), -1)
    got_feats, got_cells = (
        lax.all_to_all(
            send_feats.reshape(devices, capacity, channels),
            ("gx", "gy"),
            split_axis=0,
            concat_axis=0,
            tiled=True,
        ),
        lax.all_to_all(
            send_cells.reshape(devices, capacity),
            ("gx", "gy"),
            split_axis=0,
            concat_axis=0,
            tiled=True,
        ),
    )
    got_feats = got_feats.reshape(-1, channels)
    got_cells = got_cells.reshape(-1)
    col_ids = jnp.arange(COLS_DEV, dtype=jnp.int32)

    def one_row(row):
        wanted = row * COLS_DEV + col_ids
        onehot = (wanted[:, None] == got_cells[None, :]).astype(jnp.bfloat16)
        return jnp.dot(onehot, got_feats, preferred_element_type=jnp.float32)

    sums = lax.map(one_row, jnp.arange(ROWS_DEV, dtype=jnp.int32))
    bev_map = sums.astype(jnp.bfloat16)
    padded = with_halo(bev_map, (("gx", 0), ("gy", 1)), 1)
    total = jnp.zeros((ROWS_DEV, COLS_DEV, channels), jnp.float32)
    for shift_row in range(3):
        for shift_col in range(3):
            window = padded[shift_row : shift_row + ROWS_DEV, shift_col : shift_col + COLS_DEV]
            total = total + jnp.einsum(
                "rcd,de->rce",
                window,
                conv_weight[shift_row, shift_col],
                preferred_element_type=jnp.float32,
            )
    conv_out = jax.nn.relu(total + conv_bias).astype(jnp.bfloat16)
    return (bev_map, conv_out)


def solution(mesh):
    in_specs = (
        P(("gx", "gy"), None),
        P(("gx", "gy"), None),
        P(("gx", "gy")),
        P(("gx", "gy")),
        P(),
        P(),
    )
    out_specs = (P("gx", "gy", None), P("gx", "gy", None))
    return jax.shard_map(shards, mesh=mesh, in_specs=in_specs, out_specs=out_specs, check_vma=False)
```

profile of v0, /device:TPU:6, one launch (start us, length us, event | category | flops | bytes accessed | tf_op | source)
XLA Modules:
  0.0 401.4 jit_solution(16874526411669957181)
XLA Ops:
  1.5 10.3 %fusion.20 = f32[64,128,128]{2,1,0:T(8,128)S(1)} fusion(s32[64,128]{1,0:T(8,128)} %bitcast.88, pred[64,128]{1,0:T(8,128)(4,1)S(1)} %add_compare_fusion), kind=kOutput, calls=%fused_computation.23 | convolution fusion | flops 270548992 | bytes 4235264 | tf_op jit(solution)/shard_map/ij,bjd->bid/dot_general | solution.py:43
  11.9 4.1 %select_reduce_fusion.1 = f32[64,128]{1,0:T(8,128)S(1)} fusion(f32[64,128,128]{2,1,0:T(8,128)S(1)} %fusion.20, f32[64,128]{1,0:T(8,128)S(1)} %bitcast.92, s32[64,128]{1,0:T(8,128)S(1)} %bitcast.89, pred[64,128]{1,0:T(8,128)(4,1)S(1)} %add_compare_fusion), kind=kLoop, calls=%fused_computation.18 | loop fusion | flops 5234688 | bytes 4300800 | tf_op jit(solution)/shard_map/reduce_sum | solution.py:47
  16.1 134.9 %while.25 = (s32[]{:T(128)}, s32[10240]{0:T(1024)S(1)}, s32[64,128]{1,0:T(8,128)S(1)}, s32[64]{0:T(128)S(1)}) while((s32[]{:T(128)}, s32[10240]{0:T(1024)S(1)}, s32[64,128]{1,0:T(8,128)S(1)}, s32[64]{0:T(128)S(1)}) %tuple.57), condition=%wide.region_4.5_spmd.clone.clone, body=%wide.region_2.4_spmd.clone.sunk.clone | while | flops 3942659 | bytes 166483 | solution.py:58
  17.4 0.8 select_reduce_fusion.4
  23.7 0.8 select_reduce_fusion.4
  25.8 0.8 select_reduce_fusion.4
  32.1 0.8 select_reduce_fusion.4
  34.2 0.8 select_reduce_fusion.4
  40.6 0.8 select_reduce_fusion.4
  42.7 0.8 select_reduce_fusion.4
  46.9 0.8 select_reduce_fusion.4
  49.0 0.8 select_reduce_fusion.4
  51.1 0.8 select_reduce_fusion.4
  55.3 0.8 select_reduce_fusion.4
  57.4 0.8 select_reduce_fusion.4
  63.7 0.8 select_reduce_fusion.4
  65.8 0.8 select_reduce_fusion.4
  72.2 0.8 select_reduce_fusion.4
  151.0 56.8 %gather_fusion = s32[10240]{0:T(1024)S(1)} fusion(s32[8192]{0:T(1024)S(1)} %copy-done.1, s32[10240]{0:T(1024)S(1)} %fusion.49), kind=kCustom, calls=%fused_computation | custom fusion | bytes 122880 | tf_op jit(solution)/shard_map/jit(_take)/gather | solution.py:66
  208.5 10.5 %all-to-all-start = ((s32[128,1,80]{2,1,0:T(1,128)}), s32[128,1,80]{2,1,0:T(1,128)S(1)}, u32[]{:S(2)}, u32[]{:S(2)}) async-start(s32[128,1,80]{2,1,0:T(1,128)} %bitcast.5), calls=%async_computation | async-start | bytes 131072 | tf_op jit(solution)/shard_map/all_to_all | solution.py:75
  219.2 36.1 %gather_fusion.1 = bf16[10240,128]{1,0:T(8,128)(2,1)} fusion(bf16[8192,128]{1,0:T(8,128)(2,1)S(1)} %copy-done, s32[10240]{0:T(1024)S(1)} %fusion.49), kind=kCustom, calls=%fused_computation.1 | custom fusion | bytes 5283840 | tf_op jit(solution)/shard_map/jit(_take)/gather | solution.py:64
  255.4 5.7 %select_select_fusion = bf16[128,80,128]{2,1,0:T(8,128)(2,1)} fusion(bf16[128,80,128]{2,1,0:T(8,128)(2,1)} %bitcast.87, pred[128,80]{1,0:T(8,128)(4,1)S(1)} %broadcast_in_dim.81, pred[128,80]{1,0:T(8,128)(4,1)S(1)} %broadcast_in_dim.79), kind=kLoop, calls=%fused_computation.22 | loop fusion | flops 2621440 | bytes 5263360 | tf_op jit(solution)/shard_map/jit(_where)/select_n | solution.py:63
  261.1 10.2 %all-to-all-start.1 = ((bf16[128,80,128]{2,1,0:T(8,128)(2,1)}), bf16[128,80,128]{2,1,0:T(8,128)(2,1)}, u32[]{:S(2)}, u32[]{:S(2)}) async-start(bf16[128,80,128]{2,1,0:T(8,128)(2,1)} %select_select_fusion), calls=%async_computation.1 | async-start | bytes 5242880 | tf_op jit(solution)/shard_map/all_to_all | solution.py:68
  271.4 34.8 %all-to-all-done.1 = bf16[128,80,128]{2,1,0:T(8,128)(2,1)} async-done(((bf16[128,80,128]{2,1,0:T(8,128)(2,1)}), bf16[128,80,128]{2,1,0:T(8,128)(2,1)}, u32[]{:S(2)}, u32[]{:S(2)}) %all-to-all-start.1) | async-done | bytes 2621472 | tf_op jit(solution)/shard_map/all_to_all | solution.py:68
  306.2 73.6 %while.26 = (s32[]{:T(128)}, bf16[16,256,128]{2,1,0:T(8,128)(2,1)S(1)}, s32[16]{0:T(128)S(1)}, bf16[10240,128]{1,0:T(8,128)(2,1)}, s32[10240]{0:T(1024)S(1)}, /*index=5*/s32[1]{0:T(128)}) while((s32[]{:T(128)}, bf16[16,256,128]{2,1,0:T(8,128)(2,1)S(1)}, s32[16]{0:T(128)S(1)}, bf16[10240,128]{1,0:T(8,128)(2,1)}, ...), condition=%wide.wide.region_6.7_spmd.clone.clone, body=%wide.wide.region_5.6_spmd.clone.sunk.clone | while | flops 673710336 | bytes 2795621 | solution.py:92
  307.4 3.3 fusion.91
  312.0 3.3 fusion.91
  316.6 3.3 fusion.91
  321.2 3.3 fusion.91
  325.8 3.3 fusion.91
  330.4 3.3 fusion.91
  335.0 3.3 fusion.91
  339.6 3.3 fusion.91
  344.2 3.3 fusion.91
  348.8 3.3 fusion.91
  353.4 3.3 fusion.91
  358.0 3.3 fusion.91
  362.6 3.3 fusion.91
  367.2 3.3 fusion.91
  371.8 3.3 fusion.91
  376.4 3.3 fusion.91
  379.8 3.9 collective-permute-start
  383.7 2.0 collective-permute-start.1
  386.1 5.8 %collective-permute-done.1 = bf16[1,256,128]{2,1,0:T(8,128)(2,1)S(1)} collective-permute-done((bf16[1,256,128]{2,1,0:T(8,128)(2,1)S(1)}, bf16[1,256,128]{2,1,0:T(8,128)(2,1)S(1)}, u32[]{:S(2)}, u32[]{:S(2)}) %collective-permute-start.1) | collective-permute-done | bytes 65568 | tf_op jit(solution)/shard_map/ppermute | solution.py:20
  392.0 1.3 collective-permute-start.2
  393.3 1.3 collective-permute-start.3
  395.4 0.9 collective-permute-done.3
  399.4 2.1 maximum_convert_fusion
  (376 shorter events, 135.2 us)
Async XLA Ops:
  0.6 218.6 %copy-start = (bf16[8192,128]{1,0:T(8,128)(2,1)S(1)}, bf16[8192,128]{1,0:T(8,128)(2,1)}, u32[]{:S(2)}) copy-start(bf16[8192,128]{1,0:T(8,128)(2,1)} %param.10) | copy-start | bytes 6291460
  1.5 10.4 %copy-start.4 = (s32[8192,1]{0,1:T(1,128)S(1)}, s32[8192,1]{0,1:T(1,128)}, u32[]{:S(2)}) copy-start(s32[8192,1]{0,1:T(1,128)} %param.11) | copy-start | bytes 98308
  11.9 139.1 %copy-start.1 = (s32[8192]{0:T(1024)S(1)}, s32[8192]{0:T(1024)}, u32[]{:S(2)}) copy-start(s32[8192]{0:T(1024)} %param.12) | copy-start | bytes 98308
  208.5 52.6 %all-to-all-start = ((s32[128,1,80]{2,1,0:T(1,128)}), s32[128,1,80]{2,1,0:T(1,128)S(1)}, u32[]{:S(2)}, u32[]{:S(2)}) async-start(s32[128,1,80]{2,1,0:T(1,128)} %bitcast.5), calls=%async_computation | async-start | bytes 131072 | tf_op jit(solution)/shard_map/all_to_all | solution.py:75
  261.1 45.0 %all-to-all-start.1 = ((bf16[128,80,128]{2,1,0:T(8,128)(2,1)}), bf16[128,80,128]{2,1,0:T(8,128)(2,1)}, u32[]{:S(2)}, u32[]{:S(2)}) async-start(bf16[128,80,128]{2,1,0:T(8,128)(2,1)} %select_select_fusion), calls=%async_computation.1 | async-start | bytes 5242880 | tf_op jit(solution)/shard_map/all_to_all | solution.py:68
  306.2 79.5 %copy-start.3 = (bf16[3,3,128,128]{3,2,1,0:T(8,128)(2,1)S(1)}, bf16[3,3,128,128]{3,2,1,0:T(8,128)(2,1)}, u32[]{:S(2)}) copy-start(bf16[3,3,128,128]{3,2,1,0:T(8,128)(2,1)} %param.14) | copy-start | bytes 884740
  379.8 16.6 %copy-start.2 = (bf16[16,256,128]{2,1,0:T(8,128)(2,1)}, bf16[16,256,128]{2,1,0:T(8,128)(2,1)S(1)}, u32[]{:S(2)}) copy-start(bf16[16,256,128]{2,1,0:T(8,128)(2,1)S(1)} %get-tuple-element.67) | copy-start | bytes 3145732
  379.8 6.3 %collective-permute-start = (bf16[1,256,128]{2,1,0:T(8,128)(2,1)S(1)}, bf16[1,256,128]{2,1,0:T(8,128)(2,1)S(1)}, u32[]{:S(2)}, u32[]{:S(2)}) collective-permute-start(bf16[1,256,128]{2,1,0:T(8,128)(2,1)S(1)} %get-tuple-element.124), channel_id=1, source_target_pairs={{0,8},{8,16},{16,24},{24,32},{32,40},{40,48},{48,56},{56,64},{64,7... | collective-permute-start | bytes 196616 | tf_op jit(solution)/shard_map/ppermute | solution.py:18
  383.7 8.3 %collective-permute-start.1 = (bf16[1,256,128]{2,1,0:T(8,128)(2,1)S(1)}, bf16[1,256,128]{2,1,0:T(8,128)(2,1)S(1)}, u32[]{:S(2)}, u32[]{:S(2)}) collective-permute-start(bf16[1,256,128]{2,1,0:T(8,128)(2,1)S(1)} %get-tuple-element.125), channel_id=1, source_target_pairs={{8,0},{16,8},{24,16},{32,24},{40,32},{48,40},{56,48},{64,56},{72,6... | collective-permute-start | bytes 196616 | tf_op jit(solution)/shard_map/ppermute | solution.py:20
  392.0 3.4 collective-permute-start.2
  393.3 3.1 collective-permute-start.3
  398.7 0.7 copy-start.5
where the time goes:
time: 405 us; the launch traced here: 401 us
  local copies, waits for them, and re-layouts  146 us (36%)
  other arithmetic  100 us (25%)
  matrix products  69.2 us (17%)
  waiting for transfers between devices  41.5 us (10%)
  starting transfers between devices  29.1 us (7%)
  loops' own time  13.9 us (3%)
    gather x1, local copies, waits for them, and re-layouts, shards(): send_cells = jnp.where(filled, jnp.take(point_cell, source_row, axis=0), -1)  56.8 us
    dot_general x16, matrix products, one_row(): return jnp.dot(onehot, got_feats, preferred_element_type=jnp.float32)  53.4 us
    reduce_sum x64, other arithmetic, pick(): return (found + jnp.sum(jnp.where(matches, owners, 0), axis=0), None)  48.8 us
    dynamic_slice x64, local copies, waits for them, and re-layouts, shards(): lax.scan(pick, jnp.zeros((slots,), jnp.int32), (position.reshape(nblk, bl...  41.6 us
    add x64, other arithmetic, pick(): owners = (first + inner_idx + 1)[:, None]  39.9 us
    gather x1, local copies, waits for them, and re-layouts, shards(): jnp.take(point_feats, source_row, axis=0)  36.1 us
    all_to_all x1, waiting for transfers between devices, shards(): lax.all_to_all(send_feats.reshape(devices, capacity, channels), ('gx', 'g...  34.8 us
    another operation x1, loops' own time, shards(): sums = lax.map(one_row, jnp.arange(ROWS_DEV, dtype=jnp.int32))  10.8 us
  transfers between devices with their start and end apart: 6, of which 3 were waited for; matrix products, arithmetic and copies ran while one was open for 11% of the time, Pallas kernels for 0%

commit v1 on v0

v1 whole, which is shorter than its diff:
```python
import jax
import jax.numpy as jnp
from jax import lax
from jax.experimental import pallas as pl
from jax.experimental.pallas import tpu as pltpu
from jax.sharding import PartitionSpec as P

COLS_DEV = 256
ROWS_DEV = 16
CELLS = ROWS_DEV * COLS_DEV
LANES = 128
CAP = 80
BLOCK = 88
SUMS = 4
DUMP = CELLS
GROUP = 8


def pack_kernel(
    count_ref, cell_ref, tile_ref, feats_ref, out_ref, rows, slots, pos_v, pos_s, cells_s, cells_v, sem
):
    count = count_ref[0]
    chunks = tile_ref.shape[0]
    tiles = out_ref.shape[0]
    tile_id = lax.broadcasted_iota(jnp.int32, (tiles, LANES), 0)
    lane = lax.broadcasted_iota(jnp.int32, (1, LANES), 1)
    base = (tile_id * LANES - 1).astype(jnp.float32)
    source = lax.broadcasted_iota(jnp.int32, (LANES, 2 * LANES), 0)
    column = lax.broadcasted_iota(jnp.int32, (LANES, 2 * LANES), 1)
    upto = jnp.where((source <= column) | (column >= LANES), 1.0, 0.0).astype(jnp.bfloat16)

    def rank(i, before):
        live = i * LANES + lane < count
        hit = tile_id == jnp.where(live, tile_ref[pl.ds(i, 1), :], -1)
        found = jnp.dot(
            jnp.where(hit, 1.0, 0.0).astype(jnp.bfloat16), upto, preferred_element_type=jnp.float32
        )
        place = found[:, :LANES] + before
        slot = jnp.sum(jnp.where(hit, place, 0.0), axis=0, keepdims=True)
        pos_v[pl.ds(i, 1), :] = jnp.where(live, slot.astype(jnp.int32), tiles * LANES - 1)
        return before + found[:, LANES:]

    total = lax.fori_loop(0, chunks, rank, base) - base
    to_smem = pltpu.make_async_copy(pos_v, pos_s, sem)
    to_smem.start()

    def widen(i, carry):
        at = pl.ds(pl.multiple_of(i * LANES, LANES), LANES)
        rows[at, :] = feats_ref[at, :].astype(jnp.float32)
        return carry

    lax.fori_loop(0, chunks, widen, 0)
    to_smem.wait()

    def move(i, carry):
        def few(g, inner):
            for j in range(GROUP):
                k = g * GROUP + j
                slot = pos_s[i, k]
                cells_s[lax.shift_right_logical(slot, 7), slot & (LANES - 1)] = cell_ref[i, k]
                slots[pl.ds(slot, 1), :] = rows[pl.ds(i * LANES + k, 1), :]
            return inner

        return lax.fori_loop(0, LANES // GROUP, few, carry)

    lax.fori_loop(0, (count + LANES - 1) // LANES, move, 0)
    to_vmem = pltpu.make_async_copy(cells_s, cells_v, sem)
    to_vmem.start()
    to_vmem.wait()
    number = total.astype(jnp.int32)
    cell = jnp.where(lane < number, cells_v[...], DUMP)
    cell = jnp.where(lane == LANES - 1, number, cell)
    slots[pl.ds(CAP, tiles, LANES), :] = lax.shift_right_logical(cell, 6).astype(jnp.float32)
    slots[pl.ds(CAP + 1, tiles, LANES), :] = (cell & 63).astype(jnp.float32)

    def narrow(t, carry):
        out_ref[t] = slots[pl.ds(pl.multiple_of(t * LANES, LANES), BLOCK), :].astype(jnp.bfloat16)
        return carry

    lax.fori_loop(0, tiles, narrow, 0)


def add_kernel(got_ref, out_ref, rows, cells_v, cells_s, sem, *sums):
    sources = got_ref.shape[0]

    def widen(s, carry):
        rows[pl.ds(pl.multiple_of(s * BLOCK, 8), BLOCK), :] = got_ref[s].astype(jnp.float32)
        return carry

    lax.fori_loop(0, sources, widen, 0)
    high = rows[pl.ds(CAP, sources, BLOCK), :].astype(jnp.int32)
    low = rows[pl.ds(CAP + 1, sources, BLOCK), :].astype(jnp.int32)
    cells_v[...] = high * 64 + low
    to_smem = pltpu.make_async_copy(cells_v, cells_s, sem)
    to_smem.start()
    for part in sums:
        part[...] = jnp.zeros_like(part)
    to_smem.wait()

    def one(s, carry):
        number = cells_s[s, LANES - 1]

        def few(g, inner):
            for j in range(GROUP):
                k = g * GROUP + j
                at = pl.ds(cells_s[s, k], 1)
                part = sums[j % SUMS]
                part[at, :] = part[at, :] + rows[pl.ds(s * BLOCK + k, 1), :]
            return inner

        return lax.fori_loop(0, (number + GROUP - 1) // GROUP, few, carry)

    lax.fori_loop(0, sources, one, 0)
    step = 256

    def close(i, carry):
        at = pl.ds(pl.multiple_of(i * step, step), step)
        total = sums[0][at, :]
        for part in sums[1:]:
            total = total + part[at, :]
        out_ref[at, :] = total.astype(jnp.bfloat16)
        return carry

    lax.fori_loop(0, CELLS // step, close, 0)


def with_halo(cells, sides, width):
    for axis, dim in sides:
        count = lax.axis_size(axis)
        ends = count - 1
        head = lax.slice_in_dim(cells, 0, width, axis=dim)
        tail = lax.slice_in_dim(cells, cells.shape[dim] - width, cells.shape[dim], axis=dim)
        cells = jnp.concatenate(
            [
                lax.ppermute(tail, axis, [(i, (i + 1) % count) for i in range(ends)]),
                cells,
                lax.ppermute(head, axis, [((i + 1) % count, i) for i in range(ends)]),
            ],
            axis=dim,
        )
    return cells


VMEM = pl.BlockSpec(memory_space=pltpu.VMEM)
SMEM = pl.BlockSpec(memory_space=pltpu.SMEM)


def pack(point_feats, point_tile, point_cell, point_count, devices):
    points, channels = point_feats.shape
    chunks = points // LANES
    return pl.pallas_call(
        pack_kernel,
        out_shape=jax.ShapeDtypeStruct((devices, BLOCK, channels), jnp.bfloat16),
        in_specs=[SMEM, SMEM, VMEM, VMEM],
        out_specs=VMEM,
        scratch_shapes=[
            pltpu.VMEM((points, channels), jnp.float32),
            pltpu.VMEM((devices * LANES, channels), jnp.float32),
            pltpu.VMEM((chunks, LANES), jnp.int32),
            pltpu.SMEM((chunks, LANES), jnp.int32),
            pltpu.SMEM((devices, LANES), jnp.int32),
            pltpu.VMEM((devices, LANES), jnp.int32),
            pltpu.SemaphoreType.DMA,
        ],
        name="pack",
    )(
        point_count,
        point_cell.reshape(chunks, LANES),
        point_tile.reshape(chunks, LANES),
        point_feats,
    )


def add_up(got):
    devices, block, channels = got.shape
    return pl.pallas_call(
        add_kernel,
        out_shape=jax.ShapeDtypeStruct((CELLS, channels), jnp.bfloat16),
        in_specs=[VMEM],
        out_specs=VMEM,
        scratch_shapes=[
            pltpu.VMEM((devices * block, channels), jnp.float32),
            pltpu.VMEM((devices, LANES), jnp.int32),
            pltpu.SMEM((devices, LANES), jnp.int32),
            pltpu.SemaphoreType.DMA,
        ]
        + [pltpu.VMEM((CELLS + 8, channels), jnp.float32)] * SUMS,
        name="add_up",
    )(got)


def shards(point_feats, point_tile, point_cell, point_count, conv_weight, conv_bias):
    devices = lax.axis_size("gx") * lax.axis_size("gy")
    channels = point_feats.shape[1]
    sent = pack(point_feats, point_tile, point_cell, point_count, devices)
    got = lax.all_to_all(sent, ("gx", "gy"), split_axis=0, concat_axis=0, tiled=True)
    bev_map = add_up(got).reshape(ROWS_DEV, COLS_DEV, channels)
    padded = with_halo(bev_map, (("gx", 0), ("gy", 1)), 1)
    total = lax.conv_general_dilated(
        padded[None],
        conv_weight,
        (1, 1),
        "VALID",
        dimension_numbers=("NHWC", "HWIO", "NHWC"),
        preferred_element_type=jnp.float32,
    )[0]
    conv_out = jax.nn.relu(total + conv_bias).astype(jnp.bfloat16)
    return (bev_map, conv_out)


def solution(mesh):
    in_specs = (
        P(("gx", "gy"), None),
        P(("gx", "gy"), None),
        P(("gx", "gy")),
        P(("gx", "gy")),
        P(),
        P(),
    )
    out_specs = (P("gx", "gy", None), P("gx", "gy", None))
    return jax.shard_map(shards, mesh=mesh, in_specs=in_specs, out_specs=out_specs, check_vma=False)
```

time: 405 us -> 171 us (0.42)
  local copies, waits for them, and re-layouts: 146 us -> 3.61 us
  other arithmetic: 100 us -> 1.37 us
  Pallas kernels: 0 us -> 79.6 us
  matrix products: 69.2 us -> 2.8 us
  blocking collectives: 0 us -> 54.3 us
  waiting for transfers between devices: 41.5 us -> 8.09 us
  loops' own time: 13.9 us -> 0 us
  starting transfers between devices: 29.1 us -> 16.5 us
    gather x2 -> x0, local copies, waits for them, and re-layouts: 92.9 us -> none  [the longest x1 56.8 us: shards(): send_cells = jnp.where(filled, jnp.take(point_cell, source_row, axis=0), -1)]
    pallas_call x0 -> x2, Pallas kernels: none -> 79.6 us  [the longest x1 52.3 us: pack(): pl.pallas_call(pack_kernel, out_shape=jax.ShapeDtypeStruct((devices, BLOC...]
    dot_general x26 -> x0, matrix products: 69.2 us -> none  [the longest x16 53.4 us: one_row(): return jnp.dot(onehot, got_feats, preferred_element_type=jnp.float32)]
    all_to_all x0 -> x1, blocking collectives: none -> 54.3 us  [shards(): lax.all_to_all(sent, ('gx', 'gy'), split_axis=0, concat_axis=0, tiled=True)]
    reduce_sum x65 -> x0, other arithmetic: 52.9 us -> none  [the longest x64 48.8 us: pick(): return (found + jnp.sum(jnp.where(matches, owners, 0), axis=0), None)]
    dynamic_slice x80 -> x0, local copies, waits for them, and re-layouts: 51 us -> none  [the longest x64 41.6 us: shards(): lax.scan(pick, jnp.zeros((slots,), jnp.int32), (position.reshape(nblk, bl...]
    add x144 -> x0, other arithmetic: 40.6 us -> none  [the longest x64 39.9 us: pick(): owners = (first + inner_idx + 1)[:, None]]
    all_to_all x2 -> x0, waiting for transfers between devices: 34.8 us -> none  [the longest x1 34.8 us: shards(): lax.all_to_all(send_feats.reshape(devices, capacity, channels), ('gx', 'g...]
  transfers between devices with their start and end apart: 6 -> 4, of which waited for: 3 -> 2; matrix products, arithmetic and copies ran while one was open for 11% -> 0% of each run, Pallas kernels for 0% -> 0%
where the time goes in v1:
time: 171 us; the launch traced here: 168 us
  Pallas kernels  79.6 us (47%)
  blocking collectives  54.3 us (32%)
  starting transfers between devices  16.5 us (10%)
  waiting for transfers between devices  8.09 us (5%)
  local copies, waits for them, and re-layouts  3.61 us (2%)
  matrix products  2.8 us (2%)
    all_to_all x1, blocking collectives, shards(): lax.all_to_all(sent, ('gx', 'gy'), split_axis=0, concat_axis=0, tiled=True)  54.3 us
    pallas_call x1, Pallas kernels, pack(): pl.pallas_call(pack_kernel, out_shape=jax.ShapeDtypeStruct((devices, BLOC...  52.3 us
    pallas_call x1, Pallas kernels, add_up(): pl.pallas_call(add_kernel, out_shape=jax.ShapeDtypeStruct((CELLS, channel...  27.3 us
    ppermute x2, starting transfers between devices, with_halo(): lax.ppermute(tail, axis, [(i, (i + 1) % count) for i in range(ends)])  13.2 us
    ppermute x2, waiting for transfers between devices, with_halo(): lax.ppermute(head, axis, [((i + 1) % count, i) for i in range(ends)])  8.09 us
  transfers between devices with their start and end apart: 4, of which 2 were waited for; matrix products, arithmetic and copies ran while one was open for 0% of the time, Pallas kernels for 0%

profile of v1, /device:TPU:6, one launch (start us, length us, event | category | flops | bytes accessed | tf_op | source)
XLA Modules:
  0.0 167.7 jit_solution(12351891962203561046)
XLA Ops:
  0.6 0.0 copy-start
  1.3 52.3 %pack.1 = bf16[128,88,128]{2,1,0:T(8,128)(2,1)} custom-call(s32[1]{0:T(128)S(6)} %copy.12.count_ref, s32[64,128]{1,0:T(8,128)} %bitcast.30, s32[64,128]{1,0:T(8,128)} %bitcast.31, bf16[8192,128]{1,0:T(8,128)(2,1)} %feats_ref.1), custom_call_target="tpu_custom_call" | custom-call | tf_op jit(solution)/shard_map/pack/pallas_call | solution.py:151
  53.7 54.3 %all_to_all.5.got_ref = bf16[128,88,128]{2,1,0:T(8,128)(2,1)} all-to-all(bf16[128,88,128]{2,1,0:T(8,128)(2,1)} %pack.1), channel_id=1, replica_groups=mesh['gx'=16,'gy'=8] {'gx','gy'}, dimensions={0} | all-to-all | bytes 5767168 | tf_op jit(solution)/shard_map/all_to_all | solution.py:196
  107.9 27.3 %add_up.1 = bf16[4096,128]{1,0:T(8,128)(2,1)} custom-call(bf16[128,88,128]{2,1,0:T(8,128)(2,1)} %all_to_all.5.got_ref), custom_call_target="tpu_custom_call" | custom-call | tf_op jit(solution)/shard_map/add_up/pallas_call | solution.py:176
  135.2 0.0 copy-start.1
  135.3 1.0 slice_bitcast_fusion.2
  136.2 11.9 %collective-permute-start = (bf16[1,256,128]{2,1,0:T(8,128)(2,1)S(1)}, bf16[1,256,128]{2,1,0:T(8,128)(2,1)S(1)}, u32[]{:S(2)}, u32[]{:S(2)}) collective-permute-start(bf16[1,256,128]{2,1,0:T(8,128)(2,1)S(1)} %get-tuple-element.6), channel_id=1, source_target_pairs={{0,8},{8,16},{16,24},{24,32},{32,40},{40,48},{48,56},{56,64},{64,7... | collective-permute-start | bytes 196616 | tf_op jit(solution)/shard_map/ppermute | solution.py:135
  148.2 1.9 %collective-permute-start.1 = (bf16[1,256,128]{2,1,0:T(8,128)(2,1)S(1)}, bf16[1,256,128]{2,1,0:T(8,128)(2,1)S(1)}, u32[]{:S(2)}, u32[]{:S(2)}) collective-permute-start(bf16[1,256,128]{2,1,0:T(8,128)(2,1)S(1)} %get-tuple-element.7), channel_id=1, source_target_pairs={{8,0},{16,8},{24,16},{32,24},{40,32},{48,40},{56,48},{64,56},{72,6... | collective-permute-start | bytes 196616 | tf_op jit(solution)/shard_map/ppermute | solution.py:137
  150.1 0.0 collective-permute-done
  150.1 6.3 %collective-permute-done.1 = bf16[1,256,128]{2,1,0:T(8,128)(2,1)S(1)} collective-permute-done((bf16[1,256,128]{2,1,0:T(8,128)(2,1)S(1)}, bf16[1,256,128]{2,1,0:T(8,128)(2,1)S(1)}, u32[]{:S(2)}, u32[]{:S(2)}) %collective-permute-start.1) | collective-permute-done | bytes 65568 | tf_op jit(solution)/shard_map/ppermute | solution.py:137
  156.5 0.8 pad_maximum_fusion.2
  157.3 1.3 collective-permute-start.2
  158.6 1.3 collective-permute-start.3
  159.9 0.0 collective-permute-done.2
  159.9 1.8 %collective-permute-done.3 = bf16[18,1,128]{2,1,0:T(2,128)(2,1)S(1)} collective-permute-done((bf16[18,1,128]{2,1,0:T(2,128)(2,1)S(1)}, bf16[18,1,128]{2,1,0:T(2,128)(2,1)S(1)}, u32[]{:S(2)}, u32[]{:S(2)}) %collective-permute-start.3) | collective-permute-done | bytes 4640 | tf_op jit(solution)/shard_map/ppermute | solution.py:137
  161.6 0.0 copy-done.1
  161.6 0.4 maximum_bitcast_fusion
  162.0 0.1 pad
  162.1 0.0 copy-start.3
  162.1 0.4 reshape.21
  162.6 0.2 copy.9
  162.8 0.0 copy-done
  162.8 0.0 copy-done.3
  162.8 2.8 %convolution_select_fusion = f32[16,8,33,128]{3,1,2,0:T(8,128)S(1)} fusion(bf16[3,3,128,128]{3,2,1,0:T(8,128)(2,1)S(1)} %copy-done, bf16[18,1,7,2,128]{4,2,3,0,1:T(8,128)(2,1)S(1)} %slice.28, bf16[18,1,8,33,128]{4,2,3,0,1:T(8,128)(2,1)S(1)} %copy.9, pred[8,33]{0,1:T(8,128)(4,1)S(1)} %copy-done.3), kind=kOutput, calls=%fused_computation.6 | convolution fusion | flops 1250119680 | bytes 3738888 | tf_op jit(solution)/shard_map/conv_general_dilated | solution.py:199
  165.6 0.0 copy-start.2
  165.6 0.4 copy.10
  166.0 0.2 copy-done.2
  166.3 0.2 fusion.3
  166.5 1.2 copy.11
  (1 shorter events, 0.0 us)
Async XLA Ops:
  0.6 162.1 %copy-start = (bf16[3,3,128,128]{3,2,1,0:T(8,128)(2,1)S(1)}, bf16[3,3,128,128]{3,2,1,0:T(8,128)(2,1)}, u32[]{:S(2)}) copy-start(bf16[3,3,128,128]{3,2,1,0:T(8,128)(2,1)} %param.10) | copy-start | bytes 884740
  135.2 26.4 %copy-start.1 = (bf16[4096,128]{1,0:T(8,128)(2,1)S(1)}, bf16[4096,128]{1,0:T(8,128)(2,1)}, u32[]{:S(2)}) copy-start(bf16[4096,128]{1,0:T(8,128)(2,1)} %add_up.1) | copy-start | bytes 3145732
  136.2 13.9 %collective-permute-start = (bf16[1,256,128]{2,1,0:T(8,128)(2,1)S(1)}, bf16[1,256,128]{2,1,0:T(8,128)(2,1)S(1)}, u32[]{:S(2)}, u32[]{:S(2)}) collective-permute-start(bf16[1,256,128]{2,1,0:T(8,128)(2,1)S(1)} %get-tuple-element.6), channel_id=1, source_target_pairs={{0,8},{8,16},{16,24},{24,32},{32,40},{40,48},{48,56},{56,64},{64,7... | collective-permute-start | bytes 196616 | tf_op jit(solution)/shard_map/ppermute | solution.py:135
  148.2 8.3 %collective-permute-start.1 = (bf16[1,256,128]{2,1,0:T(8,128)(2,1)S(1)}, bf16[1,256,128]{2,1,0:T(8,128)(2,1)S(1)}, u32[]{:S(2)}, u32[]{:S(2)}) collective-permute-start(bf16[1,256,128]{2,1,0:T(8,128)(2,1)S(1)} %get-tuple-element.7), channel_id=1, source_target_pairs={{8,0},{16,8},{24,16},{32,24},{40,32},{48,40},{56,48},{64,56},{72,6... | collective-permute-start | bytes 196616 | tf_op jit(solution)/shard_map/ppermute | solution.py:137
  157.3 2.6 %collective-permute-start.2 = (bf16[18,1,128]{2,1,0:T(2,128)(2,1)S(1)}, bf16[18,1,128]{2,1,0:T(2,128)(2,1)S(1)}, u32[]{:S(2)}, u32[]{:S(2)}) collective-permute-start(bf16[18,1,128]{2,1,0:T(2,128)(2,1)S(1)} %get-tuple-element.4), channel_id=1, source_target_pairs={{0,1},{1,2},{2,3},{3,4},{4,5},{5,6},{6,7},{8,9},{9,10},{10,11},{11... | collective-permute-start | bytes 13832 | tf_op jit(solution)/shard_map/ppermute | solution.py:135
  158.6 3.1 %collective-permute-start.3 = (bf16[18,1,128]{2,1,0:T(2,128)(2,1)S(1)}, bf16[18,1,128]{2,1,0:T(2,128)(2,1)S(1)}, u32[]{:S(2)}, u32[]{:S(2)}) collective-permute-start(bf16[18,1,128]{2,1,0:T(2,128)(2,1)S(1)} %get-tuple-element.5), channel_id=1, source_target_pairs={{1,0},{2,1},{3,2},{4,3},{5,4},{6,5},{7,6},{9,8},{10,9},{11,10},{12... | collective-permute-start | bytes 13832 | tf_op jit(solution)/shard_map/ppermute | solution.py:137
  162.1 0.7 copy-start.3
  165.6 0.7 copy-start.2

commit v2 on v1

v2 whole, which is shorter than its diff:
```python
import jax
import jax.numpy as jnp
from jax import lax
from jax.experimental import pallas as pl
from jax.experimental.pallas import tpu as pltpu
from jax.sharding import PartitionSpec as P

COLS_DEV = 256
ROWS_DEV = 16
CELLS = ROWS_DEV * COLS_DEV
LANES = 128
CAP = 80
BLOCK = 88
SUMS = 8
DUMP = CELLS
GROUP = 16


def pack_kernel(
    count_ref, cell_ref, tile_ref, feats_ref, out_ref, rows, slots, pos_v, pos_f, pos_s, coded, sem
):
    count = count_ref[0]
    chunks, width = tile_ref.shape
    tiles = out_ref.shape[0]
    tile_id = lax.broadcasted_iota(jnp.int32, (tiles, width), 0)
    lane = lax.broadcasted_iota(jnp.int32, (1, width), 1)
    source = lax.broadcasted_iota(jnp.int32, (width, width + LANES), 0)
    column = lax.broadcasted_iota(jnp.int32, (width, width + LANES), 1)
    upto = jnp.where((source <= column) | (column >= width), 1.0, 0.0).astype(jnp.bfloat16)
    first = (lax.broadcasted_iota(jnp.int32, (tiles, LANES), 0) * LANES - 1).astype(jnp.float32)

    def rank(i, before):
        live = i * width + lane < count
        hit = tile_id == jnp.where(live, tile_ref[pl.ds(i, 1), :], -1)
        found = jnp.dot(
            jnp.where(hit, 1.0, 0.0).astype(jnp.bfloat16), upto, preferred_element_type=jnp.float32
        )
        place = found[:, :width] + jnp.concatenate([before] * (width // LANES), axis=1)
        slot = jnp.sum(jnp.where(hit, place, 0.0), axis=0, keepdims=True)
        pos_v[pl.ds(i, 1), :] = jnp.where(live, slot.astype(jnp.int32), tiles * LANES - 1)
        at = pl.ds(pl.multiple_of(i * width, width), width)
        rows[at, :] = feats_ref[at, :].astype(jnp.float32)
        return before + found[:, width:]

    total = lax.fori_loop(0, chunks, rank, first, unroll=4) - first
    for i in range(chunks):
        pos_f[pl.ds(i * width, width)] = pos_v[i, :]
    to_smem = pltpu.make_async_copy(pos_f, pos_s, sem)
    to_smem.start()
    coded[...] = jnp.zeros_like(coded)
    to_smem.wait()

    def move(i, carry):
        start = i * width
        for k in range(width):
            slots[pl.ds(pos_s[start + k], 1), :] = rows[pl.ds(start + k, 1), :]
        live = start + lane < count
        hit = tile_id == jnp.where(live, tile_ref[pl.ds(i, 1), :], -1)
        level = pos_v[pl.ds(i, 1), :] & (LANES - 1)
        at_level = lax.broadcasted_iota(jnp.int32, (LANES, width), 0) == level
        cell = cell_ref[pl.ds(i, 1), :]
        high = lax.shift_right_logical(cell, 6).astype(jnp.float32)
        low = (cell & 63).astype(jnp.float32)
        values = jnp.concatenate([jnp.where(hit, high, 0.0), jnp.where(hit, low, 0.0)], axis=0)
        coded[...] += lax.dot_general(
            values.astype(jnp.bfloat16),
            jnp.where(at_level, 1.0, 0.0).astype(jnp.bfloat16),
            (((1,), (1,)), ((), ())),
            preferred_element_type=jnp.float32,
        )
        return carry

    lax.fori_loop(0, (count + width - 1) // width, move, 0)
    spot = lax.broadcasted_iota(jnp.int32, (tiles, LANES), 1).astype(jnp.float32)
    high = jnp.where(spot < total, coded[:tiles, :], float(DUMP // 64))
    low = jnp.where(spot < total, coded[tiles:, :], 0.0)
    slots[pl.ds(CAP, tiles, LANES), :] = jnp.where(spot == LANES - 1, 0.0, high)
    slots[pl.ds(CAP + 1, tiles, LANES), :] = jnp.where(spot == LANES - 1, total, low)

    def narrow(t, carry):
        out_ref[t] = slots[pl.ds(pl.multiple_of(t * LANES, LANES), BLOCK), :].astype(jnp.bfloat16)
        return carry

    lax.fori_loop(0, tiles, narrow, 0, unroll=4)


def add_kernel(got_ref, out_ref, rows, cells_f, cells_s, sem, *sums):
    sources = got_ref.shape[0]

    def widen(s, carry):
        rows[pl.ds(pl.multiple_of(s * BLOCK, 8), BLOCK), :] = got_ref[s].astype(jnp.float32)
        return carry

    lax.fori_loop(0, sources, widen, 0, unroll=4)
    high = rows[pl.ds(CAP, sources, BLOCK), :].astype(jnp.int32)
    low = rows[pl.ds(CAP + 1, sources, BLOCK), :].astype(jnp.int32)
    cells_f[...] = (high * 64 + low).reshape(sources * LANES)
    to_smem = pltpu.make_async_copy(cells_f, cells_s, sem)
    to_smem.start()

    def clear(i, carry):
        for part in sums:
            part[pl.ds(pl.multiple_of(i * 256, 256), 256), :] = jnp.zeros((256, LANES), jnp.float32)
        return carry

    lax.fori_loop(0, CELLS // 256, clear, 0)
    for part in sums:
        part[pl.ds(CELLS, 8), :] = jnp.zeros((8, LANES), jnp.float32)
    to_smem.wait()

    def one(s, carry):
        number = cells_s[s * LANES + LANES - 1]

        def few(g, inner):
            at = s * LANES + g * GROUP
            base = s * BLOCK + g * GROUP
            for j in range(GROUP):
                cell = pl.ds(cells_s[at + j], 1)
                part = sums[j % SUMS]
                part[cell, :] = part[cell, :] + rows[pl.ds(base + j, 1), :]
            return inner

        return lax.fori_loop(0, lax.shift_right_logical(number + (GROUP - 1), 4), few, carry)

    lax.fori_loop(0, sources, one, 0)
    step = 256

    def close(i, carry):
        at = pl.ds(pl.multiple_of(i * step, step), step)
        total = sums[0][at, :]
        for part in sums[1:]:
            total = total + part[at, :]
        out_ref[at, :] = total.astype(jnp.bfloat16)
        return carry

    lax.fori_loop(0, CELLS // step, close, 0)


def with_halo(cells, sides, width):
    for axis, dim in sides:
        count = lax.axis_size(axis)
        ends = count - 1
        head = lax.slice_in_dim(cells, 0, width, axis=dim)
        tail = lax.slice_in_dim(cells, cells.shape[dim] - width, cells.shape[dim], axis=dim)
        cells = jnp.concatenate(
            [
                lax.ppermute(tail, axis, [(i, (i + 1) % count) for i in range(ends)]),
                cells,
                lax.ppermute(head, axis, [((i + 1) % count, i) for i in range(ends)]),
            ],
            axis=dim,
        )
    return cells


VMEM = pl.BlockSpec(memory_space=pltpu.VMEM)
SMEM = pl.BlockSpec(memory_space=pltpu.SMEM)


def pack(point_feats, point_tile, point_cell, point_count, devices):
    points, channels = point_feats.shape
    width = 2 * LANES
    chunks = points // width
    return pl.pallas_call(
        pack_kernel,
        out_shape=jax.ShapeDtypeStruct((devices, BLOCK, channels), jnp.bfloat16),
        in_specs=[SMEM, VMEM, VMEM, VMEM],
        out_specs=VMEM,
        scratch_shapes=[
            pltpu.VMEM((points, channels), jnp.float32),
            pltpu.VMEM((devices * LANES, channels), jnp.float32),
            pltpu.VMEM((chunks, width), jnp.int32),
            pltpu.VMEM((points,), jnp.int32),
            pltpu.SMEM((points,), jnp.int32),
            pltpu.VMEM((2 * devices, LANES), jnp.float32),
            pltpu.SemaphoreType.DMA,
        ],
        name="pack",
    )(
        point_count,
        point_cell.reshape(chunks, width),
        point_tile.reshape(chunks, width),
        point_feats,
    )


def add_up(got):
    devices, block, channels = got.shape
    return pl.pallas_call(
        add_kernel,
        out_shape=jax.ShapeDtypeStruct((CELLS, channels), jnp.bfloat16),
        in_specs=[VMEM],
        out_specs=VMEM,
        scratch_shapes=[
            pltpu.VMEM((devices * block, channels), jnp.float32),
            pltpu.VMEM((devices * LANES,), jnp.int32),
            pltpu.SMEM((devices * LANES,), jnp.int32),
            pltpu.SemaphoreType.DMA,
        ]
        + [pltpu.VMEM((CELLS + 8, channels), jnp.float32)] * SUMS,
        name="add_up",
    )(got)


def shards(point_feats, point_tile, point_cell, point_count, conv_weight, conv_bias):
    devices = lax.axis_size("gx") * lax.axis_size("gy")
    channels = point_feats.shape[1]
    sent = pack(point_feats, point_tile, point_cell, point_count, devices)
    got = lax.all_to_all(sent, ("gx", "gy"), split_axis=0, concat_axis=0, tiled=True)
    bev_map = add_up(got).reshape(ROWS_DEV, COLS_DEV, channels)
    padded = with_halo(bev_map, (("gx", 0), ("gy", 1)), 1)
    total = lax.conv_general_dilated(
        padded[None],
        conv_weight,
        (1, 1),
        "VALID",
        dimension_numbers=("NHWC", "HWIO", "NHWC"),
        preferred_element_type=jnp.float32,
    )[0]
    conv_out = jax.nn.relu(total + conv_bias).astype(jnp.bfloat16)
    return (bev_map, conv_out)


def solution(mesh):
    in_specs = (
        P(("gx", "gy"), None),
        P(("gx", "gy"), None),
        P(("gx", "gy")),
        P(("gx", "gy")),
        P(),
        P(),
    )
    out_specs = (P("gx", "gy", None), P("gx", "gy", None))
    return jax.shard_map(shards, mesh=mesh, in_specs=in_specs, out_specs=out_specs, check_vma=False)
```

time: 171 us -> 118 us (0.69)
  Pallas kernels: 79.6 us -> 36.5 us
  starting transfers between devices: 16.5 us -> 8.43 us
  blocking collectives: 54.3 us -> 50 us
  local copies, waits for them, and re-layouts: 3.61 us -> 6.13 us
    pallas_call x1, Pallas kernels: 52.3 us -> 17.8 us  [pack(): pl.pallas_call(pack_kernel, out_shape=jax.ShapeDtypeStruct((devices, BLOC...]
    pallas_call x1, Pallas kernels: 27.3 us -> 18.7 us  [add_up(): pl.pallas_call(add_kernel, out_shape=jax.ShapeDtypeStruct((CELLS, channel...]
    ppermute x2, starting transfers between devices: 13.2 us -> 5.13 us  [with_halo(): lax.ppermute(tail, axis, [(i, (i + 1) % count) for i in range(ends)])]
    all_to_all x1, blocking collectives: 54.3 us -> 50 us  [shards(): lax.all_to_all(sent, ('gx', 'gy'), split_axis=0, concat_axis=0, tiled=True)]
    reshape x0 -> x2, local copies, waits for them, and re-layouts: none -> 2.01 us  [the longest x1 1.38 us: pack(): point_cell.reshape(chunks, width)]
  transfers between devices with their start and end apart: 4 -> 4, of which waited for: 2 -> 3; matrix products, arithmetic and copies ran while one was open for 0% -> 0% of each run, Pallas kernels for 0% -> 0%
where the time goes in v2:
time: 118 us; the launch traced here: 116 us
  blocking collectives  50 us (42%)
  Pallas kernels  36.5 us (31%)
  starting transfers between devices  8.43 us (7%)
  waiting for transfers between devices  8.02 us (7%)
  local copies, waits for them, and re-layouts  6.13 us (5%)
  other arithmetic  2.85 us (2%)
  matrix products  2.8 us (2%)
  between operations  1.48 us (1%)
    all_to_all x1, blocking collectives, shards(): lax.all_to_all(sent, ('gx', 'gy'), split_axis=0, concat_axis=0, tiled=True)  50 us
    pallas_call x1, Pallas kernels, add_up(): pl.pallas_call(add_kernel, out_shape=jax.ShapeDtypeStruct((CELLS, channel...  18.7 us
    pallas_call x1, Pallas kernels, pack(): pl.pallas_call(pack_kernel, out_shape=jax.ShapeDtypeStruct((devices, BLOC...  17.8 us
    ppermute x2, waiting for transfers between devices, with_halo(): lax.ppermute(head, axis, [((i + 1) % count, i) for i in range(ends)])  7.71 us
    ppermute x2, starting transfers between devices, with_halo(): lax.ppermute(tail, axis, [(i, (i + 1) % count) for i in range(ends)])  5.13 us
    ppermute x2, starting transfers between devices, with_halo(): lax.ppermute(head, axis, [((i + 1) % count, i) for i in range(ends)])  3.3 us
    conv_general_dilated x1, matrix products, shards(): lax.conv_general_dilated(padded[None], conv_weight, (1, 1), 'VALID', dime...  2.8 us
  transfers between devices with their start and end apart: 4, of which 3 were waited for; matrix products, arithmetic and copies ran while one was open for 0% of the time, Pallas kernels for 0%

profile of v2, /device:TPU:6, one launch (start us, length us, event | category | flops | bytes accessed | tf_op | source)
XLA Modules:
  0.0 116.2 jit_solution(13350270323034946814)
XLA Ops:
  0.6 0.0 copy-start
  1.3 0.5 broadcast.18
  1.8 1.5 %reduce.3 = s32[8192]{0:T(1024)S(1)} reduce(s32[8192,1]{0,1:T(1,128)} %param.7, s32[]{:T(128)} %broadcast.18), dimensions={1}, to_apply=%param.7.reduce_sub_computation.3 | reduce | bytes 65540 | tf_op args[1]
  3.3 0.6 reshape.17.tile_ref
  4.0 1.4 %reshape.16.cell_ref = s32[32,256]{1,0:T(8,128)} reshape(s32[8192]{0:T(1024)} %param.8) | data formatting | bytes 65536 | tf_op jit(solution)/shard_map/reshape | solution.py:181
  5.3 17.8 %pack.1 = bf16[128,88,128]{2,1,0:T(8,128)(2,1)} custom-call(s32[1]{0:T(128)S(6)} %copy.12.count_ref, s32[32,256]{1,0:T(8,128)} %reshape.16.cell_ref, s32[32,256]{1,0:T(8,128)} %reshape.17.tile_ref, bf16[8192,128]{1,0:T(8,128)(2,1)} %feats_ref.1), custom_call_target="tpu_custom_call" | custom-call | tf_op jit(solution)/shard_map/pack/pallas_call | solution.py:164
  23.1 50.0 %all_to_all.5.got_ref = bf16[128,88,128]{2,1,0:T(8,128)(2,1)} all-to-all(bf16[128,88,128]{2,1,0:T(8,128)(2,1)} %pack.1), channel_id=1, replica_groups=mesh['gx'=16,'gy'=8] {'gx','gy'}, dimensions={0} | all-to-all | bytes 5767168 | tf_op jit(solution)/shard_map/all_to_all | solution.py:209
  73.1 18.7 %add_up.1 = bf16[4096,128]{1,0:T(8,128)(2,1)} custom-call(bf16[128,88,128]{2,1,0:T(8,128)(2,1)} %all_to_all.5.got_ref), custom_call_target="tpu_custom_call" | custom-call | tf_op jit(solution)/shard_map/add_up/pallas_call | solution.py:189
  91.8 0.0 copy-start.1
  91.8 1.0 slice_bitcast_fusion.2
  92.8 3.8 %collective-permute-start = (bf16[1,256,128]{2,1,0:T(8,128)(2,1)S(1)}, bf16[1,256,128]{2,1,0:T(8,128)(2,1)S(1)}, u32[]{:S(2)}, u32[]{:S(2)}) collective-permute-start(bf16[1,256,128]{2,1,0:T(8,128)(2,1)S(1)} %get-tuple-element.6), channel_id=1, source_target_pairs={{0,8},{8,16},{16,24},{24,32},{32,40},{40,48},{48,56},{56,64},{64,7... | collective-permute-start | bytes 196616 | tf_op jit(solution)/shard_map/ppermute | solution.py:147
  96.6 2.0 %collective-permute-start.1 = (bf16[1,256,128]{2,1,0:T(8,128)(2,1)S(1)}, bf16[1,256,128]{2,1,0:T(8,128)(2,1)S(1)}, u32[]{:S(2)}, u32[]{:S(2)}) collective-permute-start(bf16[1,256,128]{2,1,0:T(8,128)(2,1)S(1)} %get-tuple-element.7), channel_id=1, source_target_pairs={{8,0},{16,8},{24,16},{32,24},{40,32},{48,40},{56,48},{64,56},{72,6... | collective-permute-start | bytes 196616 | tf_op jit(solution)/shard_map/ppermute | solution.py:149
  98.7 0.3 collective-permute-done
  99.0 6.0 %collective-permute-done.1 = bf16[1,256,128]{2,1,0:T(8,128)(2,1)S(1)} collective-permute-done((bf16[1,256,128]{2,1,0:T(8,128)(2,1)S(1)}, bf16[1,256,128]{2,1,0:T(8,128)(2,1)S(1)}, u32[]{:S(2)}, u32[]{:S(2)}) %collective-permute-start.1) | collective-permute-done | bytes 65568 | tf_op jit(solution)/shard_map/ppermute | solution.py:149
  104.9 0.8 pad_maximum_fusion.2
  105.7 1.3 %collective-permute-start.2 = (bf16[18,1,128]{2,1,0:T(2,128)(2,1)S(1)}, bf16[18,1,128]{2,1,0:T(2,128)(2,1)S(1)}, u32[]{:S(2)}, u32[]{:S(2)}) collective-permute-start(bf16[18,1,128]{2,1,0:T(2,128)(2,1)S(1)} %get-tuple-element.4), channel_id=1, source_target_pairs={{0,1},{1,2},{2,3},{3,4},{4,5},{5,6},{6,7},{8,9},{9,10},{10,11},{11... | collective-permute-start | bytes 13832 | tf_op jit(solution)/shard_map/ppermute | solution.py:147
  107.0 1.3 %collective-permute-start.3 = (bf16[18,1,128]{2,1,0:T(2,128)(2,1)S(1)}, bf16[18,1,128]{2,1,0:T(2,128)(2,1)S(1)}, u32[]{:S(2)}, u32[]{:S(2)}) collective-permute-start(bf16[18,1,128]{2,1,0:T(2,128)(2,1)S(1)} %get-tuple-element.5), channel_id=1, source_target_pairs={{1,0},{2,1},{3,2},{4,3},{5,4},{6,5},{7,6},{9,8},{10,9},{11,10},{12... | collective-permute-start | bytes 13832 | tf_op jit(solution)/shard_map/ppermute | solution.py:149
  108.3 0.0 collective-permute-done.2
  108.3 1.8 %collective-permute-done.3 = bf16[18,1,128]{2,1,0:T(2,128)(2,1)S(1)} collective-permute-done((bf16[18,1,128]{2,1,0:T(2,128)(2,1)S(1)}, bf16[18,1,128]{2,1,0:T(2,128)(2,1)S(1)}, u32[]{:S(2)}, u32[]{:S(2)}) %collective-permute-start.3) | collective-permute-done | bytes 4640 | tf_op jit(solution)/shard_map/ppermute | solution.py:149
  110.1 0.0 copy-done.1
  110.1 0.4 maximum_bitcast_fusion
  110.5 0.1 pad
  110.6 0.0 copy-start.3
  110.6 0.4 reshape.21
  111.0 0.2 copy.9
  111.2 0.0 copy-done
  111.2 0.0 copy-done.3
  111.2 2.8 %convolution_select_fusion = f32[16,8,33,128]{3,1,2,0:T(8,128)S(1)} fusion(bf16[3,3,128,128]{3,2,1,0:T(8,128)(2,1)S(1)} %copy-done, bf16[18,1,7,2,128]{4,2,3,0,1:T(8,128)(2,1)S(1)} %slice.28, bf16[18,1,8,33,128]{4,2,3,0,1:T(8,128)(2,1)S(1)} %copy.9, pred[8,33]{0,1:T(8,128)(4,1)S(1)} %copy-done.3), kind=kOutput, calls=%fused_computation.6 | convolution fusion | flops 1250119680 | bytes 3738888 | tf_op jit(solution)/shard_map/conv_general_dilated | solution.py:212
  114.1 0.0 copy-start.2
  114.1 0.4 copy.10
  114.5 0.2 copy-done.2
  114.7 0.2 fusion.3
  114.9 1.2 %copy.11 = bf16[16,256,128]{2,1,0:T(8,128)(2,1)} copy(bf16[16,256,128]{2,0,1:T(8,128)(2,1)S(1)} %fusion.3) | data formatting | bytes 2097152
  (1 shorter events, 0.0 us)
Async XLA Ops:
  0.6 110.6 %copy-start = (bf16[3,3,128,128]{3,2,1,0:T(8,128)(2,1)S(1)}, bf16[3,3,128,128]{3,2,1,0:T(8,128)(2,1)}, u32[]{:S(2)}) copy-start(bf16[3,3,128,128]{3,2,1,0:T(8,128)(2,1)} %param.10) | copy-start | bytes 884740
  91.8 18.3 %copy-start.1 = (bf16[4096,128]{1,0:T(8,128)(2,1)S(1)}, bf16[4096,128]{1,0:T(8,128)(2,1)}, u32[]{:S(2)}) copy-start(bf16[4096,128]{1,0:T(8,128)(2,1)} %add_up.1) | copy-start | bytes 3145732
  92.8 6.2 %collective-permute-start = (bf16[1,256,128]{2,1,0:T(8,128)(2,1)S(1)}, bf16[1,256,128]{2,1,0:T(8,128)(2,1)S(1)}, u32[]{:S(2)}, u32[]{:S(2)}) collective-permute-start(bf16[1,256,128]{2,1,0:T(8,128)(2,1)S(1)} %get-tuple-element.6), channel_id=1, source_target_pairs={{0,8},{8,16},{16,24},{24,32},{32,40},{40,48},{48,56},{56,64},{64,7... | collective-permute-start | bytes 196616 | tf_op jit(solution)/shard_map/ppermute | solution.py:147
  96.6 8.3 %collective-permute-start.1 = (bf16[1,256,128]{2,1,0:T(8,128)(2,1)S(1)}, bf16[1,256,128]{2,1,0:T(8,128)(2,1)S(1)}, u32[]{:S(2)}, u32[]{:S(2)}) collective-permute-start(bf16[1,256,128]{2,1,0:T(8,128)(2,1)S(1)} %get-tuple-element.7), channel_id=1, source_target_pairs={{8,0},{16,8},{24,16},{32,24},{40,32},{48,40},{56,48},{64,56},{72,6... | collective-permute-start | bytes 196616 | tf_op jit(solution)/shard_map/ppermute | solution.py:149
  105.7 2.6 %collective-permute-start.2 = (bf16[18,1,128]{2,1,0:T(2,128)(2,1)S(1)}, bf16[18,1,128]{2,1,0:T(2,128)(2,1)S(1)}, u32[]{:S(2)}, u32[]{:S(2)}) collective-permute-start(bf16[18,1,128]{2,1,0:T(2,128)(2,1)S(1)} %get-tuple-element.4), channel_id=1, source_target_pairs={{0,1},{1,2},{2,3},{3,4},{4,5},{5,6},{6,7},{8,9},{9,10},{10,11},{11... | collective-permute-start | bytes 13832 | tf_op jit(solution)/shard_map/ppermute | solution.py:147
  107.0 3.1 %collective-permute-start.3 = (bf16[18,1,128]{2,1,0:T(2,128)(2,1)S(1)}, bf16[18,1,128]{2,1,0:T(2,128)(2,1)S(1)}, u32[]{:S(2)}, u32[]{:S(2)}) collective-permute-start(bf16[18,1,128]{2,1,0:T(2,128)(2,1)S(1)} %get-tuple-element.5), channel_id=1, source_target_pairs={{1,0},{2,1},{3,2},{4,3},{5,4},{6,5},{7,6},{9,8},{10,9},{11,10},{12... | collective-permute-start | bytes 13832 | tf_op jit(solution)/shard_map/ppermute | solution.py:149
  110.6 0.7 copy-start.3
  114.1 0.7 copy-start.2

commit v3 on v2

--- a/solution.py
+++ b/solution.py
@@ -14,13 +14,15 @@
 SUMS = 8
 DUMP = CELLS
 GROUP = 16
+EDGE = 16
 
 
 def pack_kernel(
     count_ref, cell_ref, tile_ref, feats_ref, out_ref, rows, slots, pos_v, pos_f, pos_s, coded, sem
 ):
     count = count_ref[0]
-    chunks, width = tile_ref.shape
+    width = 2 * LANES
+    chunks = tile_ref.shape[1] // width
     tiles = out_ref.shape[0]
     tile_id = lax.broadcasted_iota(jnp.int32, (tiles, width), 0)
     lane = lax.broadcasted_iota(jnp.int32, (1, width), 1)
@@ -31,7 +33,8 @@
 
     def rank(i, before):
         live = i * width + lane < count
-        hit = tile_id == jnp.where(live, tile_ref[pl.ds(i, 1), :], -1)
+        here = pl.ds(pl.multiple_of(i * width, width), width)
+        hit = tile_id == jnp.where(live, tile_ref[:, here], -1)
         found = jnp.dot(
             jnp.where(hit, 1.0, 0.0).astype(jnp.bfloat16), upto, preferred_element_type=jnp.float32
         )
@@ -55,10 +58,11 @@
         for k in range(width):
             slots[pl.ds(pos_s[start + k], 1), :] = rows[pl.ds(start + k, 1), :]
         live = start + lane < count
-        hit = tile_id == jnp.where(live, tile_ref[pl.ds(i, 1), :], -1)
+        here = pl.ds(pl.multiple_of(start, width), width)
+        hit = tile_id == jnp.where(live, tile_ref[:, here], -1)
         level = pos_v[pl.ds(i, 1), :] & (LANES - 1)
         at_level = lax.broadcasted_iota(jnp.int32, (LANES, width), 0) == level
-        cell = cell_ref[pl.ds(i, 1), :]
+        cell = cell_ref[:, here]
         high = lax.shift_right_logical(cell, 6).astype(jnp.float32)
         low = (cell & 63).astype(jnp.float32)
         values = jnp.concatenate([jnp.where(hit, high, 0.0), jnp.where(hit, low, 0.0)], axis=0)
@@ -84,7 +88,7 @@
     lax.fori_loop(0, tiles, narrow, 0, unroll=4)
 
 
-def add_kernel(got_ref, out_ref, rows, cells_f, cells_s, sem, *sums):
+def add_kernel(got_ref, out_ref, top_ref, bottom_ref, left_ref, right_ref, rows, cells_f, cells_s, sem, *sums):
     sources = got_ref.shape[0]
 
     def widen(s, carry):
@@ -134,23 +138,80 @@
         return carry
 
     lax.fori_loop(0, CELLS // step, close, 0)
-
-
-def with_halo(cells, sides, width):
-    for axis, dim in sides:
-        count = lax.axis_size(axis)
-        ends = count - 1
-        head = lax.slice_in_dim(cells, 0, width, axis=dim)
-        tail = lax.slice_in_dim(cells, cells.shape[dim] - width, cells.shape[dim], axis=dim)
-        cells = jnp.concatenate(
-            [
-                lax.ppermute(tail, axis, [(i, (i + 1) % count) for i in range(ends)]),
-                cells,
-                lax.ppermute(head, axis, [((i + 1) % count, i) for i in range(ends)]),
-            ],
-            axis=dim,
-        )
-    return cells
+    top_ref[...] = out_ref[:COLS_DEV, :]
+    bottom_ref[...] = out_ref[CELLS - COLS_DEV :, :]
+    for ref, column in ((left_ref, 0), (right_ref, COLS_DEV - 1)):
+        total = sums[0][pl.ds(column, ROWS_DEV, COLS_DEV), :]
+        for part in sums[1:]:
+            total = total + part[pl.ds(column, ROWS_DEV, COLS_DEV), :]
+        ref[...] = total.astype(jnp.bfloat16)
+
+
+def conv_kernel(
+    bev_ref, up_ref, down_ref, weight_ref, bias_ref,
+    out_ref, left_ref, right_ref, first_ref, last_ref, wide, before, after,
+):
+    for i in range(4):
+        for b in range(3):
+            for o in range(2):
+                block = (slice(i * LANES, (i + 1) * LANES), slice((2 * b + o) * LANES, (2 * b + o + 1) * LANES))
+                wide[block] = weight_ref[i - o, b] if 0 <= i - o < 3 else jnp.zeros((LANES, LANES), jnp.bfloat16)
+    before[:8, :] = jnp.zeros((8, 2 * LANES), jnp.float32)
+    after[COLS_DEV:, :] = jnp.zeros((8, 2 * LANES), jnp.float32)
+    bias = bias_ref[...]
+
+    def row(r):
+        if r < 0:
+            return up_ref[...]
+        if r >= ROWS_DEV:
+            return down_ref[...]
+        return bev_ref[r * COLS_DEV : (r + 1) * COLS_DEV, :]
+
+    for p in range(ROWS_DEV // 2):
+        four = jnp.concatenate([row(2 * p - 1 + i) for i in range(4)], axis=1)
+        taps = jnp.dot(four, wide[...], preferred_element_type=jnp.float32)
+        before[8:, :] = taps[:, : 2 * LANES]
+        after[:COLS_DEV, :] = taps[:, 4 * LANES :]
+        total = taps[:, 2 * LANES : 4 * LANES] + before[7 : 7 + COLS_DEV, :] + after[1 : 1 + COLS_DEV, :]
+        for o in range(2):
+            r = 2 * p + o
+            part = total[:, o * LANES : (o + 1) * LANES]
+            left_ref[r : r + 1, :] = part[:1, :]
+            right_ref[r : r + 1, :] = part[COLS_DEV - 1 :, :]
+            done = jnp.maximum(part + bias, 0.0).astype(jnp.bfloat16)
+            out_ref[r * COLS_DEV : (r + 1) * COLS_DEV, :] = done
+            first_ref[r] = done[:EDGE, :]
+            last_ref[r] = done[COLS_DEV - EDGE :, :]
+
+
+def edge_kernel(
+    conv_ref, left_ref, right_ref, first_ref, last_ref, west_ref, east_ref, weight_ref, bias_ref,
+    out_ref, halo, blocks, sems,
+):
+    bias = bias_ref[...]
+    column = lax.broadcasted_iota(jnp.int32, (ROWS_DEV, EDGE, LANES), 1)
+    sides = (
+        (left_ref, first_ref, west_ref, 0, 0, 0),
+        (right_ref, last_ref, east_ref, 2, EDGE - 1, COLS_DEV - EDGE),
+    )
+    copies = []
+    for k, (sum_ref, block_ref, halo_ref, b, spot, start) in enumerate(sides):
+        halo[: ROWS_DEV + 2, :] = halo_ref[...].astype(jnp.float32)
+        total = sum_ref[...]
+        for a in range(3):
+            total = total + jnp.dot(
+                halo[a : a + ROWS_DEV, :].astype(jnp.bfloat16),
+                weight_ref[a, b],
+                preferred_element_type=jnp.float32,
+            )
+        done = jnp.maximum(total + bias, 0.0)
+        block = jnp.where(column == spot, done[:, None, :], block_ref[...].astype(jnp.float32))
+        blocks[k] = block.astype(jnp.bfloat16)
+        copy = pltpu.make_async_copy(blocks.at[k], out_ref.at[:, pl.ds(start, EDGE), :], sems.at[k])
+        copy.start()
+        copies.append(copy)
+    for copy in copies:
+        copy.wait()
 
 
 VMEM = pl.BlockSpec(memory_space=pltpu.VMEM)
@@ -178,8 +239,8 @@
         name="pack",
     )(
         point_count,
-        point_cell.reshape(chunks, width),
-        point_tile.reshape(chunks, width),
+        point_cell.reshape(1, points),
+        point_tile.reshape(1, points),
         point_feats,
     )
 
@@ -188,9 +249,12 @@
     devices, block, channels = got.shape
     return pl.pallas_call(
         add_kernel,
-        out_shape=jax.ShapeDtypeStruct((CELLS, channels), jnp.bfloat16),
+        out_shape=[
+            jax.ShapeDtypeStruct((rows, channels), jnp.bfloat16)
+            for rows in (CELLS, COLS_DEV, COLS_DEV, ROWS_DEV, ROWS_DEV)
+        ],
         in_specs=[VMEM],
-        out_specs=VMEM,
+        out_specs=[VMEM] * 5,
         scratch_shapes=[
             pltpu.VMEM((devices * block, channels), jnp.float32),
             pltpu.VMEM((devices * LANES,), jnp.int32),
@@ -202,23 +266,73 @@
     )(got)
 
 
+def shift(cells, axis, step):
+    count = lax.axis_size(axis)
+    pairs = [(i, i + step) for i in range(count) if 0 <= i + step < count]
+    return lax.ppermute(cells, axis, pairs)
+
+
+def conv(bev, up, down, weight, bias):
+    cells, channels = bev.shape
+    bf16, f32 = jnp.bfloat16, jnp.float32
+    edge = (ROWS_DEV, EDGE, channels)
+    return pl.pallas_call(
+        conv_kernel,
+        out_shape=[
+            jax.ShapeDtypeStruct((cells, channels), bf16),
+            jax.ShapeDtypeStruct((ROWS_DEV, channels), f32),
+            jax.ShapeDtypeStruct((ROWS_DEV, channels), f32),
+            jax.ShapeDtypeStruct(edge, bf16),
+            jax.ShapeDtypeStruct(edge, bf16),
+        ],
+        in_specs=[VMEM] * 5,
+        out_specs=[VMEM] * 5,
+        scratch_shapes=[
+            pltpu.VMEM((4 * channels, 6 * channels), bf16),
+            pltpu.VMEM((COLS_DEV + 8, 2 * channels), f32),
+            pltpu.VMEM((COLS_DEV + 8, 2 * channels), f32),
+        ],
+        cost_estimate=pl.CostEstimate(
+            flops=2 * cells * 9 * channels * channels, bytes_accessed=4 * cells * channels, transcendentals=0
+        ),
+        name="conv",
+    )(bev, up, down, weight, bias)
+
+
+def close_edges(inner, sums_left, sums_right, first, last, west, east, weight, bias):
+    channels = weight.shape[-1]
+    whole = (ROWS_DEV, COLS_DEV, channels)
+    anywhere = pl.BlockSpec(memory_space=pl.ANY)
+    return pl.pallas_call(
+        edge_kernel,
+        out_shape=jax.ShapeDtypeStruct(whole, jnp.bfloat16),
+        in_specs=[anywhere] + [VMEM] * 8,
+        out_specs=anywhere,
+        input_output_aliases={0: 0},
+        scratch_shapes=[
+            pltpu.VMEM((ROWS_DEV + 8, channels), jnp.float32),
+            pltpu.VMEM((2, ROWS_DEV, EDGE, channels), jnp.bfloat16),
+            pltpu.SemaphoreType.DMA((2,)),
+        ],
+        name="edges",
+    )(inner.reshape(whole), sums_left, sums_right, first, last, west, east, weight, bias)
+
+
 def shards(point_feats, point_tile, point_cell, point_count, conv_weight, conv_bias):
     devices = lax.axis_size("gx") * lax.axis_size("gy")
     channels = point_feats.shape[1]
     sent = pack(point_feats, point_tile, point_cell, point_count, devices)
     got = lax.all_to_all(sent, ("gx", "gy"), split_axis=0, concat_axis=0, tiled=True)
-    bev_map = add_up(got).reshape(ROWS_DEV, COLS_DEV, channels)
-    padded = with_halo(bev_map, (("gx", 0), ("gy", 1)), 1)
-    total = lax.conv_general_dilated(
-        padded[None],
-        conv_weight,
-        (1, 1),
-        "VALID",
-        dimension_numbers=("NHWC", "HWIO", "NHWC"),
-        preferred_element_type=jnp.float32,
-    )[0]
-    conv_out = jax.nn.relu(total + conv_bias).astype(jnp.bfloat16)
-    return (bev_map, conv_out)
+    bev, top, bottom, left, right = add_up(got)
+    up = shift(bottom, "gx", 1)
+    down = shift(top, "gx", -1)
+    bias = conv_bias.reshape(1, channels)
+    last = COLS_DEV - 1
+    west = shift(jnp.concatenate([up[last:], right, down[last:]], axis=0), "gy", 1)
+    east = shift(jnp.concatenate([up[:1], left, down[:1]], axis=0), "gy", -1)
+    inner, *edges = conv(bev, up, down, conv_weight, bias)
+    conv_out = close_edges(inner, *edges, west, east, conv_weight, bias)
+    return (bev.reshape(ROWS_DEV, COLS_DEV, channels), conv_out)
 
 
 def solution(mesh):

time: 118 us -> 112 us (0.949)
  the two profiles are of different devices: /device:TPU:6 before, /device:TPU:23 now
where the time goes in v3:
time: 112 us
  blocking collectives  47.1 us (42%)
  Pallas kernels  42.5 us (38%)
  starting transfers between devices  15.1 us (13%)
  waiting for transfers between devices  3.55 us (3%)
  between operations  1.39 us (1%)
  other arithmetic  1.38 us (1%)
    all_to_all x1, blocking collectives, shards(): lax.all_to_all(sent, ('gx', 'gy'), split_axis=0, concat_axis=0, tiled=True)  47.1 us
    pallas_call x1, Pallas kernels, pack(): pl.pallas_call(pack_kernel, out_shape=jax.ShapeDtypeStruct((devices, BLOC...  18.2 us
    pallas_call x1, Pallas kernels, add_up(): pl.pallas_call(add_kernel, out_shape=[jax.ShapeDtypeStruct((rows, channel...  18 us
    ppermute x4, starting transfers between devices, shift(): return lax.ppermute(cells, axis, pairs)  15.1 us
    pallas_call x1, Pallas kernels, conv(): pl.pallas_call(conv_kernel, out_shape=[jax.ShapeDtypeStruct((cells, chann...  4.39 us
    ppermute x4, waiting for transfers between devices, shift(): return lax.ppermute(cells, axis, pairs)  3.55 us
  transfers between devices with their start and end apart: 4, of which 1 were waited for; matrix products, arithmetic and copies ran while one was open for 1% of the time, Pallas kernels for 4%

profile of v3, /device:TPU:23, one launch (start us, length us, event | category | flops | bytes accessed | tf_op | source)
XLA Modules:
  0.0 111.6 jit_solution(14958596483848287585)
XLA Ops:
  1.3 18.2 %pack.1 = bf16[128,88,128]{2,1,0:T(8,128)(2,1)} custom-call(s32[1]{0:T(128)S(6)} %copy.10.count_ref, s32[1,8192]{1,0:T(1,128)} %bitcast.6, s32[1,8192]{1,0:T(1,128)} %bitcast.7, bf16[8192,128]{1,0:T(8,128)(2,1)} %feats_ref.1), custom_call_target="tpu_custom_call" | custom-call | tf_op jit(solution)/shard_map/pack/pallas_call | solution.py:225
  19.5 47.1 %all_to_all.5.got_ref = bf16[128,88,128]{2,1,0:T(8,128)(2,1)} all-to-all(bf16[128,88,128]{2,1,0:T(8,128)(2,1)} %pack.1), channel_id=1, replica_groups=mesh['gx'=16,'gy'=8] {'gx','gy'}, dimensions={0} | all-to-all | bytes 5767168 | tf_op jit(solution)/shard_map/all_to_all | solution.py:325
  66.6 18.0 %add_up.1 = (bf16[4096,128]{1,0:T(8,128)(2,1)}, bf16[256,128]{1,0:T(8,128)(2,1)}, bf16[256,128]{1,0:T(8,128)(2,1)}, bf16[16,128]{1,0:T(8,128)(2,1)}, bf16[16,128]{1,0:T(8,128)(2,1)}) custom-call(bf16[128,88,128]{2,1,0:T(8,128)(2,1)} %all_to_all.5.got_ref), custom_call_target="tpu_custom_call" | custom-call | tf_op jit(solution)/shard_map/add_up/pallas_call | solution.py:250
  84.6 1.9 %collective-permute-start = (bf16[256,128]{1,0:T(8,128)(2,1)}, bf16[256,128]{1,0:T(8,128)(2,1)S(1)}, u32[]{:S(2)}, u32[]{:S(2)}) collective-permute-start(bf16[256,128]{1,0:T(8,128)(2,1)} %get-tuple-element.13), channel_id=1, source_target_pairs={{0,8},{8,16},{16,24},{24,32},{32,40},{40,48},{48,56},{56,64},{64,7... | collective-permute-start | bytes 196616 | tf_op jit(solution)/shard_map/ppermute | solution.py:272
  86.5 4.1 %collective-permute-start.1 = (bf16[256,128]{1,0:T(8,128)(2,1)}, bf16[256,128]{1,0:T(8,128)(2,1)S(1)}, u32[]{:S(2)}, u32[]{:S(2)}) collective-permute-start(bf16[256,128]{1,0:T(8,128)(2,1)} %get-tuple-element.14), channel_id=1, source_target_pairs={{8,0},{16,8},{24,16},{32,24},{40,32},{48,40},{56,48},{64,56},{72,6... | collective-permute-start | bytes 196616 | tf_op jit(solution)/shard_map/ppermute | solution.py:272
  90.6 0.0 collective-permute-done.up_ref
  90.6 0.0 copy-start.2
  90.6 3.5 %collective-permute-done.1.down_ref = bf16[256,128]{1,0:T(8,128)(2,1)S(1)} collective-permute-done((bf16[256,128]{1,0:T(8,128)(2,1)}, bf16[256,128]{1,0:T(8,128)(2,1)S(1)}, u32[]{:S(2)}, u32[]{:S(2)}) %collective-permute-start.1) | collective-permute-done | bytes 65568 | tf_op jit(solution)/shard_map/ppermute | solution.py:272
  94.1 0.0 copy-start.3
  94.1 0.7 pad_maximum_fusion
  94.8 7.2 %collective-permute-start.2 = (bf16[18,128]{1,0:T(8,128)(2,1)S(1)}, bf16[18,128]{1,0:T(8,128)(2,1)S(1)}, u32[]{:S(2)}, u32[]{:S(2)}) collective-permute-start(bf16[18,128]{1,0:T(8,128)(2,1)S(1)} %pad_maximum_fusion), channel_id=1, source_target_pairs={{0,1},{1,2},{2,3},{3,4},{4,5},{5,6},{6,7},{8,9},{9,10},{10,11},{11... | collective-permute-start | bytes 13832 | tf_op jit(solution)/shard_map/ppermute | solution.py:272
  102.1 0.7 pad_maximum_fusion.1
  102.8 1.9 %collective-permute-start.3 = (bf16[18,128]{1,0:T(8,128)(2,1)S(1)}, bf16[18,128]{1,0:T(8,128)(2,1)S(1)}, u32[]{:S(2)}, u32[]{:S(2)}) collective-permute-start(bf16[18,128]{1,0:T(8,128)(2,1)S(1)} %pad_maximum_fusion.1), channel_id=1, source_target_pairs={{1,0},{2,1},{3,2},{4,3},{5,4},{6,5},{7,6},{9,8},{10,9},{11,10},{12... | collective-permute-start | bytes 13832 | tf_op jit(solution)/shard_map/ppermute | solution.py:272
  104.7 0.0 copy-done.2
  104.7 0.0 copy-done.3
  104.7 4.4 %conv.1 = (bf16[4096,128]{1,0:T(8,128)(2,1)}, f32[16,128]{1,0:T(8,128)}, f32[16,128]{1,0:T(8,128)}, bf16[16,16,128]{2,1,0:T(8,128)(2,1)}, bf16[16,16,128]{2,1,0:T(8,128)(2,1)}) custom-call(bf16[4096,128]{1,0:T(8,128)(2,1)} %get-tuple-element.12.bev_ref, bf16[256,128]{1,0:T(8,128)(2,1)} %copy-done.2, bf16[256,128]{1,0:T(8,128)(2,1)} %copy-done.3, ...), custom_call_target="tpu_custom_call" | custom-call | flops 1207959552 | bytes 2097152 | tf_op jit(solution)/shard_map/conv/pallas_call | solution.py:279
  109.1 0.0 collective-permute-done.2.west_ref
  109.1 0.0 copy-start
  109.1 0.0 collective-permute-done.3.east_ref
  109.1 0.0 copy-start.1
  109.1 0.6 copy-done
  109.7 0.0 copy-done.1
  109.7 1.9 %edges.1 = bf16[16,256,128]{2,1,0:T(8,128)(2,1)} custom-call(bf16[16,256,128]{2,1,0:T(8,128)(2,1)} %bitcast.5, f32[16,128]{1,0:T(8,128)} %get-tuple-element.16.left_ref, f32[16,128]{1,0:T(8,128)} %get-tuple-element.17.right_ref, bf16[16,16,128]{2,1,0:T(8,128)(2,1)} %get-tuple-element.18.first_ref, ...), custom_call_target="tpu_custom_call", output_to_operand_aliasing={{}: (0, {})} | custom-call | tf_op jit(solution)/shard_map/edges/pallas_call | solution.py:306
  (2 shorter events, 0.0 us)
Async XLA Ops:
  84.6 6.0 %collective-permute-start = (bf16[256,128]{1,0:T(8,128)(2,1)}, bf16[256,128]{1,0:T(8,128)(2,1)S(1)}, u32[]{:S(2)}, u32[]{:S(2)}) collective-permute-start(bf16[256,128]{1,0:T(8,128)(2,1)} %get-tuple-element.13), channel_id=1, source_target_pairs={{0,8},{8,16},{16,24},{24,32},{32,40},{40,48},{48,56},{56,64},{64,7... | collective-permute-start | bytes 196616 | tf_op jit(solution)/shard_map/ppermute | solution.py:272
  86.5 7.6 %collective-permute-start.1 = (bf16[256,128]{1,0:T(8,128)(2,1)}, bf16[256,128]{1,0:T(8,128)(2,1)S(1)}, u32[]{:S(2)}, u32[]{:S(2)}) collective-permute-start(bf16[256,128]{1,0:T(8,128)(2,1)} %get-tuple-element.14), channel_id=1, source_target_pairs={{8,0},{16,8},{24,16},{32,24},{40,32},{48,40},{56,48},{64,56},{72,6... | collective-permute-start | bytes 196616 | tf_op jit(solution)/shard_map/ppermute | solution.py:272
  90.6 14.1 %copy-start.2 = (bf16[256,128]{1,0:T(8,128)(2,1)}, bf16[256,128]{1,0:T(8,128)(2,1)S(1)}, u32[]{:S(2)}) copy-start(bf16[256,128]{1,0:T(8,128)(2,1)S(1)} %collective-permute-done.up_ref) | copy-start | bytes 196612
  94.1 10.6 %copy-start.3 = (bf16[256,128]{1,0:T(8,128)(2,1)}, bf16[256,128]{1,0:T(8,128)(2,1)S(1)}, u32[]{:S(2)}) copy-start(bf16[256,128]{1,0:T(8,128)(2,1)S(1)} %collective-permute-done.1.down_ref) | copy-start | bytes 196612
  94.8 14.3 %collective-permute-start.2 = (bf16[18,128]{1,0:T(8,128)(2,1)S(1)}, bf16[18,128]{1,0:T(8,128)(2,1)S(1)}, u32[]{:S(2)}, u32[]{:S(2)}) collective-permute-start(bf16[18,128]{1,0:T(8,128)(2,1)S(1)} %pad_maximum_fusion), channel_id=1, source_target_pairs={{0,1},{1,2},{2,3},{3,4},{4,5},{5,6},{6,7},{8,9},{9,10},{10,11},{11... | collective-permute-start | bytes 13832 | tf_op jit(solution)/shard_map/ppermute | solution.py:272
  102.8 6.3 %collective-permute-start.3 = (bf16[18,128]{1,0:T(8,128)(2,1)S(1)}, bf16[18,128]{1,0:T(8,128)(2,1)S(1)}, u32[]{:S(2)}, u32[]{:S(2)}) collective-permute-start(bf16[18,128]{1,0:T(8,128)(2,1)S(1)} %pad_maximum_fusion.1), channel_id=1, source_target_pairs={{1,0},{2,1},{3,2},{4,3},{5,4},{6,5},{7,6},{9,8},{10,9},{11,10},{12... | collective-permute-start | bytes 13832 | tf_op jit(solution)/shard_map/ppermute | solution.py:272
  109.1 0.6 copy-start
  109.1 0.6 copy-start.1

commit v4 on v3

--- a/solution.py
+++ b/solution.py
@@ -13,17 +13,21 @@
 BLOCK = 88
 SUMS = 8
 DUMP = CELLS
-GROUP = 16
 EDGE = 16
+TOGETHER = 4
 
 
 def pack_kernel(
-    count_ref, cell_ref, tile_ref, feats_ref, out_ref, rows, slots, pos_v, pos_f, pos_s, coded, sem
+    count_ref, cell_ref, tile_ref, feats_hbm, out_hbm,
+    feats, even, odd, slots, pos_f, pos_s, hits, coded, sent, sem, in_sem, out_sems,
 ):
     count = count_ref[0]
     width = 2 * LANES
-    chunks = tile_ref.shape[1] // width
-    tiles = out_ref.shape[0]
+    points = tile_ref.shape[1]
+    chunks = points // width
+    tiles = out_hbm.shape[0]
+    load = pltpu.make_async_copy(feats_hbm, feats, in_sem)
+    load.start()
     tile_id = lax.broadcasted_iota(jnp.int32, (tiles, width), 0)
     lane = lax.broadcasted_iota(jnp.int32, (1, width), 1)
     source = lax.broadcasted_iota(jnp.int32, (width, width + LANES), 0)
@@ -31,73 +35,105 @@
     upto = jnp.where((source <= column) | (column >= width), 1.0, 0.0).astype(jnp.bfloat16)
     first = (lax.broadcasted_iota(jnp.int32, (tiles, LANES), 0) * LANES - 1).astype(jnp.float32)
 
-    def rank(i, before):
-        live = i * width + lane < count
-        here = pl.ds(pl.multiple_of(i * width, width), width)
-        hit = tile_id == jnp.where(live, tile_ref[:, here], -1)
-        found = jnp.dot(
-            jnp.where(hit, 1.0, 0.0).astype(jnp.bfloat16), upto, preferred_element_type=jnp.float32
-        )
-        place = found[:, :width] + jnp.concatenate([before] * (width // LANES), axis=1)
-        slot = jnp.sum(jnp.where(hit, place, 0.0), axis=0, keepdims=True)
-        pos_v[pl.ds(i, 1), :] = jnp.where(live, slot.astype(jnp.int32), tiles * LANES - 1)
-        at = pl.ds(pl.multiple_of(i * width, width), width)
-        rows[at, :] = feats_ref[at, :].astype(jnp.float32)
-        return before + found[:, width:]
-
-    total = lax.fori_loop(0, chunks, rank, first, unroll=4) - first
-    for i in range(chunks):
-        pos_f[pl.ds(i * width, width)] = pos_v[i, :]
+    tile_mark = tile_id.astype(jnp.float32).astype(jnp.bfloat16)
+    one, zero = jnp.ones((), jnp.bfloat16), jnp.zeros((), jnp.bfloat16)
+
+    def rank(g, before):
+        marks, hit = [], []
+        for c in range(TOGETHER):
+            i = g * TOGETHER + c
+            here = pl.ds(pl.multiple_of(i * width, width), width)
+            live = i * width + lane < count
+            tile = jnp.where(live, tile_ref[:, here], tiles)
+            mark = jnp.where(tile_mark == tile.astype(jnp.float32).astype(jnp.bfloat16), one, zero)
+            hits[:, here] = mark
+            marks.append(mark)
+            hit.append((tile_id == tile, live, here, i))
+        found = jnp.dot(jnp.concatenate(marks, axis=0), upto, preferred_element_type=jnp.float32)
+        for c in range(TOGETHER):
+            match, live, here, i = hit[c]
+            mine = found[c * tiles : (c + 1) * tiles, :]
+            place = mine[:, :width] + jnp.concatenate([before] * (width // LANES), axis=1)
+            slot = jnp.sum(jnp.where(match, place, 0.0), axis=0, keepdims=True).astype(jnp.int32)
+            pos_f[pl.ds(pl.multiple_of(i * width, width), width)] = jnp.where(live, slot, tiles * LANES - 1).reshape(width)
+            level = (slot & (LANES - 1)).astype(jnp.float32).astype(jnp.bfloat16)
+            at_level = tile_mark == level
+            cell = cell_ref[:, here]
+            high = lax.shift_right_logical(cell, 6).astype(jnp.float32).astype(jnp.bfloat16)
+            low = (cell & 63).astype(jnp.float32).astype(jnp.bfloat16)
+            coded[:LANES, here] = jnp.where(at_level, high, zero)
+            coded[LANES:, here] = jnp.where(at_level, low, zero)
+            before = before + mine[:, width:]
+        return before
+
+    total = lax.fori_loop(0, chunks // TOGETHER, rank, first) - first
     to_smem = pltpu.make_async_copy(pos_f, pos_s, sem)
     to_smem.start()
-    coded[...] = jnp.zeros_like(coded)
+    cells = lax.dot_general(
+        hits[...], coded[...], (((1,), (1,)), ((), ())), preferred_element_type=jnp.float32
+    )
+    load.wait()
+
+    def widen(i, rows):
+        at = pl.ds(pl.multiple_of(jnp.minimum(i, chunks - 1) * width, width), width)
+        rows[...] = feats[at, :].astype(jnp.float32)
+
+    def move(i, rows):
+        for k in range(width):
+            slot = pos_s.at[pl.ds(k, points - width + 1)][i * width]
+            slots[pl.ds(slot, 1), :] = rows[k : k + 1, :]
+
+    widen(0, even)
     to_smem.wait()
 
-    def move(i, carry):
-        start = i * width
-        for k in range(width):
-            slots[pl.ds(pos_s[start + k], 1), :] = rows[pl.ds(start + k, 1), :]
-        live = start + lane < count
-        here = pl.ds(pl.multiple_of(start, width), width)
-        hit = tile_id == jnp.where(live, tile_ref[:, here], -1)
-        level = pos_v[pl.ds(i, 1), :] & (LANES - 1)
-        at_level = lax.broadcasted_iota(jnp.int32, (LANES, width), 0) == level
-        cell = cell_ref[:, here]
-        high = lax.shift_right_logical(cell, 6).astype(jnp.float32)
-        low = (cell & 63).astype(jnp.float32)
-        values = jnp.concatenate([jnp.where(hit, high, 0.0), jnp.where(hit, low, 0.0)], axis=0)
-        coded[...] += lax.dot_general(
-            values.astype(jnp.bfloat16),
-            jnp.where(at_level, 1.0, 0.0).astype(jnp.bfloat16),
-            (((1,), (1,)), ((), ())),
-            preferred_element_type=jnp.float32,
-        )
+    def two(q, carry):
+        widen(2 * q + 1, odd)
+        move(2 * q, even)
+        widen(2 * q + 2, even)
+        move(2 * q + 1, odd)
         return carry
 
-    lax.fori_loop(0, (count + width - 1) // width, move, 0)
+    lax.fori_loop(0, lax.shift_right_logical(count + (2 * width - 1), 9), two, 0)
     spot = lax.broadcasted_iota(jnp.int32, (tiles, LANES), 1).astype(jnp.float32)
-    high = jnp.where(spot < total, coded[:tiles, :], float(DUMP // 64))
-    low = jnp.where(spot < total, coded[tiles:, :], 0.0)
-    slots[pl.ds(CAP, tiles, LANES), :] = jnp.where(spot == LANES - 1, 0.0, high)
-    slots[pl.ds(CAP + 1, tiles, LANES), :] = jnp.where(spot == LANES - 1, total, low)
+    high = jnp.where(spot < total, cells[:, :LANES], float(DUMP // 64))
+    low = jnp.where(spot < total, cells[:, LANES:], 0.0)
+    slots[pl.ds(CAP, tiles, LANES), :] = high
+    slots[pl.ds(CAP + 1, tiles, LANES), :] = low
 
     def narrow(t, carry):
-        out_ref[t] = slots[pl.ds(pl.multiple_of(t * LANES, LANES), BLOCK), :].astype(jnp.bfloat16)
+        sent[t] = slots[pl.ds(pl.multiple_of(t * LANES, LANES), BLOCK), :].astype(jnp.bfloat16)
         return carry
 
-    lax.fori_loop(0, tiles, narrow, 0, unroll=4)
-
-
-def add_kernel(got_ref, out_ref, top_ref, bottom_ref, left_ref, right_ref, rows, cells_f, cells_s, sem, *sums):
-    sources = got_ref.shape[0]
-
-    def widen(s, carry):
-        rows[pl.ds(pl.multiple_of(s * BLOCK, 8), BLOCK), :] = got_ref[s].astype(jnp.float32)
-        return carry
-
-    lax.fori_loop(0, sources, widen, 0, unroll=4)
-    high = rows[pl.ds(CAP, sources, BLOCK), :].astype(jnp.int32)
-    low = rows[pl.ds(CAP + 1, sources, BLOCK), :].astype(jnp.int32)
+    parts = out_sems.shape[0]
+    share = tiles // parts
+    stores = []
+    for k in range(parts):
+        lax.fori_loop(k * share, (k + 1) * share, narrow, 0, unroll=4)
+        part = pl.ds(k * share, share)
+        stores.append(pltpu.make_async_copy(sent.at[part], out_hbm.at[part], out_sems.at[k]))
+        stores[-1].start()
+    for store in stores:
+        store.wait()
+
+
+def add_kernel(
+    got_hbm, out_ref, top_ref, bottom_ref, left_ref, right_ref,
+    got, even, odd, meta, coded, cells_f, cells_s, sem, meta_sem, in_sems, *sums,
+):
+    sources = got_hbm.shape[0]
+    codes = pltpu.make_async_copy(got_hbm.at[:, pl.ds(CAP, 8), :], meta, meta_sem)
+    codes.start()
+    parts = in_sems.shape[0]
+    share = sources // parts
+    loads = []
+    for k in range(parts):
+        part = pl.ds(k * share, share)
+        loads.append(pltpu.make_async_copy(got_hbm.at[part, pl.ds(0, CAP), :], got.at[part], in_sems.at[k]))
+        loads[-1].start()
+    codes.wait()
+    coded[...] = meta[...].astype(jnp.float32).reshape(coded.shape)
+    high = coded[pl.ds(0, sources, 8), :].astype(jnp.int32)
+    low = coded[pl.ds(1, sources, 8), :].astype(jnp.int32)
     cells_f[...] = (high * 64 + low).reshape(sources * LANES)
     to_smem = pltpu.make_async_copy(cells_f, cells_s, sem)
     to_smem.start()
@@ -110,23 +146,28 @@
     lax.fori_loop(0, CELLS // 256, clear, 0)
     for part in sums:
         part[pl.ds(CELLS, 8), :] = jnp.zeros((8, LANES), jnp.float32)
+
+    def widen(s, rows):
+        rows[...] = got[jnp.minimum(s, sources - 1)].astype(jnp.float32)
+
+    def add(s, rows):
+        for j in range(CAP):
+            cell = pl.ds(cells_s.at[pl.ds(j, (sources - 1) * LANES + 1)][s * LANES], 1)
+            part = sums[j % SUMS]
+            part[cell, :] = part[cell, :] + rows[j : j + 1, :]
+
+    def two(q, carry):
+        widen(2 * q + 1, odd)
+        add(2 * q, even)
+        widen(2 * q + 2, even)
+        add(2 * q + 1, odd)
+        return carry
+
     to_smem.wait()
-
-    def one(s, carry):
-        number = cells_s[s * LANES + LANES - 1]
-
-        def few(g, inner):
-            at = s * LANES + g * GROUP
-            base = s * BLOCK + g * GROUP
-            for j in range(GROUP):
-                cell = pl.ds(cells_s[at + j], 1)
-                part = sums[j % SUMS]
-                part[cell, :] = part[cell, :] + rows[pl.ds(base + j, 1), :]
-            return inner
-
-        return lax.fori_loop(0, lax.shift_right_logical(number + (GROUP - 1), 4), few, carry)
-
-    lax.fori_loop(0, sources, one, 0)
+    for load in loads:
+        load.wait()
+    widen(0, even)
+    lax.fori_loop(0, sources // 2, two, 0)
     step = 256
 
     def close(i, carry):
@@ -216,25 +257,32 @@
 
 VMEM = pl.BlockSpec(memory_space=pltpu.VMEM)
 SMEM = pl.BlockSpec(memory_space=pltpu.SMEM)
+ANY = pl.BlockSpec(memory_space=pl.ANY)
 
 
 def pack(point_feats, point_tile, point_cell, point_count, devices):
     points, channels = point_feats.shape
     width = 2 * LANES
     chunks = points // width
+    bf16, f32 = jnp.bfloat16, jnp.float32
     return pl.pallas_call(
         pack_kernel,
-        out_shape=jax.ShapeDtypeStruct((devices, BLOCK, channels), jnp.bfloat16),
-        in_specs=[SMEM, VMEM, VMEM, VMEM],
-        out_specs=VMEM,
+        out_shape=jax.ShapeDtypeStruct((devices, BLOCK, channels), bf16),
+        in_specs=[SMEM, VMEM, VMEM, ANY],
+        out_specs=ANY,
         scratch_shapes=[
-            pltpu.VMEM((points, channels), jnp.float32),
-            pltpu.VMEM((devices * LANES, channels), jnp.float32),
-            pltpu.VMEM((chunks, width), jnp.int32),
+            pltpu.VMEM((points, channels), bf16),
+            pltpu.VMEM((width, channels), f32),
+            pltpu.VMEM((width, channels), f32),
+            pltpu.VMEM((devices * LANES, channels), f32),
             pltpu.VMEM((points,), jnp.int32),
             pltpu.SMEM((points,), jnp.int32),
-            pltpu.VMEM((2 * devices, LANES), jnp.float32),
+            pltpu.VMEM((devices, points), bf16),
+            pltpu.VMEM((2 * LANES, points), bf16),
+            pltpu.VMEM((devices, BLOCK, channels), bf16),
             pltpu.SemaphoreType.DMA,
+            pltpu.SemaphoreType.DMA,
+            pltpu.SemaphoreType.DMA((4,)),
         ],
         name="pack",
     )(
@@ -247,21 +295,28 @@
 
 def add_up(got):
     devices, block, channels = got.shape
+    bf16, f32 = jnp.bfloat16, jnp.float32
     return pl.pallas_call(
         add_kernel,
         out_shape=[
-            jax.ShapeDtypeStruct((rows, channels), jnp.bfloat16)
+            jax.ShapeDtypeStruct((rows, channels), bf16)
             for rows in (CELLS, COLS_DEV, COLS_DEV, ROWS_DEV, ROWS_DEV)
         ],
-        in_specs=[VMEM],
+        in_specs=[ANY],
         out_specs=[VMEM] * 5,
         scratch_shapes=[
-            pltpu.VMEM((devices * block, channels), jnp.float32),
+            pltpu.VMEM((devices, CAP, channels), bf16),
+            pltpu.VMEM((CAP, channels), f32),
+            pltpu.VMEM((CAP, channels), f32),
+            pltpu.VMEM((devices, 8, channels), bf16),
+            pltpu.VMEM((devices * 8, channels), f32),
             pltpu.VMEM((devices * LANES,), jnp.int32),
             pltpu.SMEM((devices * LANES,), jnp.int32),
             pltpu.SemaphoreType.DMA,
+            pltpu.SemaphoreType.DMA,
+            pltpu.SemaphoreType.DMA((4,)),
         ]
-        + [pltpu.VMEM((CELLS + 8, channels), jnp.float32)] * SUMS,
+        + [pltpu.VMEM((CELLS + 8, channels), f32)] * SUMS,
         name="add_up",
     )(got)
 
@@ -302,12 +357,11 @@
 def close_edges(inner, sums_left, sums_right, first, last, west, east, weight, bias):
     channels = weight.shape[-1]
     whole = (ROWS_DEV, COLS_DEV, channels)
-    anywhere = pl.BlockSpec(memory_space=pl.ANY)
     return pl.pallas_call(
         edge_kernel,
         out_shape=jax.ShapeDtypeStruct(whole, jnp.bfloat16),
-        in_specs=[anywhere] + [VMEM] * 8,
-        out_specs=anywhere,
+        in_specs=[ANY] + [VMEM] * 8,
+        out_specs=ANY,
         input_output_aliases={0: 0},
         scratch_shapes=[
             pltpu.VMEM((ROWS_DEV + 8, channels), jnp.float32),

time: 112 us -> 99.7 us (0.89)
  the two profiles are of different devices: /device:TPU:23 before, /device:TPU:6 now
where the time goes in v4:
time: 99.7 us; the launch traced here: 97.7 us
  blocking collectives  49 us (49%)
  Pallas kernels  31.2 us (31%)
  starting transfers between devices  8.4 us (8%)
  waiting for transfers between devices  5.79 us (6%)
  other arithmetic  1.38 us (1%)
  between operations  1.37 us (1%)
    all_to_all x1, blocking collectives, shards(): lax.all_to_all(sent, ('gx', 'gy'), split_axis=0, concat_axis=0, tiled=True)  49 us
    pallas_call x1, Pallas kernels, add_up(): pl.pallas_call(add_kernel, out_shape=[jax.ShapeDtypeStruct((rows, channel...  13.6 us
    pallas_call x1, Pallas kernels, pack(): pl.pallas_call(pack_kernel, out_shape=jax.ShapeDtypeStruct((devices, BLOC...  11.3 us
    ppermute x4, starting transfers between devices, shift(): return lax.ppermute(cells, axis, pairs)  8.4 us
    ppermute x4, waiting for transfers between devices, shift(): return lax.ppermute(cells, axis, pairs)  5.79 us
    pallas_call x1, Pallas kernels, conv(): pl.pallas_call(conv_kernel, out_shape=[jax.ShapeDtypeStruct((cells, chann...  4.39 us
  transfers between devices with their start and end apart: 4, of which 2 were waited for; matrix products, arithmetic and copies ran while one was open for 1% of the time, Pallas kernels for 4%

profile of v4, /device:TPU:6, one launch (start us, length us, event | category | flops | bytes accessed | tf_op | source)
XLA Modules:
  0.0 97.7 jit_solution(5932906439986361419)
XLA Ops:
  1.3 11.3 %pack.1 = bf16[128,88,128]{2,1,0:T(8,128)(2,1)} custom-call(s32[1]{0:T(128)S(6)} %copy.10.count_ref, s32[1,8192]{1,0:T(1,128)} %bitcast.6, s32[1,8192]{1,0:T(1,128)} %bitcast.7, bf16[8192,128]{1,0:T(8,128)(2,1)} %feats_hbm.1), custom_call_target="tpu_custom_call" | custom-call | tf_op jit(solution)/shard_map/pack/pallas_call | solution.py:268
  12.6 49.0 %all_to_all.5.got_hbm = bf16[128,88,128]{2,1,0:T(8,128)(2,1)} all-to-all(bf16[128,88,128]{2,1,0:T(8,128)(2,1)} %pack.1), channel_id=1, replica_groups=mesh['gx'=16,'gy'=8] {'gx','gy'}, dimensions={0} | all-to-all | bytes 5767168 | tf_op jit(solution)/shard_map/all_to_all | solution.py:379
  61.5 13.6 %add_up.1 = (bf16[4096,128]{1,0:T(8,128)(2,1)}, bf16[256,128]{1,0:T(8,128)(2,1)}, bf16[256,128]{1,0:T(8,128)(2,1)}, bf16[16,128]{1,0:T(8,128)(2,1)}, bf16[16,128]{1,0:T(8,128)(2,1)}) custom-call(bf16[128,88,128]{2,1,0:T(8,128)(2,1)} %all_to_all.5.got_hbm), custom_call_target="tpu_custom_call" | custom-call | tf_op jit(solution)/shard_map/add_up/pallas_call | solution.py:299
  75.2 3.2 %collective-permute-start = (bf16[256,128]{1,0:T(8,128)(2,1)}, bf16[256,128]{1,0:T(8,128)(2,1)S(1)}, u32[]{:S(2)}, u32[]{:S(2)}) collective-permute-start(bf16[256,128]{1,0:T(8,128)(2,1)} %get-tuple-element.13), channel_id=1, source_target_pairs={{0,8},{8,16},{16,24},{24,32},{32,40},{40,48},{48,56},{56,64},{64,7... | collective-permute-start | bytes 196616 | tf_op jit(solution)/shard_map/ppermute | solution.py:327
  78.4 2.7 %collective-permute-start.1 = (bf16[256,128]{1,0:T(8,128)(2,1)}, bf16[256,128]{1,0:T(8,128)(2,1)S(1)}, u32[]{:S(2)}, u32[]{:S(2)}) collective-permute-start(bf16[256,128]{1,0:T(8,128)(2,1)} %get-tuple-element.14), channel_id=1, source_target_pairs={{8,0},{16,8},{24,16},{32,24},{40,32},{48,40},{56,48},{64,56},{72,6... | collective-permute-start | bytes 196616 | tf_op jit(solution)/shard_map/ppermute | solution.py:327
  81.0 0.5 collective-permute-done.up_ref
  81.5 0.0 copy-start.2
  81.6 5.3 %collective-permute-done.1.down_ref = bf16[256,128]{1,0:T(8,128)(2,1)S(1)} collective-permute-done((bf16[256,128]{1,0:T(8,128)(2,1)}, bf16[256,128]{1,0:T(8,128)(2,1)S(1)}, u32[]{:S(2)}, u32[]{:S(2)}) %collective-permute-start.1) | collective-permute-done | bytes 65568 | tf_op jit(solution)/shard_map/ppermute | solution.py:327
  86.8 0.0 copy-start.3
  86.8 0.7 pad_maximum_fusion
  87.5 1.3 %collective-permute-start.2 = (bf16[18,128]{1,0:T(8,128)(2,1)S(1)}, bf16[18,128]{1,0:T(8,128)(2,1)S(1)}, u32[]{:S(2)}, u32[]{:S(2)}) collective-permute-start(bf16[18,128]{1,0:T(8,128)(2,1)S(1)} %pad_maximum_fusion), channel_id=1, source_target_pairs={{0,1},{1,2},{2,3},{3,4},{4,5},{5,6},{6,7},{8,9},{9,10},{10,11},{11... | collective-permute-start | bytes 13832 | tf_op jit(solution)/shard_map/ppermute | solution.py:327
  88.8 0.7 pad_maximum_fusion.1
  89.5 1.3 %collective-permute-start.3 = (bf16[18,128]{1,0:T(8,128)(2,1)S(1)}, bf16[18,128]{1,0:T(8,128)(2,1)S(1)}, u32[]{:S(2)}, u32[]{:S(2)}) collective-permute-start(bf16[18,128]{1,0:T(8,128)(2,1)S(1)} %pad_maximum_fusion.1), channel_id=1, source_target_pairs={{1,0},{2,1},{3,2},{4,3},{5,4},{6,5},{7,6},{9,8},{10,9},{11,10},{12... | collective-permute-start | bytes 13832 | tf_op jit(solution)/shard_map/ppermute | solution.py:327
  90.8 0.0 copy-done.2
  90.8 0.0 copy-done.3
  90.8 4.4 %conv.1 = (bf16[4096,128]{1,0:T(8,128)(2,1)}, f32[16,128]{1,0:T(8,128)}, f32[16,128]{1,0:T(8,128)}, bf16[16,16,128]{2,1,0:T(8,128)(2,1)}, bf16[16,16,128]{2,1,0:T(8,128)(2,1)}) custom-call(bf16[4096,128]{1,0:T(8,128)(2,1)} %get-tuple-element.12.bev_ref, bf16[256,128]{1,0:T(8,128)(2,1)} %copy-done.2, bf16[256,128]{1,0:T(8,128)(2,1)} %copy-done.3, ...), custom_call_target="tpu_custom_call" | custom-call | flops 1207959552 | bytes 2097152 | tf_op jit(solution)/shard_map/conv/pallas_call | solution.py:334
  95.2 0.0 collective-permute-done.2.west_ref
  95.2 0.0 copy-start
  95.2 0.0 collective-permute-done.3.east_ref
  95.2 0.0 copy-start.1
  95.2 0.6 copy-done
  95.8 0.0 copy-done.1
  95.8 1.9 %edges.1 = bf16[16,256,128]{2,1,0:T(8,128)(2,1)} custom-call(bf16[16,256,128]{2,1,0:T(8,128)(2,1)} %bitcast.5, f32[16,128]{1,0:T(8,128)} %get-tuple-element.16.left_ref, f32[16,128]{1,0:T(8,128)} %get-tuple-element.17.right_ref, bf16[16,16,128]{2,1,0:T(8,128)(2,1)} %get-tuple-element.18.first_ref, ...), custom_call_target="tpu_custom_call", output_to_operand_aliasing={{}: (0, {})} | custom-call | tf_op jit(solution)/shard_map/edges/pallas_call | solution.py:360
  (2 shorter events, 0.0 us)
Async XLA Ops:
  75.2 6.4 %collective-permute-start = (bf16[256,128]{1,0:T(8,128)(2,1)}, bf16[256,128]{1,0:T(8,128)(2,1)S(1)}, u32[]{:S(2)}, u32[]{:S(2)}) collective-permute-start(bf16[256,128]{1,0:T(8,128)(2,1)} %get-tuple-element.13), channel_id=1, source_target_pairs={{0,8},{8,16},{16,24},{24,32},{32,40},{40,48},{48,56},{56,64},{64,7... | collective-permute-start | bytes 196616 | tf_op jit(solution)/shard_map/ppermute | solution.py:327
  78.4 8.5 %collective-permute-start.1 = (bf16[256,128]{1,0:T(8,128)(2,1)}, bf16[256,128]{1,0:T(8,128)(2,1)S(1)}, u32[]{:S(2)}, u32[]{:S(2)}) collective-permute-start(bf16[256,128]{1,0:T(8,128)(2,1)} %get-tuple-element.14), channel_id=1, source_target_pairs={{8,0},{16,8},{24,16},{32,24},{40,32},{48,40},{56,48},{64,56},{72,6... | collective-permute-start | bytes 196616 | tf_op jit(solution)/shard_map/ppermute | solution.py:327
  81.5 9.2 %copy-start.2 = (bf16[256,128]{1,0:T(8,128)(2,1)}, bf16[256,128]{1,0:T(8,128)(2,1)S(1)}, u32[]{:S(2)}) copy-start(bf16[256,128]{1,0:T(8,128)(2,1)S(1)} %collective-permute-done.up_ref) | copy-start | bytes 196612
  86.8 4.0 %copy-start.3 = (bf16[256,128]{1,0:T(8,128)(2,1)}, bf16[256,128]{1,0:T(8,128)(2,1)S(1)}, u32[]{:S(2)}) copy-start(bf16[256,128]{1,0:T(8,128)(2,1)S(1)} %collective-permute-done.1.down_ref) | copy-start | bytes 196612
  87.5 7.7 %collective-permute-start.2 = (bf16[18,128]{1,0:T(8,128)(2,1)S(1)}, bf16[18,128]{1,0:T(8,128)(2,1)S(1)}, u32[]{:S(2)}, u32[]{:S(2)}) collective-permute-start(bf16[18,128]{1,0:T(8,128)(2,1)S(1)} %pad_maximum_fusion), channel_id=1, source_target_pairs={{0,1},{1,2},{2,3},{3,4},{4,5},{5,6},{6,7},{8,9},{9,10},{10,11},{11... | collective-permute-start | bytes 13832 | tf_op jit(solution)/shard_map/ppermute | solution.py:327
  89.5 5.7 %collective-permute-start.3 = (bf16[18,128]{1,0:T(8,128)(2,1)S(1)}, bf16[18,128]{1,0:T(8,128)(2,1)S(1)}, u32[]{:S(2)}, u32[]{:S(2)}) collective-permute-start(bf16[18,128]{1,0:T(8,128)(2,1)S(1)} %pad_maximum_fusion.1), channel_id=1, source_target_pairs={{1,0},{2,1},{3,2},{4,3},{5,4},{6,5},{7,6},{9,8},{10,9},{11,10},{12... | collective-permute-start | bytes 13832 | tf_op jit(solution)/shard_map/ppermute | solution.py:327
  95.2 0.6 copy-start
  95.2 0.6 copy-start.1

commit v5 on v4

v5 whole, which is shorter than its diff:
```python
import functools

import jax
import jax.numpy as jnp
from jax import lax
from jax.experimental import pallas as pl
from jax.experimental.pallas import tpu as pltpu
from jax.sharding import PartitionSpec as P

COLS_DEV = 256
ROWS_DEV = 16
CELLS = ROWS_DEV * COLS_DEV
LANES = 128
CAP = 80
BLOCK = 88
SUMS = 8
SPARE = 6
HALO = 2 * ROWS_DEV
DUMP = CELLS + HALO
EDGE = 16
MOVES = 512
TOGETHER = 4


def pack_kernel(
    across, count_ref, cell_ref, tile_ref, feats_hbm, out_hbm,
    feats, rows, slots, pos_f, pos_s, hits, coded, twins, twin_code, twin_f, twin_s, sent,
    sem, twin_sem, in_sem, out_sems,
):
    count = count_ref[0]
    width = 2 * LANES
    points = tile_ref.shape[1]
    chunks = points // width
    tiles = out_hbm.shape[0]
    load = pltpu.make_async_copy(feats_hbm, feats, in_sem)
    load.start()
    tile_id = lax.broadcasted_iota(jnp.int32, (tiles, width), 0)
    lane = lax.broadcasted_iota(jnp.int32, (1, width), 1)
    source = lax.broadcasted_iota(jnp.int32, (width, width + LANES), 0)
    column = lax.broadcasted_iota(jnp.int32, (width, width + LANES), 1)
    one, zero = jnp.ones((), jnp.bfloat16), jnp.zeros((), jnp.bfloat16)
    upto = jnp.where((source <= column) | (column >= width), 1.0, 0.0).astype(jnp.bfloat16)
    first = (lax.broadcasted_iota(jnp.int32, (tiles, LANES), 0) * LANES - 1).astype(jnp.float32)
    tile_mark = tile_id.astype(jnp.float32).astype(jnp.bfloat16)
    spare_id = lax.broadcasted_iota(jnp.int32, (8, width), 0)
    nothing = jnp.zeros((8, width), jnp.float32)
    twin_code[16:80, :] = jnp.zeros((64, points), jnp.bfloat16)
    twin_code[96:, :] = jnp.zeros((32, points), jnp.bfloat16)

    def as_bf16(x):
        return x.astype(jnp.float32).astype(jnp.bfloat16)

    def rank(g, befores):
        before, twin_before = befores
        marks, twin_marks, info = [], [], []
        for c in range(TOGETHER):
            i = g * TOGETHER + c
            here = pl.ds(pl.multiple_of(i * width, width), width)
            live = i * width + lane < count
            tile = jnp.where(live, tile_ref[:, here], tiles)
            mark = jnp.where(tile_mark == as_bf16(tile), one, zero)
            hits[:, here] = mark
            marks.append(mark)
            cell = cell_ref[:, here]
            along = cell & (COLS_DEV - 1)
            place = tile & (across - 1)
            west = live & (along == 0) & (place > 0)
            east = live & (along == COLS_DEV - 1) & (place < across - 1)
            twin = jnp.where(west, tile - 1, jnp.where(east, tile + 1, tiles))
            twin_mark = jnp.where(tile_mark == as_bf16(twin), one, zero)
            twins[:, here] = twin_mark
            twin_marks.append(twin_mark)
            code = jnp.where(west, ROWS_DEV, 0) + lax.shift_right_logical(cell, 8)
            info.append((tile, live, here, i, cell, twin, code))
        found = jnp.dot(jnp.concatenate(marks, axis=0), upto, preferred_element_type=jnp.float32)
        twin_found = jnp.dot(jnp.concatenate(twin_marks, axis=0), upto, preferred_element_type=jnp.float32)
        for c in range(TOGETHER):
            tile, live, here, i, cell, twin, code = info[c]
            mine = found[c * tiles : (c + 1) * tiles, :]
            place = mine[:, :width] + jnp.concatenate([before] * (width // LANES), axis=1)
            slot = jnp.sum(jnp.where(tile_id == tile, place, 0.0), axis=0, keepdims=True).astype(jnp.int32)
            pos_f[pl.ds(pl.multiple_of(i * width, width), width)] = jnp.where(live, slot, tiles * LANES - 1).reshape(width)
            at_level = tile_mark == as_bf16(slot & (LANES - 1))
            coded[:LANES, here] = jnp.where(at_level, as_bf16(lax.shift_right_logical(cell, 6)), zero)
            coded[LANES:, here] = jnp.where(at_level, as_bf16(cell & 63), zero)
            before = before + mine[:, width:]
            theirs = twin_found[c * tiles : (c + 1) * tiles, :]
            place = theirs[:, :width] + jnp.concatenate([twin_before] * (width // LANES), axis=1)
            order = jnp.sum(jnp.where(tile_id == twin, place, 0.0), axis=0, keepdims=True).astype(jnp.int32) - 1
            at_order = spare_id == order
            point = i * width + lane
            high = jnp.where(at_order, (point & -LANES).astype(jnp.float32), nothing)
            low = jnp.where(at_order, (point & (LANES - 1)).astype(jnp.float32), nothing)
            value = jnp.where(at_order, code.astype(jnp.float32), nothing)
            twin_code[:16, here] = jnp.concatenate([high, low], axis=0).astype(jnp.bfloat16)
            twin_code[80:96, here] = jnp.concatenate([value, nothing], axis=0).astype(jnp.bfloat16)
            twin_before = twin_before + theirs[:, width:]
        return before, twin_before

    before, twin_total = lax.fori_loop(
        0, chunks // TOGETHER, rank, (first, jnp.zeros((tiles, LANES), jnp.float32))
    )
    total = before - first
    to_smem = pltpu.make_async_copy(pos_f, pos_s, sem)
    to_smem.start()
    across_lanes = (((1,), (1,)), ((), ()))
    extra = lax.dot_general(twins[...], twin_code[...], across_lanes, preferred_element_type=jnp.float32)
    origin = (extra + pltpu.roll(extra, LANES - 8, 1)).astype(jnp.int32)
    spot = lax.broadcasted_iota(jnp.int32, (tiles, LANES), 1).astype(jnp.float32)
    known = spot < jnp.minimum(twin_total, float(SPARE))
    twin_f[...] = jnp.where(known, origin, 0).reshape(tiles * LANES)
    twins_to_smem = pltpu.make_async_copy(twin_f, twin_s, twin_sem)
    twins_to_smem.start()
    load.wait()
    rows[...] = feats[...].astype(jnp.float32)
    cells = lax.dot_general(hits[...], coded[...], across_lanes, preferred_element_type=jnp.float32)
    to_smem.wait()

    def move(i, carry):
        for k in range(MOVES):
            slot = pos_s.at[pl.ds(k, points - MOVES + 1)][i * MOVES]
            slots[pl.ds(slot, 1), :] = rows[pl.ds(i * MOVES + k, 1), :]
        return carry

    lax.fori_loop(0, (count + (MOVES - 1)) // MOVES, move, 0)
    twins_to_smem.wait()

    def move_twins(t, carry):
        for u in range(8):
            for j in range(SPARE):
                point = twin_s.at[pl.ds(u * LANES + j, (tiles - 8) * LANES + 1)][t * (8 * LANES)]
                slots[pl.ds(t * (8 * LANES) + u * LANES + CAP + 2 + j, 1), :] = rows[pl.ds(point, 1), :]
        return carry

    lax.fori_loop(0, tiles // 8, move_twins, 0)
    high = jnp.where(spot < total, cells[:, :LANES], float(DUMP // 64))
    low = jnp.where(spot < total, cells[:, LANES:], float(DUMP % 64))
    low = jnp.where((spot >= CAP) & (spot - CAP < jnp.minimum(twin_total, float(SPARE))), extra, low)
    full = jnp.max(twin_total, axis=0, keepdims=True) > SPARE
    high = jnp.where(spot == LANES - 1, 0.0, high)
    low = jnp.where(spot == LANES - 1, jnp.where(full, 1.0, 0.0), low)
    slots[pl.ds(CAP, tiles, LANES), :] = high
    slots[pl.ds(CAP + 1, tiles, LANES), :] = low

    def narrow(t, carry):
        sent[t] = slots[pl.ds(pl.multiple_of(t * LANES, LANES), BLOCK), :].astype(jnp.bfloat16)
        return carry

    parts = out_sems.shape[0]
    share = tiles // parts
    stores = []
    for k in range(parts):
        lax.fori_loop(k * share, (k + 1) * share, narrow, 0, unroll=4)
        part = pl.ds(k * share, share)
        stores.append(pltpu.make_async_copy(sent.at[part], out_hbm.at[part], out_sems.at[k]))
        stores[-1].start()
    for store in stores:
        store.wait()


def add_kernel(
    got_hbm, out_ref, top_ref, bottom_ref, left_ref, right_ref, west_ref, east_ref, full_ref,
    got, even, odd, meta, coded, cells_f, cells_s, sem, meta_sem, in_sems, *sums,
):
    sources = got_hbm.shape[0]
    codes = pltpu.make_async_copy(got_hbm.at[:, pl.ds(CAP, 8), :], meta, meta_sem)
    codes.start()
    parts = in_sems.shape[0]
    share = sources // parts
    loads = []
    for k in range(parts):
        part = pl.ds(k * share, share)
        loads.append(pltpu.make_async_copy(got_hbm.at[part], got.at[part], in_sems.at[k]))
        loads[-1].start()
    codes.wait()
    coded[...] = meta[...].astype(jnp.float32).reshape(coded.shape)
    high = coded[pl.ds(0, sources, 8), :].astype(jnp.int32)
    low = coded[pl.ds(1, sources, 8), :].astype(jnp.int32)
    cells = high * 64 + low
    full_ref[...] = jnp.broadcast_to(jnp.max(cells[:, LANES - 1 :], axis=0, keepdims=True), full_ref.shape)
    cells_f[...] = cells.reshape(sources * LANES)
    to_smem = pltpu.make_async_copy(cells_f, cells_s, sem)
    to_smem.start()

    def clear(i, carry):
        for part in sums:
            part[pl.ds(pl.multiple_of(i * 256, 256), 256), :] = jnp.zeros((256, LANES), jnp.float32)
        return carry

    lax.fori_loop(0, CELLS // 256, clear, 0)
    for part in sums:
        part[pl.ds(CELLS, HALO + 8), :] = jnp.zeros((HALO + 8, LANES), jnp.float32)

    def widen(s, rows):
        rows[...] = got[jnp.minimum(s, sources - 1)].astype(jnp.float32)

    def add(s, rows):
        for j in range(CAP + SPARE):
            cell = pl.ds(cells_s.at[pl.ds(j, (sources - 1) * LANES + 1)][s * LANES], 1)
            part = sums[j % SUMS]
            k = j if j < CAP else j + 2
            part[cell, :] = part[cell, :] + rows[k : k + 1, :]

    def two(q, carry):
        widen(2 * q + 1, odd)
        add(2 * q, even)
        widen(2 * q + 2, even)
        add(2 * q + 1, odd)
        return carry

    to_smem.wait()
    for load in loads:
        load.wait()
    widen(0, even)
    lax.fori_loop(0, sources // 2, two, 0)
    step = 256

    def close(i, carry):
        at = pl.ds(pl.multiple_of(i * step, step), step)
        total = sums[0][at, :]
        for part in sums[1:]:
            total = total + part[at, :]
        out_ref[at, :] = total.astype(jnp.bfloat16)
        return carry

    lax.fori_loop(0, CELLS // step, close, 0)

    def column(start, stride):
        at = pl.ds(start, ROWS_DEV, stride)
        total = sums[0][at, :]
        for part in sums[1:]:
            total = total + part[at, :]
        return total

    left_ref[...] = column(0, COLS_DEV).astype(jnp.bfloat16)
    right_ref[...] = column(COLS_DEV - 1, COLS_DEV).astype(jnp.bfloat16)
    west, east = column(CELLS, 1), column(CELLS + ROWS_DEV, 1)
    west_ref[...] = west.astype(jnp.bfloat16)
    east_ref[...] = east.astype(jnp.bfloat16)
    spot = lax.broadcasted_iota(jnp.int32, (EDGE, LANES), 0)
    for ref, r in ((top_ref, 0), (bottom_ref, ROWS_DEV - 1)):
        ref[:COLS_DEV, :] = out_ref[r * COLS_DEV : (r + 1) * COLS_DEV, :]
        corners = jnp.where(spot == 0, west[r : r + 1, :], jnp.where(spot == 1, east[r : r + 1, :], 0.0))
        ref[COLS_DEV:, :] = corners.astype(jnp.bfloat16)


def conv_kernel(
    bev_ref, up_ref, down_ref, west_ref, east_ref, weight_ref, bias_ref,
    out_ref, wide, before, after, side,
):
    for i in range(4):
        for b in range(3):
            for o in range(2):
                block = (slice(i * LANES, (i + 1) * LANES), slice((2 * b + o) * LANES, (2 * b + o + 1) * LANES))
                wide[block] = weight_ref[i - o, b] if 0 <= i - o < 3 else jnp.zeros((LANES, LANES), jnp.bfloat16)
    bias = bias_ref[...]
    pairs = ROWS_DEV // 2
    above = up_ref[COLS_DEV:, :].astype(jnp.float32)
    below = down_ref[COLS_DEV:, :].astype(jnp.float32)

    def beside(ref, corner, start):
        side[:1, :] = above[corner : corner + 1, :]
        side[1 : ROWS_DEV + 1, :] = ref[...].astype(jnp.float32)
        side[ROWS_DEV + 1 : ROWS_DEV + 2, :] = below[corner : corner + 1, :]
        four = jnp.concatenate([side[pl.ds(i, pairs, 2), :] for i in range(4)], axis=1)
        return jnp.dot(
            four.astype(jnp.bfloat16), wide[:, start : start + 2 * LANES], preferred_element_type=jnp.float32
        )

    west = beside(west_ref, 0, 0)
    east = beside(east_ref, 1, 4 * LANES)

    def row(r):
        if r < 0:
            return up_ref[:COLS_DEV, :]
        if r >= ROWS_DEV:
            return down_ref[:COLS_DEV, :]
        return bev_ref[r * COLS_DEV : (r + 1) * COLS_DEV, :]

    for p in range(pairs):
        four = jnp.concatenate([row(2 * p - 1 + i) for i in range(4)], axis=1)
        taps = jnp.dot(four, wide[...], preferred_element_type=jnp.float32)
        before[7:8, :] = west[p : p + 1, :]
        before[8:, :] = taps[:, : 2 * LANES]
        after[:COLS_DEV, :] = taps[:, 4 * LANES :]
        after[COLS_DEV : COLS_DEV + 1, :] = east[p : p + 1, :]
        total = taps[:, 2 * LANES : 4 * LANES] + before[7 : 7 + COLS_DEV, :] + after[1 : 1 + COLS_DEV, :]
        for o in range(2):
            r = 2 * p + o
            part = total[:, o * LANES : (o + 1) * LANES]
            out_ref[r * COLS_DEV : (r + 1) * COLS_DEV, :] = jnp.maximum(part + bias, 0.0).astype(jnp.bfloat16)


VMEM = pl.BlockSpec(memory_space=pltpu.VMEM)
SMEM = pl.BlockSpec(memory_space=pltpu.SMEM)
ANY = pl.BlockSpec(memory_space=pl.ANY)


def pack(point_feats, point_tile, point_cell, point_count, devices, across=8):
    points, channels = point_feats.shape
    if across & (across - 1):
        raise ValueError("across")
    bf16, f32, i32 = jnp.bfloat16, jnp.float32, jnp.int32
    return pl.pallas_call(
        functools.partial(pack_kernel, across),
        out_shape=jax.ShapeDtypeStruct((devices, BLOCK, channels), bf16),
        in_specs=[SMEM, VMEM, VMEM, ANY],
        out_specs=ANY,
        scratch_shapes=[
            pltpu.VMEM((points, channels), bf16),
            pltpu.VMEM((points, channels), f32),
            pltpu.VMEM((devices * LANES, channels), f32),
            pltpu.VMEM((points,), i32),
            pltpu.SMEM((points,), i32),
            pltpu.VMEM((devices, points), bf16),
            pltpu.VMEM((2 * LANES, points), bf16),
            pltpu.VMEM((devices, points), bf16),
            pltpu.VMEM((LANES, points), bf16),
            pltpu.VMEM((devices * LANES,), i32),
            pltpu.SMEM((devices * LANES,), i32),
            pltpu.VMEM((devices, BLOCK, channels), bf16),
            pltpu.SemaphoreType.DMA,
            pltpu.SemaphoreType.DMA,
            pltpu.SemaphoreType.DMA,
            pltpu.SemaphoreType.DMA((4,)),
        ],
        name="pack",
    )(
        point_count,
        point_cell.reshape(1, points),
        point_tile.reshape(1, points),
        point_feats,
    )


def add_up(got):
    devices, block, channels = got.shape
    bf16, f32, i32 = jnp.bfloat16, jnp.float32, jnp.int32
    heights = (CELLS, COLS_DEV + EDGE, COLS_DEV + EDGE) + (ROWS_DEV,) * 4
    return pl.pallas_call(
        add_kernel,
        out_shape=[jax.ShapeDtypeStruct((height, channels), bf16) for height in heights]
        + [jax.ShapeDtypeStruct((8, LANES), i32)],
        in_specs=[ANY],
        out_specs=[VMEM] * 8,
        scratch_shapes=[
            pltpu.VMEM((devices, block, channels), bf16),
            pltpu.VMEM((block, channels), f32),
            pltpu.VMEM((block, channels), f32),
            pltpu.VMEM((devices, 8, channels), bf16),
            pltpu.VMEM((devices * 8, channels), f32),
            pltpu.VMEM((devices * LANES,), i32),
            pltpu.SMEM((devices * LANES,), i32),
            pltpu.SemaphoreType.DMA,
            pltpu.SemaphoreType.DMA,
            pltpu.SemaphoreType.DMA((4,)),
        ]
        + [pltpu.VMEM((CELLS + HALO + 8, channels), f32)] * SUMS,
        name="add_up",
    )(got)


def shift(cells, axis, step):
    count = lax.axis_size(axis)
    pairs = [(i, i + step) for i in range(count) if 0 <= i + step < count]
    return lax.ppermute(cells, axis, pairs)


def conv(bev, up, down, west, east, weight, bias):
    cells, channels = bev.shape
    bf16, f32 = jnp.bfloat16, jnp.float32
    return pl.pallas_call(
        conv_kernel,
        out_shape=jax.ShapeDtypeStruct((cells, channels), bf16),
        in_specs=[VMEM] * 7,
        out_specs=VMEM,
        scratch_shapes=[
            pltpu.VMEM((4 * channels, 6 * channels), bf16),
            pltpu.VMEM((COLS_DEV + 8, 2 * channels), f32),
            pltpu.VMEM((COLS_DEV + 8, 2 * channels), f32),
            pltpu.VMEM((ROWS_DEV + 8, channels), f32),
        ],
        name="conv",
    )(bev, up, down, west, east, weight, bias)


def exchange_columns(top, bottom, left, right, west, east):
    west, east = shift(right, "gy", 1), shift(left, "gy", -1)
    rest = jnp.zeros((EDGE - 2, west.shape[1]), west.dtype)
    top = jnp.concatenate([top[:COLS_DEV], west[:1], east[:1], rest], axis=0)
    bottom = jnp.concatenate([bottom[:COLS_DEV], west[ROWS_DEV - 1 :], east[ROWS_DEV - 1 :], rest], axis=0)
    return top, bottom, west, east


def keep_columns(top, bottom, left, right, west, east):
    return top, bottom, west, east


def shards(point_feats, point_tile, point_cell, point_count, conv_weight, conv_bias):
    across = lax.axis_size("gy")
    devices = lax.axis_size("gx") * across
    channels = point_feats.shape[1]
    sent = pack(point_feats, point_tile, point_cell, point_count, devices, across)
    got = lax.all_to_all(sent, ("gx", "gy"), split_axis=0, concat_axis=0, tiled=True)
    bev, top, bottom, left, right, west, east, full = add_up(got)
    top, bottom, west, east = lax.cond(
        full[0, 0] > 0, exchange_columns, keep_columns, top, bottom, left, right, west, east
    )
    up = shift(bottom, "gx", 1)
    down = shift(top, "gx", -1)
    conv_out = conv(bev, up, down, west, east, conv_weight, conv_bias.reshape(1, channels))
    whole = (ROWS_DEV, COLS_DEV, channels)
    return (bev.reshape(whole), conv_out.reshape(whole))


def solution(mesh):
    in_specs = (
        P(("gx", "gy"), None),
        P(("gx", "gy"), None),
        P(("gx", "gy")),
        P(("gx", "gy")),
        P(),
        P(),
    )
    out_specs = (P("gx", "gy", None), P("gx", "gy", None))
    return jax.shard_map(shards, mesh=mesh, in_specs=in_specs, out_specs=out_specs, check_vma=False)
```

time: 99.7 us -> 98.9 us (level); the launches traced: 97.7 us -> 98.5 us
  starting transfers between devices: 8.4 us -> 5.84 us
  Pallas kernels: 31.2 us -> 33.6 us
  other arithmetic: 1.38 us -> 0 us
  local copies, waits for them, and re-layouts: 0.6 us -> 1.85 us
    ppermute x4 -> x2, starting transfers between devices: 8.4 us -> 5.84 us  [shift(): return lax.ppermute(cells, axis, pairs)]
    pallas_call x4 -> x3, Pallas kernels: 31.2 us -> 33.6 us  [the longest x1 15.2 us: pack(): pl.pallas_call(functools.partial(pack_kernel, across), out_shape=jax.Shap...]
    concatenate x2 -> x0, other arithmetic: 1.38 us -> none  [the longest x1 0.69 us: shards(): east = shift(jnp.concatenate([up[:1], left, down[:1]], axis=0), 'gy', -1)]
    slice x2 -> x1, local copies, waits for them, and re-layouts: 0.01 us -> 1.22 us  [shards(): full[0, 0] > 0]
    ppermute x4 -> x2, waiting for transfers between devices: 5.79 us -> 6.26 us  [shift(): return lax.ppermute(cells, axis, pairs)]
  transfers between devices with their start and end apart: 4 -> 2, of which waited for: 2 -> 2; matrix products, arithmetic and copies ran while one was open for 1% -> 0% of each run, Pallas kernels for 4% -> 0%
where the time goes in v5:
time: 98.9 us; the launch traced here: 98.5 us
  blocking collectives  49 us (50%)
  Pallas kernels  33.6 us (34%)
  waiting for transfers between devices  6.26 us (6%)
  starting transfers between devices  5.84 us (6%)
  between operations  1.96 us (2%)
  local copies, waits for them, and re-layouts  1.85 us (2%)
    all_to_all x1, blocking collectives, shards(): lax.all_to_all(sent, ('gx', 'gy'), split_axis=0, concat_axis=0, tiled=True)  49 us
    pallas_call x1, Pallas kernels, pack(): pl.pallas_call(functools.partial(pack_kernel, across), out_shape=jax.Shap...  15.2 us
    pallas_call x1, Pallas kernels, add_up(): pl.pallas_call(add_kernel, out_shape=[jax.ShapeDtypeStruct((height, chann...  14.1 us
    ppermute x2, waiting for transfers between devices, shift(): return lax.ppermute(cells, axis, pairs)  6.26 us
    ppermute x2, starting transfers between devices, shift(): return lax.ppermute(cells, axis, pairs)  5.84 us
    pallas_call x1, Pallas kernels, conv(): pl.pallas_call(conv_kernel, out_shape=jax.ShapeDtypeStruct((cells, channe...  4.32 us
  transfers between devices with their start and end apart: 2, of which 2 were waited for; matrix products, arithmetic and copies ran while one was open for 0% of the time, Pallas kernels for 0%

profile of v5, /device:TPU:6, one launch (start us, length us, event | category | flops | bytes accessed | tf_op | source)
XLA Modules:
  0.0 98.5 jit_solution(7700423189995350259)
XLA Ops:
  1.3 15.2 %pack.1 = bf16[128,88,128]{2,1,0:T(8,128)(2,1)} custom-call(s32[1]{0:T(128)S(6)} %copy.16.count_ref, s32[1,8192]{1,0:T(1,128)} %bitcast.8, s32[1,8192]{1,0:T(1,128)} %bitcast.9, bf16[8192,128]{1,0:T(8,128)(2,1)} %feats_hbm.1), custom_call_target="tpu_custom_call" | custom-call | tf_op jit(solution)/shard_map/pack/pallas_call | solution.py:304
  16.5 49.0 %all_to_all.5.got_hbm = bf16[128,88,128]{2,1,0:T(8,128)(2,1)} all-to-all(bf16[128,88,128]{2,1,0:T(8,128)(2,1)} %pack.1), channel_id=1, replica_groups=mesh['gx'=16,'gy'=8] {'gx','gy'}, dimensions={0} | all-to-all | bytes 5767168 | tf_op jit(solution)/shard_map/all_to_all | solution.py:404
  65.4 14.1 %add_up.1 = (bf16[4096,128]{1,0:T(8,128)(2,1)}, bf16[272,128]{1,0:T(8,128)(2,1)S(1)}, bf16[272,128]{1,0:T(8,128)(2,1)S(1)}, bf16[16,128]{1,0:T(8,128)(2,1)S(1)},...) custom-call(bf16[128,88,128]{2,1,0:T(8,128)(2,1)} %all_to_all.5.got_hbm), custom_call_target="tpu_custom_call" | custom-call | tf_op jit(solution)/shard_map/add_up/pallas_call | solution.py:340
  79.5 1.2 %slice.21 = s32[1,1]{1,0:T(1,128)} slice(s32[8,128]{1,0:T(8,128)} %get-tuple-element.35), slice={[0:1], [0:1]} | slice | bytes 8 | tf_op jit(solution)/shard_map/slice | solution.py:407
  81.4 3.8 %collective-permute-start.2 = (bf16[272,128]{1,0:T(8,128)(2,1)S(1)}, bf16[272,128]{1,0:T(8,128)(2,1)S(1)}, u32[]{:S(2)}, u32[]{:S(2)}) collective-permute-start(bf16[272,128]{1,0:T(8,128)(2,1)S(1)} %get-tuple-element.42), channel_id=1, source_target_pairs={{0,8},{8,16},{16,24},{24,32},{32,40},{40,48},{48,56},{56,64},{64,7... | collective-permute-start | bytes 208904 | tf_op jit(solution)/shard_map/ppermute | solution.py:366
  85.2 2.0 %collective-permute-start.3 = (bf16[272,128]{1,0:T(8,128)(2,1)S(1)}, bf16[272,128]{1,0:T(8,128)(2,1)S(1)}, u32[]{:S(2)}, u32[]{:S(2)}) collective-permute-start(bf16[272,128]{1,0:T(8,128)(2,1)S(1)} %get-tuple-element.43), channel_id=1, source_target_pairs={{8,0},{16,8},{24,16},{32,24},{40,32},{48,40},{56,48},{64,56},{72,6... | collective-permute-start | bytes 208904 | tf_op jit(solution)/shard_map/ppermute | solution.py:366
  87.2 0.3 collective-permute-done.2.up_ref
  87.6 0.0 copy-start
  87.6 5.9 %collective-permute-done.3.down_ref = bf16[272,128]{1,0:T(8,128)(2,1)S(1)} collective-permute-done((bf16[272,128]{1,0:T(8,128)(2,1)S(1)}, bf16[272,128]{1,0:T(8,128)(2,1)S(1)}, u32[]{:S(2)}, u32[]{:S(2)}) %collective-permute-start.3) | collective-permute-done | bytes 69664 | tf_op jit(solution)/shard_map/ppermute | solution.py:366
  93.5 0.0 copy-start.1
  93.5 0.0 copy-done
  93.5 0.6 copy-done.1
  94.1 4.3 %conv.1 = bf16[4096,128]{1,0:T(8,128)(2,1)} custom-call(bf16[4096,128]{1,0:T(8,128)(2,1)} %get-tuple-element.34.bev_ref, bf16[272,128]{1,0:T(8,128)(2,1)} %copy-done, bf16[272,128]{1,0:T(8,128)(2,1)} %copy-done.1, bf16[16,128]{1,0:T(8,128)(2,1)} %get-tuple-element.44.west_ref, bf16[16,128]{1,0:T(8,128)(2,1)} %get-tuple-element.45.east_ref, ...), custom_call_target="tpu_custom_call" | custom-call | tf_op jit(solution)/shard_map/conv/pallas_call | solution.py:372
  (1 shorter events, 0.0 us)
Async XLA Ops:
  81.4 6.2 %collective-permute-start.2 = (bf16[272,128]{1,0:T(8,128)(2,1)S(1)}, bf16[272,128]{1,0:T(8,128)(2,1)S(1)}, u32[]{:S(2)}, u32[]{:S(2)}) collective-permute-start(bf16[272,128]{1,0:T(8,128)(2,1)S(1)} %get-tuple-element.42), channel_id=1, source_target_pairs={{0,8},{8,16},{16,24},{24,32},{32,40},{40,48},{48,56},{56,64},{64,7... | collective-permute-start | bytes 208904 | tf_op jit(solution)/shard_map/ppermute | solution.py:366
  85.2 8.3 %collective-permute-start.3 = (bf16[272,128]{1,0:T(8,128)(2,1)S(1)}, bf16[272,128]{1,0:T(8,128)(2,1)S(1)}, u32[]{:S(2)}, u32[]{:S(2)}) collective-permute-start(bf16[272,128]{1,0:T(8,128)(2,1)S(1)} %get-tuple-element.43), channel_id=1, source_target_pairs={{8,0},{16,8},{24,16},{32,24},{40,32},{48,40},{56,48},{64,56},{72,6... | collective-permute-start | bytes 208904 | tf_op jit(solution)/shard_map/ppermute | solution.py:366
  87.6 5.9 %copy-start = (bf16[272,128]{1,0:T(8,128)(2,1)}, bf16[272,128]{1,0:T(8,128)(2,1)S(1)}, u32[]{:S(2)}) copy-start(bf16[272,128]{1,0:T(8,128)(2,1)S(1)} %collective-permute-done.2.up_ref) | copy-start | bytes 208900
  93.5 0.6 copy-start.1

commit v6 on v5

--- a/solution.py
+++ b/solution.py
@@ -19,7 +19,7 @@
 DUMP = CELLS + HALO
 EDGE = 16
 MOVES = 512
-TOGETHER = 4
+TOGETHER = 8
 
 
 def pack_kernel(
@@ -40,15 +40,21 @@
     column = lax.broadcasted_iota(jnp.int32, (width, width + LANES), 1)
     one, zero = jnp.ones((), jnp.bfloat16), jnp.zeros((), jnp.bfloat16)
     upto = jnp.where((source <= column) | (column >= width), 1.0, 0.0).astype(jnp.bfloat16)
-    first = (lax.broadcasted_iota(jnp.int32, (tiles, LANES), 0) * LANES - 1).astype(jnp.float32)
     tile_mark = tile_id.astype(jnp.float32).astype(jnp.bfloat16)
     spare_id = lax.broadcasted_iota(jnp.int32, (8, width), 0)
     nothing = jnp.zeros((8, width), jnp.float32)
-    twin_code[16:80, :] = jnp.zeros((64, points), jnp.bfloat16)
-    twin_code[96:, :] = jnp.zeros((32, points), jnp.bfloat16)
 
     def as_bf16(x):
         return x.astype(jnp.float32).astype(jnp.bfloat16)
+
+    def pick(mark, found, before):
+        place = found[:, :width].astype(jnp.bfloat16) + jnp.concatenate([before] * (width // LANES), axis=1)
+        place = jnp.where(mark, place, zero)
+        while place.shape[0] > 16:
+            half = place.shape[0] // 2
+            place = place[:half, :] + place[half:, :]
+        order = jnp.sum(place.astype(jnp.float32), axis=0, keepdims=True).astype(jnp.int32) - 1
+        return order, before + found[:, width:].astype(jnp.bfloat16)
 
     def rank(g, befores):
         before, twin_before = befores
@@ -58,7 +64,8 @@
             here = pl.ds(pl.multiple_of(i * width, width), width)
             live = i * width + lane < count
             tile = jnp.where(live, tile_ref[:, here], tiles)
-            mark = jnp.where(tile_mark == as_bf16(tile), one, zero)
+            match = tile_mark == as_bf16(tile)
+            mark = jnp.where(match, one, zero)
             hits[:, here] = mark
             marks.append(mark)
             cell = cell_ref[:, here]
@@ -67,50 +74,45 @@
             west = live & (along == 0) & (place > 0)
             east = live & (along == COLS_DEV - 1) & (place < across - 1)
             twin = jnp.where(west, tile - 1, jnp.where(east, tile + 1, tiles))
-            twin_mark = jnp.where(tile_mark == as_bf16(twin), one, zero)
+            twin_match = tile_mark == as_bf16(twin)
+            twin_mark = jnp.where(twin_match, one, zero)
             twins[:, here] = twin_mark
             twin_marks.append(twin_mark)
             code = jnp.where(west, ROWS_DEV, 0) + lax.shift_right_logical(cell, 8)
-            info.append((tile, live, here, i, cell, twin, code))
+            info.append((tile, live, here, i, cell, code, match, twin_match))
         found = jnp.dot(jnp.concatenate(marks, axis=0), upto, preferred_element_type=jnp.float32)
         twin_found = jnp.dot(jnp.concatenate(twin_marks, axis=0), upto, preferred_element_type=jnp.float32)
         for c in range(TOGETHER):
-            tile, live, here, i, cell, twin, code = info[c]
-            mine = found[c * tiles : (c + 1) * tiles, :]
-            place = mine[:, :width] + jnp.concatenate([before] * (width // LANES), axis=1)
-            slot = jnp.sum(jnp.where(tile_id == tile, place, 0.0), axis=0, keepdims=True).astype(jnp.int32)
-            pos_f[pl.ds(pl.multiple_of(i * width, width), width)] = jnp.where(live, slot, tiles * LANES - 1).reshape(width)
-            at_level = tile_mark == as_bf16(slot & (LANES - 1))
+            tile, live, here, i, cell, code, match, twin_match = info[c]
+            level, before = pick(match, found[c * tiles : (c + 1) * tiles, :], before)
+            slot = jnp.where(live, tile * LANES + level, tiles * LANES - 1)
+            pos_f[pl.ds(pl.multiple_of(i * width, width), width)] = slot.reshape(width)
+            at_level = tile_mark == as_bf16(level)
             coded[:LANES, here] = jnp.where(at_level, as_bf16(lax.shift_right_logical(cell, 6)), zero)
             coded[LANES:, here] = jnp.where(at_level, as_bf16(cell & 63), zero)
-            before = before + mine[:, width:]
-            theirs = twin_found[c * tiles : (c + 1) * tiles, :]
-            place = theirs[:, :width] + jnp.concatenate([twin_before] * (width // LANES), axis=1)
-            order = jnp.sum(jnp.where(tile_id == twin, place, 0.0), axis=0, keepdims=True).astype(jnp.int32) - 1
+            order, twin_before = pick(twin_match, twin_found[c * tiles : (c + 1) * tiles, :], twin_before)
             at_order = spare_id == order
             point = i * width + lane
             high = jnp.where(at_order, (point & -LANES).astype(jnp.float32), nothing)
             low = jnp.where(at_order, (point & (LANES - 1)).astype(jnp.float32), nothing)
             value = jnp.where(at_order, code.astype(jnp.float32), nothing)
             twin_code[:16, here] = jnp.concatenate([high, low], axis=0).astype(jnp.bfloat16)
-            twin_code[80:96, here] = jnp.concatenate([value, nothing], axis=0).astype(jnp.bfloat16)
-            twin_before = twin_before + theirs[:, width:]
+            twin_code[16:, here] = jnp.concatenate([value, nothing], axis=0).astype(jnp.bfloat16)
         return before, twin_before
 
-    before, twin_total = lax.fori_loop(
-        0, chunks // TOGETHER, rank, (first, jnp.zeros((tiles, LANES), jnp.float32))
-    )
-    total = before - first
+    start = jnp.zeros((tiles, LANES), jnp.bfloat16)
+    total, twin_total = lax.fori_loop(0, chunks // TOGETHER, rank, (start, start))
+    total, twin_total = total.astype(jnp.float32), twin_total.astype(jnp.float32)
     to_smem = pltpu.make_async_copy(pos_f, pos_s, sem)
     to_smem.start()
     across_lanes = (((1,), (1,)), ((), ()))
-    extra = lax.dot_general(twins[...], twin_code[...], across_lanes, preferred_element_type=jnp.float32)
-    origin = (extra + pltpu.roll(extra, LANES - 8, 1)).astype(jnp.int32)
-    spot = lax.broadcasted_iota(jnp.int32, (tiles, LANES), 1).astype(jnp.float32)
-    known = spot < jnp.minimum(twin_total, float(SPARE))
-    twin_f[...] = jnp.where(known, origin, 0).reshape(tiles * LANES)
+    extra = lax.dot_general(twin_code[...], twins[...], across_lanes, preferred_element_type=jnp.float32)
+    twin_f[...] = (extra[:8, :] + extra[8:16, :]).astype(jnp.int32).reshape(8 * tiles)
     twins_to_smem = pltpu.make_async_copy(twin_f, twin_s, twin_sem)
     twins_to_smem.start()
+    spot = lax.broadcasted_iota(jnp.int32, (tiles, LANES), 1).astype(jnp.float32)
+    blank = jnp.zeros((CAP, tiles), jnp.float32)
+    codes = jnp.concatenate([blank, extra[16:, :], jnp.zeros((LANES - CAP - 16, tiles), jnp.float32)], axis=0).T
     load.wait()
     rows[...] = feats[...].astype(jnp.float32)
     cells = lax.dot_general(hits[...], coded[...], across_lanes, preferred_element_type=jnp.float32)
@@ -128,14 +130,14 @@
     def move_twins(t, carry):
         for u in range(8):
             for j in range(SPARE):
-                point = twin_s.at[pl.ds(u * LANES + j, (tiles - 8) * LANES + 1)][t * (8 * LANES)]
+                point = twin_s.at[pl.ds(j * tiles + u, tiles - 7)][t * 8]
                 slots[pl.ds(t * (8 * LANES) + u * LANES + CAP + 2 + j, 1), :] = rows[pl.ds(point, 1), :]
         return carry
 
     lax.fori_loop(0, tiles // 8, move_twins, 0)
     high = jnp.where(spot < total, cells[:, :LANES], float(DUMP // 64))
     low = jnp.where(spot < total, cells[:, LANES:], float(DUMP % 64))
-    low = jnp.where((spot >= CAP) & (spot - CAP < jnp.minimum(twin_total, float(SPARE))), extra, low)
+    low = jnp.where((spot >= CAP) & (spot - CAP < jnp.minimum(twin_total, float(SPARE))), codes, low)
     full = jnp.max(twin_total, axis=0, keepdims=True) > SPARE
     high = jnp.where(spot == LANES - 1, 0.0, high)
     low = jnp.where(spot == LANES - 1, jnp.where(full, 1.0, 0.0), low)
@@ -159,7 +161,7 @@
 
 
 def add_kernel(
-    got_hbm, out_ref, top_ref, bottom_ref, left_ref, right_ref, west_ref, east_ref, full_ref,
+    got_hbm, out_ref, top_ref, bottom_ref, sides_ref, full_ref,
     got, even, odd, meta, coded, cells_f, cells_s, sem, meta_sem, in_sems, *sums,
 ):
     sources = got_hbm.shape[0]
@@ -177,7 +179,7 @@
     high = coded[pl.ds(0, sources, 8), :].astype(jnp.int32)
     low = coded[pl.ds(1, sources, 8), :].astype(jnp.int32)
     cells = high * 64 + low
-    full_ref[...] = jnp.broadcast_to(jnp.max(cells[:, LANES - 1 :], axis=0, keepdims=True), full_ref.shape)
+    full_ref[0] = jnp.max(cells[:, LANES - 1 :])
     cells_f[...] = cells.reshape(sources * LANES)
     to_smem = pltpu.make_async_copy(cells_f, cells_s, sem)
     to_smem.start()
@@ -232,11 +234,9 @@
             total = total + part[at, :]
         return total
 
-    left_ref[...] = column(0, COLS_DEV).astype(jnp.bfloat16)
-    right_ref[...] = column(COLS_DEV - 1, COLS_DEV).astype(jnp.bfloat16)
     west, east = column(CELLS, 1), column(CELLS + ROWS_DEV, 1)
-    west_ref[...] = west.astype(jnp.bfloat16)
-    east_ref[...] = east.astype(jnp.bfloat16)
+    sides_ref[:ROWS_DEV, :] = west.astype(jnp.bfloat16)
+    sides_ref[ROWS_DEV:, :] = east.astype(jnp.bfloat16)
     spot = lax.broadcasted_iota(jnp.int32, (EDGE, LANES), 0)
     for ref, r in ((top_ref, 0), (bottom_ref, ROWS_DEV - 1)):
         ref[:COLS_DEV, :] = out_ref[r * COLS_DEV : (r + 1) * COLS_DEV, :]
@@ -245,7 +245,7 @@
 
 
 def conv_kernel(
-    bev_ref, up_ref, down_ref, west_ref, east_ref, weight_ref, bias_ref,
+    bev_ref, up_ref, down_ref, sides_ref, weight_ref, bias_ref,
     out_ref, wide, before, after, side,
 ):
     for i in range(4):
@@ -258,17 +258,17 @@
     above = up_ref[COLS_DEV:, :].astype(jnp.float32)
     below = down_ref[COLS_DEV:, :].astype(jnp.float32)
 
-    def beside(ref, corner, start):
+    def beside(corner, start):
         side[:1, :] = above[corner : corner + 1, :]
-        side[1 : ROWS_DEV + 1, :] = ref[...].astype(jnp.float32)
+        side[1 : ROWS_DEV + 1, :] = sides_ref[corner * ROWS_DEV : (corner + 1) * ROWS_DEV, :].astype(jnp.float32)
         side[ROWS_DEV + 1 : ROWS_DEV + 2, :] = below[corner : corner + 1, :]
         four = jnp.concatenate([side[pl.ds(i, pairs, 2), :] for i in range(4)], axis=1)
         return jnp.dot(
             four.astype(jnp.bfloat16), wide[:, start : start + 2 * LANES], preferred_element_type=jnp.float32
         )
 
-    west = beside(west_ref, 0, 0)
-    east = beside(east_ref, 1, 4 * LANES)
+    west = beside(0, 0)
+    east = beside(1, 4 * LANES)
 
     def row(r):
         if r < 0:
@@ -315,9 +315,9 @@
             pltpu.VMEM((devices, points), bf16),
             pltpu.VMEM((2 * LANES, points), bf16),
             pltpu.VMEM((devices, points), bf16),
-            pltpu.VMEM((LANES, points), bf16),
-            pltpu.VMEM((devices * LANES,), i32),
-            pltpu.SMEM((devices * LANES,), i32),
+            pltpu.VMEM((32, points), bf16),
+            pltpu.VMEM((devices * 8,), i32),
+            pltpu.SMEM((devices * 8,), i32),
             pltpu.VMEM((devices, BLOCK, channels), bf16),
             pltpu.SemaphoreType.DMA,
             pltpu.SemaphoreType.DMA,
@@ -336,13 +336,13 @@
 def add_up(got):
     devices, block, channels = got.shape
     bf16, f32, i32 = jnp.bfloat16, jnp.float32, jnp.int32
-    heights = (CELLS, COLS_DEV + EDGE, COLS_DEV + EDGE) + (ROWS_DEV,) * 4
+    heights = (CELLS, COLS_DEV + EDGE, COLS_DEV + EDGE, HALO)
     return pl.pallas_call(
         add_kernel,
         out_shape=[jax.ShapeDtypeStruct((height, channels), bf16) for height in heights]
-        + [jax.ShapeDtypeStruct((8, LANES), i32)],
+        + [jax.ShapeDtypeStruct((1,), i32)],
         in_specs=[ANY],
-        out_specs=[VMEM] * 8,
+        out_specs=[VMEM] * 4 + [SMEM],
         scratch_shapes=[
             pltpu.VMEM((devices, block, channels), bf16),
             pltpu.VMEM((block, channels), f32),
@@ -366,13 +366,13 @@
     return lax.ppermute(cells, axis, pairs)
 
 
-def conv(bev, up, down, west, east, weight, bias):
+def conv(bev, up, down, sides, weight, bias):
     cells, channels = bev.shape
     bf16, f32 = jnp.bfloat16, jnp.float32
     return pl.pallas_call(
         conv_kernel,
         out_shape=jax.ShapeDtypeStruct((cells, channels), bf16),
-        in_specs=[VMEM] * 7,
+        in_specs=[VMEM] * 6,
         out_specs=VMEM,
         scratch_shapes=[
             pltpu.VMEM((4 * channels, 6 * channels), bf16),
@@ -381,19 +381,20 @@
             pltpu.VMEM((ROWS_DEV + 8, channels), f32),
         ],
         name="conv",
-    )(bev, up, down, west, east, weight, bias)
-
-
-def exchange_columns(top, bottom, left, right, west, east):
-    west, east = shift(right, "gy", 1), shift(left, "gy", -1)
+    )(bev, up, down, sides, weight, bias)
+
+
+def exchange_columns(bev, top, bottom, sides):
+    cells = bev.reshape(ROWS_DEV, COLS_DEV, -1)
+    west, east = shift(cells[:, -1], "gy", 1), shift(cells[:, 0], "gy", -1)
     rest = jnp.zeros((EDGE - 2, west.shape[1]), west.dtype)
     top = jnp.concatenate([top[:COLS_DEV], west[:1], east[:1], rest], axis=0)
     bottom = jnp.concatenate([bottom[:COLS_DEV], west[ROWS_DEV - 1 :], east[ROWS_DEV - 1 :], rest], axis=0)
-    return top, bottom, west, east
-
-
-def keep_columns(top, bottom, left, right, west, east):
-    return top, bottom, west, east
+    return top, bottom, jnp.concatenate([west, east], axis=0)
+
+
+def keep_columns(bev, top, bottom, sides):
+    return top, bottom, sides
 
 
 def shards(point_feats, point_tile, point_cell, point_count, conv_weight, conv_bias):
@@ -402,13 +403,11 @@
     channels = point_feats.shape[1]
     sent = pack(point_feats, point_tile, point_cell, point_count, devices, across)
     got = lax.all_to_all(sent, ("gx", "gy"), split_axis=0, concat_axis=0, tiled=True)
-    bev, top, bottom, left, right, west, east, full = add_up(got)
-    top, bottom, west, east = lax.cond(
-        full[0, 0] > 0, exchange_columns, keep_columns, top, bottom, left, right, west, east
-    )
+    bev, top, bottom, sides, full = add_up(got)
+    top, bottom, sides = lax.switch(full[0], (keep_columns, exchange_columns), bev, top, bottom, sides)
     up = shift(bottom, "gx", 1)
     down = shift(top, "gx", -1)
-    conv_out = conv(bev, up, down, west, east, conv_weight, conv_bias.reshape(1, channels))
+    conv_out = conv(bev, up, down, sides, conv_weight, conv_bias.reshape(1, channels))
     whole = (ROWS_DEV, COLS_DEV, channels)
     return (bev.reshape(whole), conv_out.reshape(whole))
 

time: 98.9 us -> 96.3 us (0.974)
  local copies, waits for them, and re-layouts: 1.85 us -> 0.64 us
  Pallas kernels: 33.6 us -> 32.4 us
    pallas_call x1, Pallas kernels: 15.2 us -> 13.8 us  [pack(): pl.pallas_call(functools.partial(pack_kernel, across), out_shape=jax.Shap...]
    slice x1 -> x0, local copies, waits for them, and re-layouts: 1.22 us -> none  [shards(): full[0, 0] > 0]
where the time goes in v6:
time: 96.3 us; the launch traced here: 96.2 us
  blocking collectives  49.4 us (51%)
  Pallas kernels  32.4 us (34%)
  waiting for transfers between devices  5.91 us (6%)
  starting transfers between devices  5.84 us (6%)
  between operations  1.98 us (2%)
    all_to_all x1, blocking collectives, shards(): lax.all_to_all(sent, ('gx', 'gy'), split_axis=0, concat_axis=0, tiled=True)  49.4 us
    pallas_call x1, Pallas kernels, add_up(): pl.pallas_call(add_kernel, out_shape=[jax.ShapeDtypeStruct((height, chann...  14.6 us
    pallas_call x1, Pallas kernels, pack(): pl.pallas_call(functools.partial(pack_kernel, across), out_shape=jax.Shap...  13.8 us
    ppermute x2, waiting for transfers between devices, shift(): return lax.ppermute(cells, axis, pairs)  5.91 us
    ppermute x2, starting transfers between devices, shift(): return lax.ppermute(cells, axis, pairs)  5.84 us
    pallas_call x1, Pallas kernels, conv(): pl.pallas_call(conv_kernel, out_shape=jax.ShapeDtypeStruct((cells, channe...  3.99 us
  transfers between devices with their start and end apart: 2, of which 2 were waited for; matrix products, arithmetic and copies ran while one was open for 0% of the time, Pallas kernels for 0%

profile of v6, /device:TPU:6, one launch (start us, length us, event | category | flops | bytes accessed | tf_op | source)
XLA Modules:
  0.0 96.2 jit_solution(12525447873383169615)
XLA Ops:
  1.3 13.8 %pack.1 = bf16[128,88,128]{2,1,0:T(8,128)(2,1)} custom-call(s32[1]{0:T(128)S(6)} %copy.21.count_ref, s32[1,8192]{1,0:T(1,128)} %bitcast.16, s32[1,8192]{1,0:T(1,128)} %bitcast.17, bf16[8192,128]{1,0:T(8,128)(2,1)} %feats_hbm.1), custom_call_target="tpu_custom_call" | custom-call | tf_op jit(solution)/shard_map/pack/pallas_call | solution.py:304
  15.1 49.4 %all_to_all.5.got_hbm = bf16[128,88,128]{2,1,0:T(8,128)(2,1)} all-to-all(bf16[128,88,128]{2,1,0:T(8,128)(2,1)} %pack.1), channel_id=1, replica_groups=mesh['gx'=16,'gy'=8] {'gx','gy'}, dimensions={0} | all-to-all | bytes 5767168 | tf_op jit(solution)/shard_map/all_to_all | solution.py:405
  64.5 14.6 %add_up.1 = (bf16[4096,128]{1,0:T(8,128)(2,1)S(1)}, bf16[272,128]{1,0:T(8,128)(2,1)S(1)}, bf16[272,128]{1,0:T(8,128)(2,1)S(1)}, bf16[32,128]{1,0:T(8,128)(2,1)S(1)}, s32[1]{0:T(128)}) custom-call(bf16[128,88,128]{2,1,0:T(8,128)(2,1)} %all_to_all.5.got_hbm), custom_call_target="tpu_custom_call" | custom-call | tf_op jit(solution)/shard_map/add_up/pallas_call | solution.py:340
  79.1 0.0 copy-start
  79.8 3.4 %collective-permute-start.2 = (bf16[272,128]{1,0:T(8,128)(2,1)S(1)}, bf16[272,128]{1,0:T(8,128)(2,1)S(1)}, u32[]{:S(2)}, u32[]{:S(2)}) collective-permute-start(bf16[272,128]{1,0:T(8,128)(2,1)S(1)} %get-tuple-element.30), channel_id=1, source_target_pairs={{0,8},{8,16},{16,24},{24,32},{32,40},{40,48},{48,56},{56,64},{64,7... | collective-permute-start | bytes 208904 | tf_op jit(solution)/shard_map/ppermute | solution.py:366
  83.2 2.4 %collective-permute-start.3 = (bf16[272,128]{1,0:T(8,128)(2,1)S(1)}, bf16[272,128]{1,0:T(8,128)(2,1)S(1)}, u32[]{:S(2)}, u32[]{:S(2)}) collective-permute-start(bf16[272,128]{1,0:T(8,128)(2,1)S(1)} %get-tuple-element.31), channel_id=1, source_target_pairs={{8,0},{16,8},{24,16},{32,24},{40,32},{48,40},{56,48},{64,56},{72,6... | collective-permute-start | bytes 208904 | tf_op jit(solution)/shard_map/ppermute | solution.py:366
  85.6 0.3 collective-permute-done.2.up_ref
  86.0 0.0 copy-start.1
  86.0 5.6 %collective-permute-done.3.down_ref = bf16[272,128]{1,0:T(8,128)(2,1)S(1)} collective-permute-done((bf16[272,128]{1,0:T(8,128)(2,1)S(1)}, bf16[272,128]{1,0:T(8,128)(2,1)S(1)}, u32[]{:S(2)}, u32[]{:S(2)}) %collective-permute-start.3) | collective-permute-done | bytes 69664 | tf_op jit(solution)/shard_map/ppermute | solution.py:366
  91.5 0.0 copy-start.2
  91.5 0.0 copy-done.1
  91.5 0.6 copy-done.2
  92.2 4.0 %conv.1 = bf16[4096,128]{1,0:T(8,128)(2,1)} custom-call(bf16[4096,128]{1,0:T(8,128)(2,1)S(1)} %get-tuple-element.25.bev_ref, bf16[272,128]{1,0:T(8,128)(2,1)} %copy-done.1, bf16[272,128]{1,0:T(8,128)(2,1)} %copy-done.2, bf16[32,128]{1,0:T(8,128)(2,1)S(1)} %get-tuple-element.32.sides_ref, bf16[3,3,128,128]{3,2,1,0:T(8,128)(2,1)} %weight_ref.1, f32[1,128]{1,0:T(1,128)} %bitcast.20), custom_call_target="tpu_custom_call" | custom-call | tf_op jit(solution)/shard_map/conv/pallas_call | solution.py:372
  96.2 0.0 copy-done
  (1 shorter events, 0.0 us)
Async XLA Ops:
  79.1 17.1 %copy-start = (bf16[4096,128]{1,0:T(8,128)(2,1)}, bf16[4096,128]{1,0:T(8,128)(2,1)S(1)}, u32[]{:S(2)}) copy-start(bf16[4096,128]{1,0:T(8,128)(2,1)S(1)} %get-tuple-element.25.bev_ref) | copy-start | bytes 3145732
  79.8 6.2 %collective-permute-start.2 = (bf16[272,128]{1,0:T(8,128)(2,1)S(1)}, bf16[272,128]{1,0:T(8,128)(2,1)S(1)}, u32[]{:S(2)}, u32[]{:S(2)}) collective-permute-start(bf16[272,128]{1,0:T(8,128)(2,1)S(1)} %get-tuple-element.30), channel_id=1, source_target_pairs={{0,8},{8,16},{16,24},{24,32},{32,40},{40,48},{48,56},{56,64},{64,7... | collective-permute-start | bytes 208904 | tf_op jit(solution)/shard_map/ppermute | solution.py:366
  83.2 8.3 %collective-permute-start.3 = (bf16[272,128]{1,0:T(8,128)(2,1)S(1)}, bf16[272,128]{1,0:T(8,128)(2,1)S(1)}, u32[]{:S(2)}, u32[]{:S(2)}) collective-permute-start(bf16[272,128]{1,0:T(8,128)(2,1)S(1)} %get-tuple-element.31), channel_id=1, source_target_pairs={{8,0},{16,8},{24,16},{32,24},{40,32},{48,40},{56,48},{64,56},{72,6... | collective-permute-start | bytes 208904 | tf_op jit(solution)/shard_map/ppermute | solution.py:366
  86.0 5.6 %copy-start.1 = (bf16[272,128]{1,0:T(8,128)(2,1)}, bf16[272,128]{1,0:T(8,128)(2,1)S(1)}, u32[]{:S(2)}) copy-start(bf16[272,128]{1,0:T(8,128)(2,1)S(1)} %collective-permute-done.2.up_ref) | copy-start | bytes 208900
  91.5 0.6 copy-start.2

commit v7 on v6

--- a/solution.py
+++ b/solution.py
@@ -87,9 +87,9 @@
             level, before = pick(match, found[c * tiles : (c + 1) * tiles, :], before)
             slot = jnp.where(live, tile * LANES + level, tiles * LANES - 1)
             pos_f[pl.ds(pl.multiple_of(i * width, width), width)] = slot.reshape(width)
-            at_level = tile_mark == as_bf16(level)
-            coded[:LANES, here] = jnp.where(at_level, as_bf16(lax.shift_right_logical(cell, 6)), zero)
-            coded[LANES:, here] = jnp.where(at_level, as_bf16(cell & 63), zero)
+            at_level = tile_mark[:CAP, :] == as_bf16(level)
+            coded[:CAP, here] = jnp.where(at_level, as_bf16(lax.shift_right_logical(cell, 6)), zero)
+            coded[CAP:, here] = jnp.where(at_level, as_bf16(cell & 63), zero)
             order, twin_before = pick(twin_match, twin_found[c * tiles : (c + 1) * tiles, :], twin_before)
             at_order = spare_id == order
             point = i * width + lane
@@ -115,7 +115,8 @@
     codes = jnp.concatenate([blank, extra[16:, :], jnp.zeros((LANES - CAP - 16, tiles), jnp.float32)], axis=0).T
     load.wait()
     rows[...] = feats[...].astype(jnp.float32)
-    cells = lax.dot_general(hits[...], coded[...], across_lanes, preferred_element_type=jnp.float32)
+    cells = lax.dot_general(coded[...], hits[...], across_lanes, preferred_element_type=jnp.float32)
+    filler = jnp.zeros((LANES - CAP, tiles), jnp.float32)
     to_smem.wait()
 
     def move(i, carry):
@@ -135,8 +136,8 @@
         return carry
 
     lax.fori_loop(0, tiles // 8, move_twins, 0)
-    high = jnp.where(spot < total, cells[:, :LANES], float(DUMP // 64))
-    low = jnp.where(spot < total, cells[:, LANES:], float(DUMP % 64))
+    high = jnp.where(spot < total, jnp.concatenate([cells[:CAP, :], filler], axis=0).T, float(DUMP // 64))
+    low = jnp.where(spot < total, jnp.concatenate([cells[CAP:, :], filler], axis=0).T, float(DUMP % 64))
     low = jnp.where((spot >= CAP) & (spot - CAP < jnp.minimum(twin_total, float(SPARE))), codes, low)
     full = jnp.max(twin_total, axis=0, keepdims=True) > SPARE
     high = jnp.where(spot == LANES - 1, 0.0, high)
@@ -244,31 +245,62 @@
         ref[COLS_DEV:, :] = corners.astype(jnp.bfloat16)
 
 
-def conv_kernel(
-    bev_ref, up_ref, down_ref, sides_ref, weight_ref, bias_ref,
-    out_ref, wide, before, after, side,
-):
+def fill_wide(weight_ref, wide):
     for i in range(4):
         for b in range(3):
             for o in range(2):
                 block = (slice(i * LANES, (i + 1) * LANES), slice((2 * b + o) * LANES, (2 * b + o + 1) * LANES))
                 wide[block] = weight_ref[i - o, b] if 0 <= i - o < 3 else jnp.zeros((LANES, LANES), jnp.bfloat16)
-    bias = bias_ref[...]
-    pairs = ROWS_DEV // 2
+
+
+def conv_rows(row, pairs, west, east, bias, out_ref, wide, before, after):
+    for k, p in enumerate(pairs):
+        four = jnp.concatenate([row(2 * p - 1 + i) for i in range(4)], axis=1)
+        taps = jnp.dot(four, wide[...], preferred_element_type=jnp.float32)
+        before[7:8, :] = west[k : k + 1, :]
+        before[8:, :] = taps[:, : 2 * LANES]
+        after[:COLS_DEV, :] = taps[:, 4 * LANES :]
+        after[COLS_DEV : COLS_DEV + 1, :] = east[k : k + 1, :]
+        total = taps[:, 2 * LANES : 4 * LANES] + before[7 : 7 + COLS_DEV, :] + after[1 : 1 + COLS_DEV, :]
+        done = jnp.maximum(total + jnp.concatenate([bias, bias], axis=1), 0.0).astype(jnp.bfloat16)
+        out_ref[2 * k * COLS_DEV : (2 * k + 1) * COLS_DEV, :] = done[:, :LANES]
+        out_ref[(2 * k + 1) * COLS_DEV : (2 * k + 2) * COLS_DEV, :] = done[:, LANES:]
+
+
+def beside(corner, start, above, below, sides_ref, wide, side):
+    side[:1, :] = above[corner : corner + 1, :]
+    side[1 : ROWS_DEV + 1, :] = sides_ref[corner * ROWS_DEV : (corner + 1) * ROWS_DEV, :].astype(jnp.float32)
+    side[ROWS_DEV + 1 : ROWS_DEV + 2, :] = below[corner : corner + 1, :]
+    four = jnp.concatenate([side[pl.ds(i, ROWS_DEV // 2, 2), :] for i in range(4)], axis=1)
+    return jnp.dot(four.astype(jnp.bfloat16), wide[:, start : start + 2 * LANES], preferred_element_type=jnp.float32)
+
+
+def inner_kernel(bev_ref, sides_ref, weight_ref, bias_ref, out_hbm, out, wide, before, after, side, sem):
+    fill_wide(weight_ref, wide)
+    nothing = jnp.zeros((EDGE, LANES), jnp.float32)
+    west = beside(0, 0, nothing, nothing, sides_ref, wide, side)
+    east = beside(1, 4 * LANES, nothing, nothing, sides_ref, wide, side)
+
+    def row(r):
+        return bev_ref[r * COLS_DEV : (r + 1) * COLS_DEV, :]
+
+    last = ROWS_DEV // 2 - 1
+    conv_rows(row, range(1, last), west[1:last, :], east[1:last, :], bias_ref[...], out, wide, before, after)
+    part = pl.ds(2 * COLS_DEV, (ROWS_DEV - 4) * COLS_DEV)
+    store = pltpu.make_async_copy(out, out_hbm.at[part], sem)
+    store.start()
+    store.wait()
+
+
+def outer_kernel(
+    conv_ref, bev_ref, up_ref, down_ref, sides_ref, weight_ref, bias_ref,
+    out_hbm, out, wide, before, after, side, sems,
+):
+    fill_wide(weight_ref, wide)
     above = up_ref[COLS_DEV:, :].astype(jnp.float32)
     below = down_ref[COLS_DEV:, :].astype(jnp.float32)
-
-    def beside(corner, start):
-        side[:1, :] = above[corner : corner + 1, :]
-        side[1 : ROWS_DEV + 1, :] = sides_ref[corner * ROWS_DEV : (corner + 1) * ROWS_DEV, :].astype(jnp.float32)
-        side[ROWS_DEV + 1 : ROWS_DEV + 2, :] = below[corner : corner + 1, :]
-        four = jnp.concatenate([side[pl.ds(i, pairs, 2), :] for i in range(4)], axis=1)
-        return jnp.dot(
-            four.astype(jnp.bfloat16), wide[:, start : start + 2 * LANES], preferred_element_type=jnp.float32
-        )
-
-    west = beside(0, 0)
-    east = beside(1, 4 * LANES)
+    west = beside(0, 0, above, below, sides_ref, wide, side)
+    east = beside(1, 4 * LANES, above, below, sides_ref, wide, side)
 
     def row(r):
         if r < 0:
@@ -277,18 +309,19 @@
             return down_ref[:COLS_DEV, :]
         return bev_ref[r * COLS_DEV : (r + 1) * COLS_DEV, :]
 
-    for p in range(pairs):
-        four = jnp.concatenate([row(2 * p - 1 + i) for i in range(4)], axis=1)
-        taps = jnp.dot(four, wide[...], preferred_element_type=jnp.float32)
-        before[7:8, :] = west[p : p + 1, :]
-        before[8:, :] = taps[:, : 2 * LANES]
-        after[:COLS_DEV, :] = taps[:, 4 * LANES :]
-        after[COLS_DEV : COLS_DEV + 1, :] = east[p : p + 1, :]
-        total = taps[:, 2 * LANES : 4 * LANES] + before[7 : 7 + COLS_DEV, :] + after[1 : 1 + COLS_DEV, :]
-        for o in range(2):
-            r = 2 * p + o
-            part = total[:, o * LANES : (o + 1) * LANES]
-            out_ref[r * COLS_DEV : (r + 1) * COLS_DEV, :] = jnp.maximum(part + bias, 0.0).astype(jnp.bfloat16)
+    last = ROWS_DEV // 2 - 1
+    ends = (0, last)
+    pick = [jnp.concatenate([x[:1, :], x[last:, :]], axis=0) for x in (west, east)]
+    conv_rows(row, ends, *pick, bias_ref[...], out, wide, before, after)
+    size = 2 * COLS_DEV
+    stores = [
+        pltpu.make_async_copy(out.at[pl.ds(k * size, size)], out_hbm.at[pl.ds(p * size, size)], sems.at[k])
+        for k, p in enumerate(ends)
+    ]
+    for store in stores:
+        store.start()
+    for store in stores:
+        store.wait()
 
 
 VMEM = pl.BlockSpec(memory_space=pltpu.VMEM)
@@ -313,7 +346,7 @@
             pltpu.VMEM((points,), i32),
             pltpu.SMEM((points,), i32),
             pltpu.VMEM((devices, points), bf16),
-            pltpu.VMEM((2 * LANES, points), bf16),
+            pltpu.VMEM((2 * CAP, points), bf16),
             pltpu.VMEM((devices, points), bf16),
             pltpu.VMEM((32, points), bf16),
             pltpu.VMEM((devices * 8,), i32),
@@ -366,22 +399,26 @@
     return lax.ppermute(cells, axis, pairs)
 
 
-def conv(bev, up, down, sides, weight, bias):
-    cells, channels = bev.shape
+def conv_call(kernel, name, ins, rows, sems, aliases, flops, *operands):
+    bev, channels = operands[-4 if len(ins) == 4 else 1], LANES
     bf16, f32 = jnp.bfloat16, jnp.float32
     return pl.pallas_call(
-        conv_kernel,
-        out_shape=jax.ShapeDtypeStruct((cells, channels), bf16),
-        in_specs=[VMEM] * 6,
-        out_specs=VMEM,
+        kernel,
+        out_shape=jax.ShapeDtypeStruct(bev.shape, bf16),
+        in_specs=ins,
+        out_specs=ANY,
+        input_output_aliases=aliases,
         scratch_shapes=[
+            pltpu.VMEM((rows * COLS_DEV, channels), bf16),
             pltpu.VMEM((4 * channels, 6 * channels), bf16),
             pltpu.VMEM((COLS_DEV + 8, 2 * channels), f32),
             pltpu.VMEM((COLS_DEV + 8, 2 * channels), f32),
             pltpu.VMEM((ROWS_DEV + 8, channels), f32),
+            sems,
         ],
-        name="conv",
-    )(bev, up, down, sides, weight, bias)
+        cost_estimate=pl.CostEstimate(flops=flops, bytes_accessed=2 * rows * COLS_DEV * channels, transcendentals=0),
+        name=name,
+    )(*operands)
 
 
 def exchange_columns(bev, top, bottom, sides):
@@ -407,7 +444,16 @@
     top, bottom, sides = lax.switch(full[0], (keep_columns, exchange_columns), bev, top, bottom, sides)
     up = shift(bottom, "gx", 1)
     down = shift(top, "gx", -1)
-    conv_out = conv(bev, up, down, sides, conv_weight, conv_bias.reshape(1, channels))
+    bias = conv_bias.reshape(1, channels)
+    dma = pltpu.SemaphoreType.DMA
+    work = 2 * CELLS * 9 * channels * channels
+    inner = conv_call(
+        inner_kernel, "inner", [VMEM] * 4, ROWS_DEV - 4, dma, {}, work, bev, sides, conv_weight, bias
+    )
+    conv_out = conv_call(
+        outer_kernel, "outer", [ANY] + [VMEM] * 6, 4, dma((2,)), {0: 0}, work // 4,
+        inner, bev, up, down, sides, conv_weight, bias,
+    )
     whole = (ROWS_DEV, COLS_DEV, channels)
     return (bev.reshape(whole), conv_out.reshape(whole))
 

time: 96.3 us -> 94.2 us (0.978)
  waiting for transfers between devices: 5.91 us -> 2.8 us
    ppermute x2, waiting for transfers between devices: 5.91 us -> 2.8 us  [shift(): return lax.ppermute(cells, axis, pairs)]
    pallas_call x1 -> x2, Pallas kernels: 3.99 us -> 5.91 us  [conv_call(): pl.pallas_call(kernel, out_shape=jax.ShapeDtypeStruct(bev.shape, bf16), i...]
    pallas_call x1, Pallas kernels: 14.6 us -> 13.5 us  [add_up(): pl.pallas_call(add_kernel, out_shape=[jax.ShapeDtypeStruct((height, chann...]
  transfers between devices with their start and end apart: 2 -> 2, of which waited for: 2 -> 1; matrix products, arithmetic and copies ran while one was open for 0% -> 0% of each run, Pallas kernels for 0% -> 4%
where the time goes in v7:
time: 94.2 us; the launch traced here: 93.2 us
  blocking collectives  49.4 us (52%)
  Pallas kernels  32.5 us (35%)
  starting transfers between devices  5.84 us (6%)
  waiting for transfers between devices  2.8 us (3%)
  between operations  2.01 us (2%)
    all_to_all x1, blocking collectives, shards(): lax.all_to_all(sent, ('gx', 'gy'), split_axis=0, concat_axis=0, tiled=True)  49.4 us
    pallas_call x1, Pallas kernels, add_up(): pl.pallas_call(add_kernel, out_shape=[jax.ShapeDtypeStruct((height, chann...  13.5 us
    pallas_call x1, Pallas kernels, pack(): pl.pallas_call(functools.partial(pack_kernel, across), out_shape=jax.Shap...  13.1 us
    pallas_call x2, Pallas kernels, conv_call(): pl.pallas_call(kernel, out_shape=jax.ShapeDtypeStruct(bev.shape, bf16), i...  5.91 us
    ppermute x2, starting transfers between devices, shift(): return lax.ppermute(cells, axis, pairs)  5.84 us
    ppermute x2, waiting for transfers between devices, shift(): return lax.ppermute(cells, axis, pairs)  2.8 us
  transfers between devices with their start and end apart: 2, of which 1 were waited for; matrix products, arithmetic and copies ran while one was open for 0% of the time, Pallas kernels for 4%

profile of v7, /device:TPU:6, one launch (start us, length us, event | category | flops | bytes accessed | tf_op | source)
XLA Modules:
  0.0 93.2 jit_solution(9990403979090780280)
XLA Ops:
  1.3 13.1 %pack.1 = bf16[128,88,128]{2,1,0:T(8,128)(2,1)} custom-call(s32[1]{0:T(128)S(6)} %copy.23.count_ref, s32[1,8192]{1,0:T(1,128)} %bitcast.16, s32[1,8192]{1,0:T(1,128)} %bitcast.17, bf16[8192,128]{1,0:T(8,128)(2,1)} %feats_hbm.1), custom_call_target="tpu_custom_call" | custom-call | tf_op jit(solution)/shard_map/pack/pallas_call | solution.py:337
  14.4 49.4 %all_to_all.5.got_hbm = bf16[128,88,128]{2,1,0:T(8,128)(2,1)} all-to-all(bf16[128,88,128]{2,1,0:T(8,128)(2,1)} %pack.1), channel_id=1, replica_groups=mesh['gx'=16,'gy'=8] {'gx','gy'}, dimensions={0} | all-to-all | bytes 5767168 | tf_op jit(solution)/shard_map/all_to_all | solution.py:442
  63.8 13.5 %add_up.1 = (bf16[4096,128]{1,0:T(8,128)(2,1)S(1)}, bf16[272,128]{1,0:T(8,128)(2,1)S(1)}, bf16[272,128]{1,0:T(8,128)(2,1)S(1)}, bf16[32,128]{1,0:T(8,128)(2,1)S(1)}, s32[1]{0:T(128)}) custom-call(bf16[128,88,128]{2,1,0:T(8,128)(2,1)} %all_to_all.5.got_hbm), custom_call_target="tpu_custom_call" | custom-call | tf_op jit(solution)/shard_map/add_up/pallas_call | solution.py:373
  77.3 0.0 copy-start
  78.0 3.8 %collective-permute-start.2 = (bf16[272,128]{1,0:T(8,128)(2,1)S(1)}, bf16[272,128]{1,0:T(8,128)(2,1)S(1)}, u32[]{:S(2)}, u32[]{:S(2)}) collective-permute-start(bf16[272,128]{1,0:T(8,128)(2,1)S(1)} %get-tuple-element.31), channel_id=1, source_target_pairs={{0,8},{8,16},{16,24},{24,32},{32,40},{40,48},{48,56},{56,64},{64,7... | collective-permute-start | bytes 208904 | tf_op jit(solution)/shard_map/ppermute | solution.py:399
  81.8 2.1 %collective-permute-start.3 = (bf16[272,128]{1,0:T(8,128)(2,1)S(1)}, bf16[272,128]{1,0:T(8,128)(2,1)S(1)}, u32[]{:S(2)}, u32[]{:S(2)}) collective-permute-start(bf16[272,128]{1,0:T(8,128)(2,1)S(1)} %get-tuple-element.32), channel_id=1, source_target_pairs={{8,0},{16,8},{24,16},{32,24},{40,32},{48,40},{56,48},{64,56},{72,6... | collective-permute-start | bytes 208904 | tf_op jit(solution)/shard_map/ppermute | solution.py:399
  83.8 3.4 %inner.1.conv_ref = bf16[4096,128]{1,0:T(8,128)(2,1)} custom-call(bf16[4096,128]{1,0:T(8,128)(2,1)S(1)} %get-tuple-element.25.bev_ref, bf16[32,128]{1,0:T(8,128)(2,1)S(1)} %get-tuple-element.30.sides_ref, bf16[3,3,128,128]{3,2,1,0:T(8,128)(2,1)} %weight_ref.3, f32[1,128]{1,0:T(1,128)} %bitcast.20), custom_call_target="tpu_custom_call" | custom-call | flops 1207959552 | bytes 786432 | tf_op jit(solution)/shard_map/inner/pallas_call | solution.py:405
  87.3 0.0 collective-permute-done.2.up_ref
  87.3 0.0 copy-start.1
  87.3 2.8 %collective-permute-done.3.down_ref = bf16[272,128]{1,0:T(8,128)(2,1)S(1)} collective-permute-done((bf16[272,128]{1,0:T(8,128)(2,1)S(1)}, bf16[272,128]{1,0:T(8,128)(2,1)S(1)}, u32[]{:S(2)}, u32[]{:S(2)}) %collective-permute-start.3) | collective-permute-done | bytes 69664 | tf_op jit(solution)/shard_map/ppermute | solution.py:399
  90.1 0.0 copy-done.1
  90.1 0.0 copy-start.2
  90.1 0.6 copy-done.2
  90.7 2.5 %outer.1 = bf16[4096,128]{1,0:T(8,128)(2,1)} custom-call(bf16[4096,128]{1,0:T(8,128)(2,1)} %inner.1.conv_ref, bf16[4096,128]{1,0:T(8,128)(2,1)S(1)} %get-tuple-element.25.bev_ref, bf16[272,128]{1,0:T(8,128)(2,1)} %copy-done.1, bf16[272,128]{1,0:T(8,128)(2,1)} %copy-done.2, ...), custom_call_target="tpu_custom_call", output_to_operand_aliasing={{}: (0, {})} | custom-call | flops 301989888 | bytes 262144 | tf_op jit(solution)/shard_map/outer/pallas_call | solution.py:405
  93.2 0.0 copy-done
  (1 shorter events, 0.0 us)
Async XLA Ops:
  77.3 15.9 %copy-start = (bf16[4096,128]{1,0:T(8,128)(2,1)}, bf16[4096,128]{1,0:T(8,128)(2,1)S(1)}, u32[]{:S(2)}) copy-start(bf16[4096,128]{1,0:T(8,128)(2,1)S(1)} %get-tuple-element.25.bev_ref) | copy-start | bytes 3145732
  78.0 9.3 %collective-permute-start.2 = (bf16[272,128]{1,0:T(8,128)(2,1)S(1)}, bf16[272,128]{1,0:T(8,128)(2,1)S(1)}, u32[]{:S(2)}, u32[]{:S(2)}) collective-permute-start(bf16[272,128]{1,0:T(8,128)(2,1)S(1)} %get-tuple-element.31), channel_id=1, source_target_pairs={{0,8},{8,16},{16,24},{24,32},{32,40},{40,48},{48,56},{56,64},{64,7... | collective-permute-start | bytes 208904 | tf_op jit(solution)/shard_map/ppermute | solution.py:399
  81.8 8.3 %collective-permute-start.3 = (bf16[272,128]{1,0:T(8,128)(2,1)S(1)}, bf16[272,128]{1,0:T(8,128)(2,1)S(1)}, u32[]{:S(2)}, u32[]{:S(2)}) collective-permute-start(bf16[272,128]{1,0:T(8,128)(2,1)S(1)} %get-tuple-element.32), channel_id=1, source_target_pairs={{8,0},{16,8},{24,16},{32,24},{40,32},{48,40},{56,48},{64,56},{72,6... | collective-permute-start | bytes 208904 | tf_op jit(solution)/shard_map/ppermute | solution.py:399
  87.3 2.8 %copy-start.1 = (bf16[272,128]{1,0:T(8,128)(2,1)}, bf16[272,128]{1,0:T(8,128)(2,1)S(1)}, u32[]{:S(2)}) copy-start(bf16[272,128]{1,0:T(8,128)(2,1)S(1)} %collective-permute-done.2.up_ref) | copy-start | bytes 208900
  90.1 0.6 copy-start.2

commit v8 on v7

--- a/solution.py
+++ b/solution.py
@@ -18,20 +18,22 @@
 HALO = 2 * ROWS_DEV
 DUMP = CELLS + HALO
 EDGE = 16
+PACK_VMEM = 60 * 2**20
+ADD_VMEM = 32 * 2**20
 MOVES = 512
 TOGETHER = 8
 
 
 def pack_kernel(
-    across, count_ref, cell_ref, tile_ref, feats_hbm, out_hbm,
-    feats, rows, slots, pos_f, pos_s, hits, coded, twins, twin_code, twin_f, twin_s, sent,
-    sem, twin_sem, in_sem, out_sems,
+    across, count_ref, cell_ref, tile_ref, feats_hbm, out_ref,
+    feats, rows, slots, pos_f, pos_s, hits, coded, twins, twin_code, twin_f, twin_s,
+    sem, twin_sem, in_sem,
 ):
     count = count_ref[0]
     width = 2 * LANES
     points = tile_ref.shape[1]
     chunks = points // width
-    tiles = out_hbm.shape[0]
+    tiles = out_ref.shape[0]
     load = pltpu.make_async_copy(feats_hbm, feats, in_sem)
     load.start()
     tile_id = lax.broadcasted_iota(jnp.int32, (tiles, width), 0)
@@ -146,37 +148,18 @@
     slots[pl.ds(CAP + 1, tiles, LANES), :] = low
 
     def narrow(t, carry):
-        sent[t] = slots[pl.ds(pl.multiple_of(t * LANES, LANES), BLOCK), :].astype(jnp.bfloat16)
-        return carry
-
-    parts = out_sems.shape[0]
-    share = tiles // parts
-    stores = []
-    for k in range(parts):
-        lax.fori_loop(k * share, (k + 1) * share, narrow, 0, unroll=4)
-        part = pl.ds(k * share, share)
-        stores.append(pltpu.make_async_copy(sent.at[part], out_hbm.at[part], out_sems.at[k]))
-        stores[-1].start()
-    for store in stores:
-        store.wait()
+        out_ref[t] = slots[pl.ds(pl.multiple_of(t * LANES, LANES), BLOCK), :].astype(jnp.bfloat16)
+        return carry
+
+    lax.fori_loop(0, tiles, narrow, 0, unroll=4)
 
 
 def add_kernel(
-    got_hbm, out_ref, top_ref, bottom_ref, sides_ref, full_ref,
-    got, even, odd, meta, coded, cells_f, cells_s, sem, meta_sem, in_sems, *sums,
+    got_ref, out_ref, top_ref, bottom_ref, sides_ref, full_ref,
+    even, odd, coded, cells_f, cells_s, sem, *sums,
 ):
-    sources = got_hbm.shape[0]
-    codes = pltpu.make_async_copy(got_hbm.at[:, pl.ds(CAP, 8), :], meta, meta_sem)
-    codes.start()
-    parts = in_sems.shape[0]
-    share = sources // parts
-    loads = []
-    for k in range(parts):
-        part = pl.ds(k * share, share)
-        loads.append(pltpu.make_async_copy(got_hbm.at[part], got.at[part], in_sems.at[k]))
-        loads[-1].start()
-    codes.wait()
-    coded[...] = meta[...].astype(jnp.float32).reshape(coded.shape)
+    sources = got_ref.shape[0]
+    coded[...] = got_ref[:, CAP:, :].astype(jnp.float32).reshape(coded.shape)
     high = coded[pl.ds(0, sources, 8), :].astype(jnp.int32)
     low = coded[pl.ds(1, sources, 8), :].astype(jnp.int32)
     cells = high * 64 + low
@@ -195,7 +178,7 @@
         part[pl.ds(CELLS, HALO + 8), :] = jnp.zeros((HALO + 8, LANES), jnp.float32)
 
     def widen(s, rows):
-        rows[...] = got[jnp.minimum(s, sources - 1)].astype(jnp.float32)
+        rows[...] = got_ref[jnp.minimum(s, sources - 1)].astype(jnp.float32)
 
     def add(s, rows):
         for j in range(CAP + SPARE):
@@ -212,8 +195,6 @@
         return carry
 
     to_smem.wait()
-    for load in loads:
-        load.wait()
     widen(0, even)
     lax.fori_loop(0, sources // 2, two, 0)
     step = 256
@@ -338,7 +319,7 @@
         functools.partial(pack_kernel, across),
         out_shape=jax.ShapeDtypeStruct((devices, BLOCK, channels), bf16),
         in_specs=[SMEM, VMEM, VMEM, ANY],
-        out_specs=ANY,
+        out_specs=VMEM,
         scratch_shapes=[
             pltpu.VMEM((points, channels), bf16),
             pltpu.VMEM((points, channels), f32),
@@ -351,12 +332,11 @@
             pltpu.VMEM((32, points), bf16),
             pltpu.VMEM((devices * 8,), i32),
             pltpu.SMEM((devices * 8,), i32),
-            pltpu.VMEM((devices, BLOCK, channels), bf16),
             pltpu.SemaphoreType.DMA,
             pltpu.SemaphoreType.DMA,
             pltpu.SemaphoreType.DMA,
-            pltpu.SemaphoreType.DMA((4,)),
         ],
+        compiler_params=pltpu.CompilerParams(vmem_limit_bytes=PACK_VMEM),
         name="pack",
     )(
         point_count,
@@ -374,19 +354,16 @@
         add_kernel,
         out_shape=[jax.ShapeDtypeStruct((height, channels), bf16) for height in heights]
         + [jax.ShapeDtypeStruct((1,), i32)],
-        in_specs=[ANY],
+        in_specs=[VMEM],
         out_specs=[VMEM] * 4 + [SMEM],
+        compiler_params=pltpu.CompilerParams(vmem_limit_bytes=ADD_VMEM),
         scratch_shapes=[
-            pltpu.VMEM((devices, block, channels), bf16),
             pltpu.VMEM((block, channels), f32),
             pltpu.VMEM((block, channels), f32),
-            pltpu.VMEM((devices, 8, channels), bf16),
             pltpu.VMEM((devices * 8, channels), f32),
             pltpu.VMEM((devices * LANES,), i32),
             pltpu.SMEM((devices * LANES,), i32),
             pltpu.SemaphoreType.DMA,
-            pltpu.SemaphoreType.DMA,
-            pltpu.SemaphoreType.DMA((4,)),
         ]
         + [pltpu.VMEM((CELLS + HALO + 8, channels), f32)] * SUMS,
         name="add_up",
@@ -416,6 +393,7 @@
             pltpu.VMEM((ROWS_DEV + 8, channels), f32),
             sems,
         ],
+        compiler_params=pltpu.CompilerParams(vmem_limit_bytes=16 * 2**20),
         cost_estimate=pl.CostEstimate(flops=flops, bytes_accessed=2 * rows * COLS_DEV * channels, transcendentals=0),
         name=name,
     )(*operands)

time: 94.2 us -> 90.2 us (0.958)
  Pallas kernels: 32.5 us -> 29.8 us
    pallas_call x2, Pallas kernels: 5.91 us -> 4.01 us  [conv_call(): pl.pallas_call(kernel, out_shape=jax.ShapeDtypeStruct(bev.shape, bf16), i...]
    pallas_call x1, Pallas kernels: 13.5 us -> 12.1 us  [add_up(): pl.pallas_call(add_kernel, out_shape=[jax.ShapeDtypeStruct((height, chann...]
  transfers between devices with their start and end apart: 2 -> 2, of which waited for: 1 -> 1; matrix products, arithmetic and copies ran while one was open for 0% -> 0% of each run, Pallas kernels for 4% -> 3%
where the time goes in v8:
time: 90.2 us; the launch traced here: 89.9 us
  blocking collectives  48.8 us (54%)
  Pallas kernels  29.8 us (33%)
  starting transfers between devices  5.84 us (6%)
  waiting for transfers between devices  3.44 us (4%)
  between operations  2.01 us (2%)
    all_to_all x1, blocking collectives, shards(): lax.all_to_all(sent, ('gx', 'gy'), split_axis=0, concat_axis=0, tiled=True)  48.8 us
    pallas_call x1, Pallas kernels, pack(): pl.pallas_call(functools.partial(pack_kernel, across), out_shape=jax.Shap...  13.7 us
    pallas_call x1, Pallas kernels, add_up(): pl.pallas_call(add_kernel, out_shape=[jax.ShapeDtypeStruct((height, chann...  12.1 us
    ppermute x2, starting transfers between devices, shift(): return lax.ppermute(cells, axis, pairs)  5.84 us
    pallas_call x2, Pallas kernels, conv_call(): pl.pallas_call(kernel, out_shape=jax.ShapeDtypeStruct(bev.shape, bf16), i...  4.01 us
    ppermute x2, waiting for transfers between devices, shift(): return lax.ppermute(cells, axis, pairs)  3.44 us
  transfers between devices with their start and end apart: 2, of which 1 were waited for; matrix products, arithmetic and copies ran while one was open for 0% of the time, Pallas kernels for 3%

profile of v8, /device:TPU:6, one launch (start us, length us, event | category | flops | bytes accessed | tf_op | source)
XLA Modules:
  0.0 89.9 jit_solution(4429572193108215340)
XLA Ops:
  1.3 13.7 %pack.1 = bf16[128,88,128]{2,1,0:T(8,128)(2,1)} custom-call(s32[1]{0:T(128)S(6)} %copy.23.count_ref, s32[1,8192]{1,0:T(1,128)} %bitcast.18, s32[1,8192]{1,0:T(1,128)} %bitcast.19, bf16[8192,128]{1,0:T(8,128)(2,1)} %feats_hbm.1), custom_call_target="tpu_custom_call" | custom-call | tf_op jit(solution)/shard_map/pack/pallas_call | solution.py:318
  14.9 48.8 %all_to_all.5.got_ref = bf16[128,88,128]{2,1,0:T(8,128)(2,1)S(1)} all-to-all(bf16[128,88,128]{2,1,0:T(8,128)(2,1)} %pack.1), channel_id=1, replica_groups=mesh['gx'=16,'gy'=8] {'gx','gy'}, dimensions={0} | all-to-all | bytes 5767168 | tf_op jit(solution)/shard_map/all_to_all | solution.py:420
  63.7 0.0 copy-start
  63.7 0.0 copy-start.1
  63.7 12.1 %add_up.1 = (bf16[4096,128]{1,0:T(8,128)(2,1)S(1)}, bf16[272,128]{1,0:T(8,128)(2,1)S(1)}, bf16[272,128]{1,0:T(8,128)(2,1)S(1)}, bf16[32,128]{1,0:T(8,128)(2,1)S(1)}, s32[1]{0:T(128)}) custom-call(bf16[128,88,128]{2,1,0:T(8,128)(2,1)S(1)} %all_to_all.5.got_ref), custom_call_target="tpu_custom_call" | custom-call | tf_op jit(solution)/shard_map/add_up/pallas_call | solution.py:353
  75.9 0.0 copy-start.2
  76.5 3.5 %collective-permute-start.2 = (bf16[272,128]{1,0:T(8,128)(2,1)S(1)}, bf16[272,128]{1,0:T(8,128)(2,1)S(1)}, u32[]{:S(2)}, u32[]{:S(2)}) collective-permute-start(bf16[272,128]{1,0:T(8,128)(2,1)S(1)} %get-tuple-element.31), channel_id=1, source_target_pairs={{0,8},{8,16},{16,24},{24,32},{32,40},{40,48},{48,56},{56,64},{64,7... | collective-permute-start | bytes 208904 | tf_op jit(solution)/shard_map/ppermute | solution.py:376
  80.1 2.3 %collective-permute-start.3 = (bf16[272,128]{1,0:T(8,128)(2,1)S(1)}, bf16[272,128]{1,0:T(8,128)(2,1)S(1)}, u32[]{:S(2)}, u32[]{:S(2)}) collective-permute-start(bf16[272,128]{1,0:T(8,128)(2,1)S(1)} %get-tuple-element.32), channel_id=1, source_target_pairs={{8,0},{16,8},{24,16},{32,24},{40,32},{48,40},{56,48},{64,56},{72,6... | collective-permute-start | bytes 208904 | tf_op jit(solution)/shard_map/ppermute | solution.py:376
  82.4 0.0 copy-done
  82.4 0.0 copy-done.1
  82.4 2.5 %inner.1.conv_ref = bf16[4096,128]{1,0:T(8,128)(2,1)} custom-call(bf16[4096,128]{1,0:T(8,128)(2,1)S(1)} %get-tuple-element.25.bev_ref, bf16[32,128]{1,0:T(8,128)(2,1)S(1)} %get-tuple-element.30.sides_ref, bf16[3,3,128,128]{3,2,1,0:T(8,128)(2,1)S(1)} %copy-done, f32[1,128]{1,0:T(1,128)S(1)} %bitcast.13), custom_call_target="tpu_custom_call" | custom-call | flops 1207959552 | bytes 786432 | tf_op jit(solution)/shard_map/inner/pallas_call | solution.py:382
  85.0 0.0 collective-permute-done.2.up_ref
  85.0 3.4 %collective-permute-done.3.down_ref = bf16[272,128]{1,0:T(8,128)(2,1)S(1)} collective-permute-done((bf16[272,128]{1,0:T(8,128)(2,1)S(1)}, bf16[272,128]{1,0:T(8,128)(2,1)S(1)}, u32[]{:S(2)}, u32[]{:S(2)}) %collective-permute-start.3) | collective-permute-done | bytes 69664 | tf_op jit(solution)/shard_map/ppermute | solution.py:376
  88.4 1.5 %outer.1 = bf16[4096,128]{1,0:T(8,128)(2,1)} custom-call(bf16[4096,128]{1,0:T(8,128)(2,1)} %inner.1.conv_ref, bf16[4096,128]{1,0:T(8,128)(2,1)S(1)} %get-tuple-element.25.bev_ref, bf16[272,128]{1,0:T(8,128)(2,1)S(1)} %collective-permute-done.2.up_ref, bf16[272,128]{1,0:T(8,128)(2,1)S(1)} %collective-permute-done.3.down_ref, ...), custom_call_target="tpu_custom_call", output_to_operand_aliasing={{}: (0, {})} | custom-call | flops 301989888 | bytes 262144 | tf_op jit(solution)/shard_map/outer/pallas_call | solution.py:382
  89.9 0.0 copy-done.2
  (1 shorter events, 0.0 us)
Async XLA Ops:
  63.7 18.7 %copy-start = (bf16[3,3,128,128]{3,2,1,0:T(8,128)(2,1)S(1)}, bf16[3,3,128,128]{3,2,1,0:T(8,128)(2,1)}, u32[]{:S(2)}) copy-start(bf16[3,3,128,128]{3,2,1,0:T(8,128)(2,1)} %weight_ref.3) | copy-start | bytes 884740
  63.7 18.7 %copy-start.1 = (f32[128]{0:T(128)S(1)}, f32[128]{0:T(128)}, u32[]{:S(2)}) copy-start(f32[128]{0:T(128)} %param.13) | copy-start | bytes 1540
  75.9 14.0 %copy-start.2 = (bf16[4096,128]{1,0:T(8,128)(2,1)}, bf16[4096,128]{1,0:T(8,128)(2,1)S(1)}, u32[]{:S(2)}) copy-start(bf16[4096,128]{1,0:T(8,128)(2,1)S(1)} %get-tuple-element.25.bev_ref) | copy-start | bytes 3145732
  76.5 8.4 %collective-permute-start.2 = (bf16[272,128]{1,0:T(8,128)(2,1)S(1)}, bf16[272,128]{1,0:T(8,128)(2,1)S(1)}, u32[]{:S(2)}, u32[]{:S(2)}) collective-permute-start(bf16[272,128]{1,0:T(8,128)(2,1)S(1)} %get-tuple-element.31), channel_id=1, source_target_pairs={{0,8},{8,16},{16,24},{24,32},{32,40},{40,48},{48,56},{56,64},{64,7... | collective-permute-start | bytes 208904 | tf_op jit(solution)/shard_map/ppermute | solution.py:376
  80.1 8.3 %collective-permute-start.3 = (bf16[272,128]{1,0:T(8,128)(2,1)S(1)}, bf16[272,128]{1,0:T(8,128)(2,1)S(1)}, u32[]{:S(2)}, u32[]{:S(2)}) collective-permute-start(bf16[272,128]{1,0:T(8,128)(2,1)S(1)} %get-tuple-element.32), channel_id=1, source_target_pairs={{8,0},{16,8},{24,16},{32,24},{40,32},{48,40},{56,48},{64,56},{72,6... | collective-permute-start | bytes 208904 | tf_op jit(solution)/shard_map/ppermute | solution.py:376

commit v9 on v8

--- a/solution.py
+++ b/solution.py
@@ -18,24 +18,22 @@
 HALO = 2 * ROWS_DEV
 DUMP = CELLS + HALO
 EDGE = 16
-PACK_VMEM = 60 * 2**20
+PACK_VMEM = 40 * 2**20
 ADD_VMEM = 32 * 2**20
 MOVES = 512
 TOGETHER = 8
 
 
 def pack_kernel(
-    across, count_ref, cell_ref, tile_ref, feats_hbm, out_ref,
-    feats, rows, slots, pos_f, pos_s, hits, coded, twins, twin_code, twin_f, twin_s,
-    sem, twin_sem, in_sem,
+    across, count_ref, cell_ref, tile_ref, feats_ref, out_ref,
+    rows, slots, pos_f, pos_s, hits, coded, twins, twin_code, twin_f, twin_s,
+    sem, twin_sem,
 ):
     count = count_ref[0]
     width = 2 * LANES
     points = tile_ref.shape[1]
     chunks = points // width
     tiles = out_ref.shape[0]
-    load = pltpu.make_async_copy(feats_hbm, feats, in_sem)
-    load.start()
     tile_id = lax.broadcasted_iota(jnp.int32, (tiles, width), 0)
     lane = lax.broadcasted_iota(jnp.int32, (1, width), 1)
     source = lax.broadcasted_iota(jnp.int32, (width, width + LANES), 0)
@@ -115,8 +113,7 @@
     spot = lax.broadcasted_iota(jnp.int32, (tiles, LANES), 1).astype(jnp.float32)
     blank = jnp.zeros((CAP, tiles), jnp.float32)
     codes = jnp.concatenate([blank, extra[16:, :], jnp.zeros((LANES - CAP - 16, tiles), jnp.float32)], axis=0).T
-    load.wait()
-    rows[...] = feats[...].astype(jnp.float32)
+    rows[...] = feats_ref[...].astype(jnp.float32)
     cells = lax.dot_general(coded[...], hits[...], across_lanes, preferred_element_type=jnp.float32)
     filler = jnp.zeros((LANES - CAP, tiles), jnp.float32)
     to_smem.wait()
@@ -318,10 +315,9 @@
     return pl.pallas_call(
         functools.partial(pack_kernel, across),
         out_shape=jax.ShapeDtypeStruct((devices, BLOCK, channels), bf16),
-        in_specs=[SMEM, VMEM, VMEM, ANY],
+        in_specs=[SMEM, VMEM, VMEM, VMEM],
         out_specs=VMEM,
         scratch_shapes=[
-            pltpu.VMEM((points, channels), bf16),
             pltpu.VMEM((points, channels), f32),
             pltpu.VMEM((devices * LANES, channels), f32),
             pltpu.VMEM((points,), i32),
@@ -332,7 +328,6 @@
             pltpu.VMEM((32, points), bf16),
             pltpu.VMEM((devices * 8,), i32),
             pltpu.SMEM((devices * 8,), i32),
-            pltpu.SemaphoreType.DMA,
             pltpu.SemaphoreType.DMA,
             pltpu.SemaphoreType.DMA,
         ],

time: 90.2 us -> 89.6 us (level)
  Pallas kernels: 29.8 us -> 25.7 us
  local copies, waits for them, and re-layouts: 0.01 us -> 3.11 us
    pallas_call x1, Pallas kernels: 13.7 us -> 9.89 us  [pack(): pl.pallas_call(functools.partial(pack_kernel, across), out_shape=jax.Shap...]
    unnamed x6 -> x12, local copies, waits for them, and re-layouts: 0.01 us -> 3.11 us
where the time goes in v9:
time: 89.6 us; the launch traced here: 89.2 us
  blocking collectives  48.6 us (54%)
  Pallas kernels  25.7 us (29%)
  starting transfers between devices  5.89 us (7%)
  waiting for transfers between devices  3.81 us (4%)
  local copies, waits for them, and re-layouts  3.11 us (3%)
  between operations  2.03 us (2%)
    all_to_all x1, blocking collectives, shards(): lax.all_to_all(sent, ('gx', 'gy'), split_axis=0, concat_axis=0, tiled=True)  48.6 us
    pallas_call x1, Pallas kernels, add_up(): pl.pallas_call(add_kernel, out_shape=[jax.ShapeDtypeStruct((height, chann...  11.8 us
    pallas_call x1, Pallas kernels, pack(): pl.pallas_call(functools.partial(pack_kernel, across), out_shape=jax.Shap...  9.89 us
    ppermute x2, starting transfers between devices, shift(): return lax.ppermute(cells, axis, pairs)  5.89 us
    pallas_call x2, Pallas kernels, conv_call(): pl.pallas_call(kernel, out_shape=jax.ShapeDtypeStruct(bev.shape, bf16), i...  4.01 us
    ppermute x2, waiting for transfers between devices, shift(): return lax.ppermute(cells, axis, pairs)  3.81 us
    unnamed x12, local copies, waits for them, and re-layouts  3.11 us
  transfers between devices with their start and end apart: 2, of which 1 were waited for; matrix products, arithmetic and copies ran while one was open for 0% of the time, Pallas kernels for 3%

profile of v9, /device:TPU:6, one launch (start us, length us, event | category | flops | bytes accessed | tf_op | source)
XLA Modules:
  0.0 89.2 jit_solution(1414064038517627763)
XLA Ops:
  1.3 0.0 copy-start
  1.3 1.6 %copy-done = bf16[8192,128]{1,0:T(8,128)(2,1)S(1)} copy-done((bf16[8192,128]{1,0:T(8,128)(2,1)S(1)}, bf16[8192,128]{1,0:T(8,128)(2,1)}, u32[]{:S(2)}) %copy-start) | copy-done | bytes 2097176
  2.9 0.0 copy-start.2
  2.9 0.8 copy-done.2
  3.6 0.0 copy-start.3
  3.6 0.8 copy-done.3
  4.4 9.9 %pack.1 = bf16[128,88,128]{2,1,0:T(8,128)(2,1)S(1)} custom-call(s32[1]{0:T(128)S(6)} %copy.23.count_ref, s32[1,8192]{1,0:T(1,128)S(1)} %bitcast.13, s32[1,8192]{1,0:T(1,128)S(1)} %bitcast.14, bf16[8192,128]{1,0:T(8,128)(2,1)S(1)} %copy-done), custom_call_target="tpu_custom_call" | custom-call | tf_op jit(solution)/shard_map/pack/pallas_call | solution.py:315
  14.3 48.6 %all_to_all.5.got_ref = bf16[128,88,128]{2,1,0:T(8,128)(2,1)S(1)} all-to-all(bf16[128,88,128]{2,1,0:T(8,128)(2,1)S(1)} %pack.1), channel_id=1, replica_groups=mesh['gx'=16,'gy'=8] {'gx','gy'}, dimensions={0} | all-to-all | bytes 5767168 | tf_op jit(solution)/shard_map/all_to_all | solution.py:415
  62.9 0.0 copy-start.1
  62.9 0.0 copy-start.4
  62.9 11.8 %add_up.1 = (bf16[4096,128]{1,0:T(8,128)(2,1)S(1)}, bf16[272,128]{1,0:T(8,128)(2,1)S(1)}, bf16[272,128]{1,0:T(8,128)(2,1)S(1)}, bf16[32,128]{1,0:T(8,128)(2,1)S(1)}, s32[1]{0:T(128)}) custom-call(bf16[128,88,128]{2,1,0:T(8,128)(2,1)S(1)} %all_to_all.5.got_ref), custom_call_target="tpu_custom_call" | custom-call | tf_op jit(solution)/shard_map/add_up/pallas_call | solution.py:348
  74.8 0.0 copy-start.5
  75.5 4.0 %collective-permute-start.2 = (bf16[272,128]{1,0:T(8,128)(2,1)S(1)}, bf16[272,128]{1,0:T(8,128)(2,1)S(1)}, u32[]{:S(2)}, u32[]{:S(2)}) collective-permute-start(bf16[272,128]{1,0:T(8,128)(2,1)S(1)} %get-tuple-element.31), channel_id=1, source_target_pairs={{0,8},{8,16},{16,24},{24,32},{32,40},{40,48},{48,56},{56,64},{64,7... | collective-permute-start | bytes 208904 | tf_op jit(solution)/shard_map/ppermute | solution.py:371
  79.4 1.9 %collective-permute-start.3 = (bf16[272,128]{1,0:T(8,128)(2,1)S(1)}, bf16[272,128]{1,0:T(8,128)(2,1)S(1)}, u32[]{:S(2)}, u32[]{:S(2)}) collective-permute-start(bf16[272,128]{1,0:T(8,128)(2,1)S(1)} %get-tuple-element.32), channel_id=1, source_target_pairs={{8,0},{16,8},{24,16},{32,24},{40,32},{48,40},{56,48},{64,56},{72,6... | collective-permute-start | bytes 208904 | tf_op jit(solution)/shard_map/ppermute | solution.py:371
  81.4 0.0 copy-done.1
  81.4 0.0 copy-done.4
  81.4 2.5 %inner.1.conv_ref = bf16[4096,128]{1,0:T(8,128)(2,1)} custom-call(bf16[4096,128]{1,0:T(8,128)(2,1)S(1)} %get-tuple-element.25.bev_ref, bf16[32,128]{1,0:T(8,128)(2,1)S(1)} %get-tuple-element.30.sides_ref, bf16[3,3,128,128]{3,2,1,0:T(8,128)(2,1)S(1)} %copy-done.1, f32[1,128]{1,0:T(1,128)S(1)} %bitcast.15), custom_call_target="tpu_custom_call" | custom-call | flops 1207959552 | bytes 786432 | tf_op jit(solution)/shard_map/inner/pallas_call | solution.py:377
  83.9 0.0 collective-permute-done.2.up_ref
  83.9 3.8 %collective-permute-done.3.down_ref = bf16[272,128]{1,0:T(8,128)(2,1)S(1)} collective-permute-done((bf16[272,128]{1,0:T(8,128)(2,1)S(1)}, bf16[272,128]{1,0:T(8,128)(2,1)S(1)}, u32[]{:S(2)}, u32[]{:S(2)}) %collective-permute-start.3) | collective-permute-done | bytes 69664 | tf_op jit(solution)/shard_map/ppermute | solution.py:371
  87.7 1.5 %outer.1 = bf16[4096,128]{1,0:T(8,128)(2,1)} custom-call(bf16[4096,128]{1,0:T(8,128)(2,1)} %inner.1.conv_ref, bf16[4096,128]{1,0:T(8,128)(2,1)S(1)} %get-tuple-element.25.bev_ref, bf16[272,128]{1,0:T(8,128)(2,1)S(1)} %collective-permute-done.2.up_ref, bf16[272,128]{1,0:T(8,128)(2,1)S(1)} %collective-permute-done.3.down_ref, ...), custom_call_target="tpu_custom_call", output_to_operand_aliasing={{}: (0, {})} | custom-call | flops 301989888 | bytes 262144 | tf_op jit(solution)/shard_map/outer/pallas_call | solution.py:377
  89.2 0.0 copy-done.5
  (1 shorter events, 0.0 us)
Async XLA Ops:
  1.3 1.6 %copy-start = (bf16[8192,128]{1,0:T(8,128)(2,1)S(1)}, bf16[8192,128]{1,0:T(8,128)(2,1)}, u32[]{:S(2)}) copy-start(bf16[8192,128]{1,0:T(8,128)(2,1)} %feats_ref.1) | copy-start | bytes 6291460
  2.9 0.8 copy-start.2
  3.6 0.8 copy-start.3
  62.9 18.4 %copy-start.1 = (bf16[3,3,128,128]{3,2,1,0:T(8,128)(2,1)S(1)}, bf16[3,3,128,128]{3,2,1,0:T(8,128)(2,1)}, u32[]{:S(2)}) copy-start(bf16[3,3,128,128]{3,2,1,0:T(8,128)(2,1)} %weight_ref.3) | copy-start | bytes 884740
  62.9 18.5 %copy-start.4 = (f32[128]{0:T(128)S(1)}, f32[128]{0:T(128)}, u32[]{:S(2)}) copy-start(f32[128]{0:T(128)} %param.13) | copy-start | bytes 1540
  74.8 14.4 %copy-start.5 = (bf16[4096,128]{1,0:T(8,128)(2,1)}, bf16[4096,128]{1,0:T(8,128)(2,1)S(1)}, u32[]{:S(2)}) copy-start(bf16[4096,128]{1,0:T(8,128)(2,1)S(1)} %get-tuple-element.25.bev_ref) | copy-start | bytes 3145732
  75.5 8.5 %collective-permute-start.2 = (bf16[272,128]{1,0:T(8,128)(2,1)S(1)}, bf16[272,128]{1,0:T(8,128)(2,1)S(1)}, u32[]{:S(2)}, u32[]{:S(2)}) collective-permute-start(bf16[272,128]{1,0:T(8,128)(2,1)S(1)} %get-tuple-element.31), channel_id=1, source_target_pairs={{0,8},{8,16},{16,24},{24,32},{32,40},{40,48},{48,56},{56,64},{64,7... | collective-permute-start | bytes 208904 | tf_op jit(solution)/shard_map/ppermute | solution.py:371
  79.4 8.3 %collective-permute-start.3 = (bf16[272,128]{1,0:T(8,128)(2,1)S(1)}, bf16[272,128]{1,0:T(8,128)(2,1)S(1)}, u32[]{:S(2)}, u32[]{:S(2)}) collective-permute-start(bf16[272,128]{1,0:T(8,128)(2,1)S(1)} %get-tuple-element.32), channel_id=1, source_target_pairs={{8,0},{16,8},{24,16},{32,24},{40,32},{48,40},{56,48},{64,56},{72,6... | collective-permute-start | bytes 208904 | tf_op jit(solution)/shard_map/ppermute | solution.py:371

commit v10 on v9

--- a/solution.py
+++ b/solution.py
@@ -21,19 +21,17 @@
 PACK_VMEM = 40 * 2**20
 ADD_VMEM = 32 * 2**20
 MOVES = 512
-TOGETHER = 8
-
-
-def pack_kernel(
-    across, count_ref, cell_ref, tile_ref, feats_ref, out_ref,
-    rows, slots, pos_f, pos_s, hits, coded, twins, twin_code, twin_f, twin_s,
-    sem, twin_sem,
+TOGETHER = 16
+
+
+def place_kernel(
+    across, count_ref, cell_ref, tile_ref, pos_f, twin_f, high_ref, low_ref, hits, coded, twins, twin_code,
 ):
     count = count_ref[0]
     width = 2 * LANES
     points = tile_ref.shape[1]
     chunks = points // width
-    tiles = out_ref.shape[0]
+    tiles = high_ref.shape[0]
     tile_id = lax.broadcasted_iota(jnp.int32, (tiles, width), 0)
     lane = lax.broadcasted_iota(jnp.int32, (1, width), 1)
     source = lax.broadcasted_iota(jnp.int32, (width, width + LANES), 0)
@@ -103,46 +101,56 @@
     start = jnp.zeros((tiles, LANES), jnp.bfloat16)
     total, twin_total = lax.fori_loop(0, chunks // TOGETHER, rank, (start, start))
     total, twin_total = total.astype(jnp.float32), twin_total.astype(jnp.float32)
-    to_smem = pltpu.make_async_copy(pos_f, pos_s, sem)
-    to_smem.start()
     across_lanes = (((1,), (1,)), ((), ()))
     extra = lax.dot_general(twin_code[...], twins[...], across_lanes, preferred_element_type=jnp.float32)
     twin_f[...] = (extra[:8, :] + extra[8:16, :]).astype(jnp.int32).reshape(8 * tiles)
-    twins_to_smem = pltpu.make_async_copy(twin_f, twin_s, twin_sem)
-    twins_to_smem.start()
     spot = lax.broadcasted_iota(jnp.int32, (tiles, LANES), 1).astype(jnp.float32)
     blank = jnp.zeros((CAP, tiles), jnp.float32)
     codes = jnp.concatenate([blank, extra[16:, :], jnp.zeros((LANES - CAP - 16, tiles), jnp.float32)], axis=0).T
-    rows[...] = feats_ref[...].astype(jnp.float32)
     cells = lax.dot_general(coded[...], hits[...], across_lanes, preferred_element_type=jnp.float32)
     filler = jnp.zeros((LANES - CAP, tiles), jnp.float32)
-    to_smem.wait()
-
-    def move(i, carry):
-        for k in range(MOVES):
-            slot = pos_s.at[pl.ds(k, points - MOVES + 1)][i * MOVES]
-            slots[pl.ds(slot, 1), :] = rows[pl.ds(i * MOVES + k, 1), :]
-        return carry
-
-    lax.fori_loop(0, (count + (MOVES - 1)) // MOVES, move, 0)
-    twins_to_smem.wait()
-
-    def move_twins(t, carry):
-        for u in range(8):
-            for j in range(SPARE):
-                point = twin_s.at[pl.ds(j * tiles + u, tiles - 7)][t * 8]
-                slots[pl.ds(t * (8 * LANES) + u * LANES + CAP + 2 + j, 1), :] = rows[pl.ds(point, 1), :]
-        return carry
-
-    lax.fori_loop(0, tiles // 8, move_twins, 0)
     high = jnp.where(spot < total, jnp.concatenate([cells[:CAP, :], filler], axis=0).T, float(DUMP // 64))
     low = jnp.where(spot < total, jnp.concatenate([cells[CAP:, :], filler], axis=0).T, float(DUMP % 64))
     low = jnp.where((spot >= CAP) & (spot - CAP < jnp.minimum(twin_total, float(SPARE))), codes, low)
     full = jnp.max(twin_total, axis=0, keepdims=True) > SPARE
     high = jnp.where(spot == LANES - 1, 0.0, high)
     low = jnp.where(spot == LANES - 1, jnp.where(full, 1.0, 0.0), low)
-    slots[pl.ds(CAP, tiles, LANES), :] = high
-    slots[pl.ds(CAP + 1, tiles, LANES), :] = low
+    high_ref[...] = high
+    low_ref[...] = low
+
+
+def pack_kernel(
+    count_ref, pos_f, twin_f, high_ref, low_ref, feats_ref, out_ref, rows, slots, pos_s, twin_s, sem, twin_sem
+):
+    count = count_ref[0]
+    points = feats_ref.shape[0]
+    tiles = out_ref.shape[0]
+    to_smem = pltpu.make_async_copy(pos_f, pos_s, sem)
+    to_smem.start()
+    twins_to_smem = pltpu.make_async_copy(twin_f, twin_s, twin_sem)
+    twins_to_smem.start()
+    rows[...] = feats_ref[...].astype(jnp.float32)
+    to_smem.wait()
+
+    def move(i, carry):
+        for k in range(MOVES):
+            slot = pos_s.at[pl.ds(k, points - MOVES + 1)][i * MOVES]
+            slots[pl.ds(slot, 1), :] = rows[pl.ds(i * MOVES + k, 1), :]
+        return carry
+
+    lax.fori_loop(0, (count + (MOVES - 1)) // MOVES, move, 0)
+    twins_to_smem.wait()
+
+    def move_twins(t, carry):
+        for u in range(8):
+            for j in range(SPARE):
+                point = twin_s.at[pl.ds(j * tiles + u, tiles - 7)][t * 8]
+                slots[pl.ds(t * (8 * LANES) + u * LANES + CAP + 2 + j, 1), :] = rows[pl.ds(point, 1), :]
+        return carry
+
+    lax.fori_loop(0, tiles // 8, move_twins, 0)
+    slots[pl.ds(CAP, tiles, LANES), :] = high_ref[...]
+    slots[pl.ds(CAP + 1, tiles, LANES), :] = low_ref[...]
 
     def narrow(t, carry):
         out_ref[t] = slots[pl.ds(pl.multiple_of(t * LANES, LANES), BLOCK), :].astype(jnp.bfloat16)
@@ -312,33 +320,43 @@
     if across & (across - 1):
         raise ValueError("across")
     bf16, f32, i32 = jnp.bfloat16, jnp.float32, jnp.int32
+    params = pltpu.CompilerParams(vmem_limit_bytes=PACK_VMEM)
+    placed = pl.pallas_call(
+        functools.partial(place_kernel, across),
+        out_shape=[
+            jax.ShapeDtypeStruct((points,), i32),
+            jax.ShapeDtypeStruct((devices * 8,), i32),
+            jax.ShapeDtypeStruct((devices, LANES), f32),
+            jax.ShapeDtypeStruct((devices, LANES), f32),
+        ],
+        in_specs=[SMEM, VMEM, VMEM],
+        out_specs=[VMEM] * 4,
+        scratch_shapes=[
+            pltpu.VMEM((devices, points), bf16),
+            pltpu.VMEM((2 * CAP, points), bf16),
+            pltpu.VMEM((devices, points), bf16),
+            pltpu.VMEM((32, points), bf16),
+        ],
+        compiler_params=params,
+        cost_estimate=pl.CostEstimate(flops=2 * points * devices * 1024, bytes_accessed=8 * points, transcendentals=0),
+        name="place",
+    )(point_count, point_cell.reshape(1, points), point_tile.reshape(1, points))
     return pl.pallas_call(
-        functools.partial(pack_kernel, across),
+        pack_kernel,
         out_shape=jax.ShapeDtypeStruct((devices, BLOCK, channels), bf16),
-        in_specs=[SMEM, VMEM, VMEM, VMEM],
+        in_specs=[SMEM] + [VMEM] * 5,
         out_specs=VMEM,
         scratch_shapes=[
             pltpu.VMEM((points, channels), f32),
             pltpu.VMEM((devices * LANES, channels), f32),
-            pltpu.VMEM((points,), i32),
             pltpu.SMEM((points,), i32),
-            pltpu.VMEM((devices, points), bf16),
-            pltpu.VMEM((2 * CAP, points), bf16),
-            pltpu.VMEM((devices, points), bf16),
-            pltpu.VMEM((32, points), bf16),
-            pltpu.VMEM((devices * 8,), i32),
             pltpu.SMEM((devices * 8,), i32),
             pltpu.SemaphoreType.DMA,
             pltpu.SemaphoreType.DMA,
         ],
-        compiler_params=pltpu.CompilerParams(vmem_limit_bytes=PACK_VMEM),
+        compiler_params=params,
         name="pack",
-    )(
-        point_count,
-        point_cell.reshape(1, points),
-        point_tile.reshape(1, points),
-        point_feats,
-    )
+    )(point_count, *placed, point_feats)
 
 
 def add_up(got):

time: 89.6 us -> 88.7 us (0.990)
  local copies, waits for them, and re-layouts: 3.11 us -> 1.53 us
  Pallas kernels: 25.7 us -> 26.8 us
    unnamed x12, local copies, waits for them, and re-layouts: 3.11 us -> 1.53 us
    pallas_call x1 -> x2, Pallas kernels: 9.89 us -> 10.9 us  [the longest x1 6.48 us: pack(): pl.pallas_call(pack_kernel, out_shape=jax.ShapeDtypeStruct((devices, BLOC...]
where the time goes in v10:
time: 88.7 us; the launch traced here: 88 us
  blocking collectives  48.1 us (54%)
  Pallas kernels  26.8 us (30%)
  starting transfers between devices  5.84 us (7%)
  waiting for transfers between devices  3.69 us (4%)
  between operations  2.04 us (2%)
  local copies, waits for them, and re-layouts  1.53 us (2%)
    all_to_all x1, blocking collectives, shards(): lax.all_to_all(sent, ('gx', 'gy'), split_axis=0, concat_axis=0, tiled=True)  48.1 us
    pallas_call x1, Pallas kernels, add_up(): pl.pallas_call(add_kernel, out_shape=[jax.ShapeDtypeStruct((height, chann...  11.8 us
    pallas_call x1, Pallas kernels, pack(): pl.pallas_call(pack_kernel, out_shape=jax.ShapeDtypeStruct((devices, BLOC...  6.48 us
    ppermute x2, starting transfers between devices, shift(): return lax.ppermute(cells, axis, pairs)  5.84 us
    pallas_call x1, Pallas kernels, pack(): pl.pallas_call(functools.partial(place_kernel, across), out_shape=[jax.Sh...  4.45 us
    pallas_call x2, Pallas kernels, conv_call(): pl.pallas_call(kernel, out_shape=jax.ShapeDtypeStruct(bev.shape, bf16), i...  4 us
    ppermute x2, waiting for transfers between devices, shift(): return lax.ppermute(cells, axis, pairs)  3.69 us
  transfers between devices with their start and end apart: 2, of which 1 were waited for; matrix products, arithmetic and copies ran while one was open for 0% of the time, Pallas kernels for 3%

profile of v10, /device:TPU:6, one launch (start us, length us, event | category | flops | bytes accessed | tf_op | source)
XLA Modules:
  0.0 88.0 jit_solution(7682092033534750570)
XLA Ops:
  1.3 0.0 copy-start.3
  1.3 0.7 copy-done.3
  2.0 0.0 copy-start.4
  2.0 0.8 copy-done.4
  2.8 0.0 copy-start
  2.8 4.5 %place.1 = (s32[8192]{0:T(1024)S(1)}, s32[1024]{0:T(1024)S(1)}, f32[128,128]{1,0:T(8,128)S(1)}, f32[128,128]{1,0:T(8,128)S(1)}) custom-call(s32[1]{0:T(128)S(6)} %copy.23.count_ref, s32[1,8192]{1,0:T(1,128)S(1)} %bitcast.15, s32[1,8192]{1,0:T(1,128)S(1)} %bitcast.16), custom_call_target="tpu_custom_call" | custom-call | flops 2147483648 | bytes 65536 | tf_op jit(solution)/shard_map/place/pallas_call | solution.py:324
  7.3 0.0 copy-done
  7.3 6.5 %pack.1 = bf16[128,88,128]{2,1,0:T(8,128)(2,1)S(1)} custom-call(s32[1]{0:T(128)S(6)} %copy.23.count_ref, s32[8192]{0:T(1024)S(1)} %get-tuple-element.29.pos_f, s32[1024]{0:T(1024)S(1)} %get-tuple-element.30.twin_f, f32[128,128]{1,0:T(8,128)S(1)} %get-tuple-element.31.high_ref, f32[128,128]{1,0:T(8,128)S(1)} %get-tuple-element.32.low_ref, ...), custom_call_target="tpu_custom_call" | custom-call | tf_op jit(solution)/shard_map/pack/pallas_call | solution.py:344
  13.8 48.1 %all_to_all.5.got_ref = bf16[128,88,128]{2,1,0:T(8,128)(2,1)S(1)} all-to-all(bf16[128,88,128]{2,1,0:T(8,128)(2,1)S(1)} %pack.1), channel_id=1, replica_groups=mesh['gx'=16,'gy'=8] {'gx','gy'}, dimensions={0} | all-to-all | bytes 5767168 | tf_op jit(solution)/shard_map/all_to_all | solution.py:433
  61.9 0.0 copy-start.1
  61.9 0.0 copy-start.2
  61.9 11.8 %add_up.1 = (bf16[4096,128]{1,0:T(8,128)(2,1)S(1)}, bf16[272,128]{1,0:T(8,128)(2,1)S(1)}, bf16[272,128]{1,0:T(8,128)(2,1)S(1)}, bf16[32,128]{1,0:T(8,128)(2,1)S(1)}, s32[1]{0:T(128)}) custom-call(bf16[128,88,128]{2,1,0:T(8,128)(2,1)S(1)} %all_to_all.5.got_ref), custom_call_target="tpu_custom_call" | custom-call | tf_op jit(solution)/shard_map/add_up/pallas_call | solution.py:366
  73.7 0.0 copy-start.5
  74.4 3.8 %collective-permute-start.2 = (bf16[272,128]{1,0:T(8,128)(2,1)S(1)}, bf16[272,128]{1,0:T(8,128)(2,1)S(1)}, u32[]{:S(2)}, u32[]{:S(2)}) collective-permute-start(bf16[272,128]{1,0:T(8,128)(2,1)S(1)} %get-tuple-element.39), channel_id=1, source_target_pairs={{0,8},{8,16},{16,24},{24,32},{32,40},{40,48},{48,56},{56,64},{64,7... | collective-permute-start | bytes 208904 | tf_op jit(solution)/shard_map/ppermute | solution.py:389
  78.2 2.0 %collective-permute-start.3 = (bf16[272,128]{1,0:T(8,128)(2,1)S(1)}, bf16[272,128]{1,0:T(8,128)(2,1)S(1)}, u32[]{:S(2)}, u32[]{:S(2)}) collective-permute-start(bf16[272,128]{1,0:T(8,128)(2,1)S(1)} %get-tuple-element.40), channel_id=1, source_target_pairs={{8,0},{16,8},{24,16},{32,24},{40,32},{48,40},{56,48},{64,56},{72,6... | collective-permute-start | bytes 208904 | tf_op jit(solution)/shard_map/ppermute | solution.py:389
  80.2 0.0 copy-done.1
  80.3 0.0 copy-done.2
  80.3 2.5 %inner.1.conv_ref = bf16[4096,128]{1,0:T(8,128)(2,1)} custom-call(bf16[4096,128]{1,0:T(8,128)(2,1)S(1)} %get-tuple-element.33.bev_ref, bf16[32,128]{1,0:T(8,128)(2,1)S(1)} %get-tuple-element.38.sides_ref, bf16[3,3,128,128]{3,2,1,0:T(8,128)(2,1)S(1)} %copy-done.1, f32[1,128]{1,0:T(1,128)S(1)} %bitcast.13), custom_call_target="tpu_custom_call" | custom-call | flops 1207959552 | bytes 786432 | tf_op jit(solution)/shard_map/inner/pallas_call | solution.py:395
  82.8 0.0 collective-permute-done.2.up_ref
  82.8 3.7 %collective-permute-done.3.down_ref = bf16[272,128]{1,0:T(8,128)(2,1)S(1)} collective-permute-done((bf16[272,128]{1,0:T(8,128)(2,1)S(1)}, bf16[272,128]{1,0:T(8,128)(2,1)S(1)}, u32[]{:S(2)}, u32[]{:S(2)}) %collective-permute-start.3) | collective-permute-done | bytes 69664 | tf_op jit(solution)/shard_map/ppermute | solution.py:389
  86.5 1.5 %outer.1 = bf16[4096,128]{1,0:T(8,128)(2,1)} custom-call(bf16[4096,128]{1,0:T(8,128)(2,1)} %inner.1.conv_ref, bf16[4096,128]{1,0:T(8,128)(2,1)S(1)} %get-tuple-element.33.bev_ref, bf16[272,128]{1,0:T(8,128)(2,1)S(1)} %collective-permute-done.2.up_ref, bf16[272,128]{1,0:T(8,128)(2,1)S(1)} %collective-permute-done.3.down_ref, ...), custom_call_target="tpu_custom_call", output_to_operand_aliasing={{}: (0, {})} | custom-call | flops 301989888 | bytes 262144 | tf_op jit(solution)/shard_map/outer/pallas_call | solution.py:395
  88.0 0.0 copy-done.5
  (1 shorter events, 0.0 us)
Async XLA Ops:
  1.3 0.8 copy-start.3
  2.0 0.8 copy-start.4
  2.8 4.5 %copy-start = (bf16[8192,128]{1,0:T(8,128)(2,1)S(1)}, bf16[8192,128]{1,0:T(8,128)(2,1)}, u32[]{:S(2)}) copy-start(bf16[8192,128]{1,0:T(8,128)(2,1)} %feats_ref.1) | copy-start | bytes 6291460
  61.9 18.4 %copy-start.1 = (bf16[3,3,128,128]{3,2,1,0:T(8,128)(2,1)S(1)}, bf16[3,3,128,128]{3,2,1,0:T(8,128)(2,1)}, u32[]{:S(2)}) copy-start(bf16[3,3,128,128]{3,2,1,0:T(8,128)(2,1)} %weight_ref.3) | copy-start | bytes 884740
  61.9 18.4 %copy-start.2 = (f32[128]{0:T(128)S(1)}, f32[128]{0:T(128)}, u32[]{:S(2)}) copy-start(f32[128]{0:T(128)} %param.13) | copy-start | bytes 1540
  73.7 14.3 %copy-start.5 = (bf16[4096,128]{1,0:T(8,128)(2,1)}, bf16[4096,128]{1,0:T(8,128)(2,1)S(1)}, u32[]{:S(2)}) copy-start(bf16[4096,128]{1,0:T(8,128)(2,1)S(1)} %get-tuple-element.33.bev_ref) | copy-start | bytes 3145732
  74.4 8.4 %collective-permute-start.2 = (bf16[272,128]{1,0:T(8,128)(2,1)S(1)}, bf16[272,128]{1,0:T(8,128)(2,1)S(1)}, u32[]{:S(2)}, u32[]{:S(2)}) collective-permute-start(bf16[272,128]{1,0:T(8,128)(2,1)S(1)} %get-tuple-element.39), channel_id=1, source_target_pairs={{0,8},{8,16},{16,24},{24,32},{32,40},{40,48},{48,56},{56,64},{64,7... | collective-permute-start | bytes 208904 | tf_op jit(solution)/shard_map/ppermute | solution.py:389
  78.2 8.3 %collective-permute-start.3 = (bf16[272,128]{1,0:T(8,128)(2,1)S(1)}, bf16[272,128]{1,0:T(8,128)(2,1)S(1)}, u32[]{:S(2)}, u32[]{:S(2)}) collective-permute-start(bf16[272,128]{1,0:T(8,128)(2,1)S(1)} %get-tuple-element.40), channel_id=1, source_target_pairs={{8,0},{16,8},{24,16},{32,24},{40,32},{48,40},{56,48},{64,56},{72,6... | collective-permute-start | bytes 208904 | tf_op jit(solution)/shard_map/ppermute | solution.py:389

commit v11 on v10

--- a/solution.py
+++ b/solution.py
@@ -261,7 +261,7 @@
     return jnp.dot(four.astype(jnp.bfloat16), wide[:, start : start + 2 * LANES], preferred_element_type=jnp.float32)
 
 
-def inner_kernel(bev_ref, sides_ref, weight_ref, bias_ref, out_hbm, out, wide, before, after, side, sem):
+def inner_kernel(bev_ref, sides_ref, weight_ref, bias_ref, out_hbm, wide, out, before, after, side, sem):
     fill_wide(weight_ref, wide)
     nothing = jnp.zeros((EDGE, LANES), jnp.float32)
     west = beside(0, 0, nothing, nothing, sides_ref, wide, side)
@@ -279,10 +279,9 @@
 
 
 def outer_kernel(
-    conv_ref, bev_ref, up_ref, down_ref, sides_ref, weight_ref, bias_ref,
-    out_hbm, out, wide, before, after, side, sems,
+    conv_ref, bev_ref, up_ref, down_ref, sides_ref, wide, bias_ref,
+    out_hbm, out, before, after, side, sems,
 ):
-    fill_wide(weight_ref, wide)
     above = up_ref[COLS_DEV:, :].astype(jnp.float32)
     below = down_ref[COLS_DEV:, :].astype(jnp.float32)
     west = beside(0, 0, above, below, sides_ref, wide, side)
@@ -389,18 +388,17 @@
     return lax.ppermute(cells, axis, pairs)
 
 
-def conv_call(kernel, name, ins, rows, sems, aliases, flops, *operands):
+def conv_call(kernel, name, ins, rows, sems, aliases, flops, extra, *operands):
     bev, channels = operands[-4 if len(ins) == 4 else 1], LANES
     bf16, f32 = jnp.bfloat16, jnp.float32
     return pl.pallas_call(
         kernel,
-        out_shape=jax.ShapeDtypeStruct(bev.shape, bf16),
+        out_shape=[jax.ShapeDtypeStruct(bev.shape, bf16)] + extra,
         in_specs=ins,
-        out_specs=ANY,
+        out_specs=[ANY] + [VMEM] * len(extra),
         input_output_aliases=aliases,
         scratch_shapes=[
             pltpu.VMEM((rows * COLS_DEV, channels), bf16),
-            pltpu.VMEM((4 * channels, 6 * channels), bf16),
             pltpu.VMEM((COLS_DEV + 8, 2 * channels), f32),
             pltpu.VMEM((COLS_DEV + 8, 2 * channels), f32),
             pltpu.VMEM((ROWS_DEV + 8, channels), f32),
@@ -438,12 +436,13 @@
     bias = conv_bias.reshape(1, channels)
     dma = pltpu.SemaphoreType.DMA
     work = 2 * CELLS * 9 * channels * channels
-    inner = conv_call(
-        inner_kernel, "inner", [VMEM] * 4, ROWS_DEV - 4, dma, {}, work, bev, sides, conv_weight, bias
+    inner, wide = conv_call(
+        inner_kernel, "inner", [VMEM] * 4, ROWS_DEV - 4, dma, {}, work,
+        [jax.ShapeDtypeStruct((4 * channels, 6 * channels), jnp.bfloat16)], bev, sides, conv_weight, bias
     )
-    conv_out = conv_call(
-        outer_kernel, "outer", [ANY] + [VMEM] * 6, 4, dma((2,)), {0: 0}, work // 4,
-        inner, bev, up, down, sides, conv_weight, bias,
+    (conv_out,) = conv_call(
+        outer_kernel, "outer", [ANY] + [VMEM] * 6, 4, dma((2,)), {0: 0}, work // 4, [],
+        inner, bev, up, down, sides, wide, bias,
     )
     whole = (ROWS_DEV, COLS_DEV, channels)
     return (bev.reshape(whole), conv_out.reshape(whole))

time: 88.7 us -> 88.7 us (level)
    pallas_call x1, Pallas kernels: 11.8 us -> 12.9 us  [add_up(): pl.pallas_call(add_kernel, out_shape=[jax.ShapeDtypeStruct((height, chann...]
where the time goes in v11:
time: 88.7 us
  blocking collectives  48.9 us (55%)
  Pallas kernels  27 us (30%)
  starting transfers between devices  5.84 us (7%)
  waiting for transfers between devices  3.36 us (4%)
  between operations  2.04 us (2%)
  local copies, waits for them, and re-layouts  1.53 us (2%)
    all_to_all x1, blocking collectives, shards(): lax.all_to_all(sent, ('gx', 'gy'), split_axis=0, concat_axis=0, tiled=True)  48.9 us
    pallas_call x1, Pallas kernels, add_up(): pl.pallas_call(add_kernel, out_shape=[jax.ShapeDtypeStruct((height, chann...  12.9 us
    ppermute x2, starting transfers between devices, shift(): return lax.ppermute(cells, axis, pairs)  5.84 us
    pallas_call x1, Pallas kernels, pack(): pl.pallas_call(pack_kernel, out_shape=jax.ShapeDtypeStruct((devices, BLOC...  5.66 us
    pallas_call x1, Pallas kernels, pack(): pl.pallas_call(functools.partial(place_kernel, across), out_shape=[jax.Sh...  4.45 us
    pallas_call x2, Pallas kernels, conv_call(): pl.pallas_call(kernel, out_shape=[jax.ShapeDtypeStruct(bev.shape, bf16)]...  4.02 us
    ppermute x2, waiting for transfers between devices, shift(): return lax.ppermute(cells, axis, pairs)  3.36 us
  transfers between devices with their start and end apart: 2, of which 1 were waited for; matrix products, arithmetic and copies ran while one was open for 0% of the time, Pallas kernels for 3%

profile of v11, /device:TPU:6, one launch (start us, length us, event | category | flops | bytes accessed | tf_op | source)
XLA Modules:
  0.0 88.7 jit_solution(10027207409472862012)
XLA Ops:
  1.3 0.0 copy-start.3
  1.3 0.7 copy-done.3
  2.0 0.0 copy-start.4
  2.0 0.8 copy-done.4
  2.8 0.0 copy-start
  2.8 4.5 %place.1 = (s32[8192]{0:T(1024)S(1)}, s32[1024]{0:T(1024)S(1)}, f32[128,128]{1,0:T(8,128)S(1)}, f32[128,128]{1,0:T(8,128)S(1)}) custom-call(s32[1]{0:T(128)S(6)} %copy.23.count_ref, s32[1,8192]{1,0:T(1,128)S(1)} %bitcast.15, s32[1,8192]{1,0:T(1,128)S(1)} %bitcast.16), custom_call_target="tpu_custom_call" | custom-call | flops 2147483648 | bytes 65536 | tf_op jit(solution)/shard_map/place/pallas_call | solution.py:323
  7.3 0.0 copy-done
  7.3 5.7 %pack.1 = bf16[128,88,128]{2,1,0:T(8,128)(2,1)S(1)} custom-call(s32[1]{0:T(128)S(6)} %copy.23.count_ref, s32[8192]{0:T(1024)S(1)} %get-tuple-element.31.pos_f, s32[1024]{0:T(1024)S(1)} %get-tuple-element.32.twin_f, f32[128,128]{1,0:T(8,128)S(1)} %get-tuple-element.33.high_ref, f32[128,128]{1,0:T(8,128)S(1)} %get-tuple-element.34.low_ref, ...), custom_call_target="tpu_custom_call" | custom-call | tf_op jit(solution)/shard_map/pack/pallas_call | solution.py:343
  12.9 48.9 %all_to_all.5.got_ref = bf16[128,88,128]{2,1,0:T(8,128)(2,1)S(1)} all-to-all(bf16[128,88,128]{2,1,0:T(8,128)(2,1)S(1)} %pack.1), channel_id=1, replica_groups=mesh['gx'=16,'gy'=8] {'gx','gy'}, dimensions={0} | all-to-all | bytes 5767168 | tf_op jit(solution)/shard_map/all_to_all | solution.py:431
  61.9 0.0 copy-start.1
  61.9 0.0 copy-start.2
  61.9 12.9 %add_up.1 = (bf16[4096,128]{1,0:T(8,128)(2,1)S(1)}, bf16[272,128]{1,0:T(8,128)(2,1)S(1)}, bf16[272,128]{1,0:T(8,128)(2,1)S(1)}, bf16[32,128]{1,0:T(8,128)(2,1)S(1)}, s32[1]{0:T(128)}) custom-call(bf16[128,88,128]{2,1,0:T(8,128)(2,1)S(1)} %all_to_all.5.got_ref), custom_call_target="tpu_custom_call" | custom-call | tf_op jit(solution)/shard_map/add_up/pallas_call | solution.py:365
  74.8 0.0 copy-start.5
  75.5 3.5 %collective-permute-start.2 = (bf16[272,128]{1,0:T(8,128)(2,1)S(1)}, bf16[272,128]{1,0:T(8,128)(2,1)S(1)}, u32[]{:S(2)}, u32[]{:S(2)}) collective-permute-start(bf16[272,128]{1,0:T(8,128)(2,1)S(1)} %get-tuple-element.42), channel_id=1, source_target_pairs={{0,8},{8,16},{16,24},{24,32},{32,40},{40,48},{48,56},{56,64},{64,7... | collective-permute-start | bytes 208904 | tf_op jit(solution)/shard_map/ppermute | solution.py:388
  79.0 2.3 %collective-permute-start.3 = (bf16[272,128]{1,0:T(8,128)(2,1)S(1)}, bf16[272,128]{1,0:T(8,128)(2,1)S(1)}, u32[]{:S(2)}, u32[]{:S(2)}) collective-permute-start(bf16[272,128]{1,0:T(8,128)(2,1)S(1)} %get-tuple-element.43), channel_id=1, source_target_pairs={{8,0},{16,8},{24,16},{32,24},{40,32},{48,40},{56,48},{64,56},{72,6... | collective-permute-start | bytes 208904 | tf_op jit(solution)/shard_map/ppermute | solution.py:388
  81.3 0.0 copy-done.1
  81.3 0.0 copy-done.2
  81.3 2.6 %inner.1 = (bf16[4096,128]{1,0:T(8,128)(2,1)}, bf16[512,768]{1,0:T(8,128)(2,1)S(1)}) custom-call(bf16[4096,128]{1,0:T(8,128)(2,1)S(1)} %get-tuple-element.35.bev_ref, bf16[32,128]{1,0:T(8,128)(2,1)S(1)} %get-tuple-element.40.sides_ref, bf16[3,3,128,128]{3,2,1,0:T(8,128)(2,1)S(1)} %copy-done.2, f32[1,128]{1,0:T(1,128)S(1)} %bitcast.13), custom_call_target="tpu_custom_call" | custom-call | flops 1207959552 | bytes 786432 | tf_op jit(solution)/shard_map/inner/pallas_call | solution.py:394
  84.0 0.0 collective-permute-done.2.up_ref
  84.0 3.4 %collective-permute-done.3.down_ref = bf16[272,128]{1,0:T(8,128)(2,1)S(1)} collective-permute-done((bf16[272,128]{1,0:T(8,128)(2,1)S(1)}, bf16[272,128]{1,0:T(8,128)(2,1)S(1)}, u32[]{:S(2)}, u32[]{:S(2)}) %collective-permute-start.3) | collective-permute-done | bytes 69664 | tf_op jit(solution)/shard_map/ppermute | solution.py:388
  87.3 1.4 %outer.1 = bf16[4096,128]{1,0:T(8,128)(2,1)} custom-call(bf16[4096,128]{1,0:T(8,128)(2,1)} %get-tuple-element.41.conv_ref, bf16[4096,128]{1,0:T(8,128)(2,1)S(1)} %get-tuple-element.35.bev_ref, bf16[272,128]{1,0:T(8,128)(2,1)S(1)} %collective-permute-done.2.up_ref, ...), custom_call_target="tpu_custom_call", output_to_operand_aliasing={{}: (0, {})} | custom-call | flops 301989888 | bytes 262144 | tf_op jit(solution)/shard_map/outer/pallas_call | solution.py:394
  88.7 0.0 copy-done.5
  (1 shorter events, 0.0 us)
Async XLA Ops:
  1.3 0.8 copy-start.3
  2.0 0.8 copy-start.4
  2.8 4.5 %copy-start = (bf16[8192,128]{1,0:T(8,128)(2,1)S(1)}, bf16[8192,128]{1,0:T(8,128)(2,1)}, u32[]{:S(2)}) copy-start(bf16[8192,128]{1,0:T(8,128)(2,1)} %feats_ref.1) | copy-start | bytes 6291460
  61.9 19.5 %copy-start.1 = (f32[128]{0:T(128)S(1)}, f32[128]{0:T(128)}, u32[]{:S(2)}) copy-start(f32[128]{0:T(128)} %param.13) | copy-start | bytes 1540
  61.9 19.5 %copy-start.2 = (bf16[3,3,128,128]{3,2,1,0:T(8,128)(2,1)S(1)}, bf16[3,3,128,128]{3,2,1,0:T(8,128)(2,1)}, u32[]{:S(2)}) copy-start(bf16[3,3,128,128]{3,2,1,0:T(8,128)(2,1)} %weight_ref.1) | copy-start | bytes 884740
  74.8 14.0 %copy-start.5 = (bf16[4096,128]{1,0:T(8,128)(2,1)}, bf16[4096,128]{1,0:T(8,128)(2,1)S(1)}, u32[]{:S(2)}) copy-start(bf16[4096,128]{1,0:T(8,128)(2,1)S(1)} %get-tuple-element.35.bev_ref) | copy-start | bytes 3145732
  75.5 8.5 %collective-permute-start.2 = (bf16[272,128]{1,0:T(8,128)(2,1)S(1)}, bf16[272,128]{1,0:T(8,128)(2,1)S(1)}, u32[]{:S(2)}, u32[]{:S(2)}) collective-permute-start(bf16[272,128]{1,0:T(8,128)(2,1)S(1)} %get-tuple-element.42), channel_id=1, source_target_pairs={{0,8},{8,16},{16,24},{24,32},{32,40},{40,48},{48,56},{56,64},{64,7... | collective-permute-start | bytes 208904 | tf_op jit(solution)/shard_map/ppermute | solution.py:388
  79.0 8.3 %collective-permute-start.3 = (bf16[272,128]{1,0:T(8,128)(2,1)S(1)}, bf16[272,128]{1,0:T(8,128)(2,1)S(1)}, u32[]{:S(2)}, u32[]{:S(2)}) collective-permute-start(bf16[272,128]{1,0:T(8,128)(2,1)S(1)} %get-tuple-element.43), channel_id=1, source_target_pairs={{8,0},{16,8},{24,16},{32,24},{40,32},{48,40},{56,48},{64,56},{72,6... | collective-permute-start | bytes 208904 | tf_op jit(solution)/shard_map/ppermute | solution.py:388

commit v12 on v11

--- a/solution.py
+++ b/solution.py
@@ -21,7 +21,7 @@
 PACK_VMEM = 40 * 2**20
 ADD_VMEM = 32 * 2**20
 MOVES = 512
-TOGETHER = 16
+TOGETHER = 32
 
 
 def place_kernel(

time: 88.7 us -> 88.1 us (level)
  no operation moved by 1% of the time
where the time goes in v12:
time: 88.1 us; the launch traced here: 87.9 us
  blocking collectives  48.4 us (55%)
  Pallas kernels  26.8 us (30%)
  starting transfers between devices  5.84 us (7%)
  waiting for transfers between devices  3.25 us (4%)
  between operations  2.04 us (2%)
  local copies, waits for them, and re-layouts  1.53 us (2%)
    all_to_all x1, blocking collectives, shards(): lax.all_to_all(sent, ('gx', 'gy'), split_axis=0, concat_axis=0, tiled=True)  48.4 us
    pallas_call x1, Pallas kernels, add_up(): pl.pallas_call(add_kernel, out_shape=[jax.ShapeDtypeStruct((height, chann...  13 us
    pallas_call x1, Pallas kernels, pack(): pl.pallas_call(pack_kernel, out_shape=jax.ShapeDtypeStruct((devices, BLOC...  5.94 us
    ppermute x2, starting transfers between devices, shift(): return lax.ppermute(cells, axis, pairs)  5.84 us
    pallas_call x2, Pallas kernels, conv_call(): pl.pallas_call(kernel, out_shape=[jax.ShapeDtypeStruct(bev.shape, bf16)]...  4.01 us
    pallas_call x1, Pallas kernels, pack(): pl.pallas_call(functools.partial(place_kernel, across), out_shape=[jax.Sh...  3.9 us
    ppermute x2, waiting for transfers between devices, shift(): return lax.ppermute(cells, axis, pairs)  3.25 us
  transfers between devices with their start and end apart: 2, of which 1 were waited for; matrix products, arithmetic and copies ran while one was open for 0% of the time, Pallas kernels for 3%

profile of v12, /device:TPU:6, one launch (start us, length us, event | category | flops | bytes accessed | tf_op | source)
XLA Modules:
  0.0 87.9 jit_solution(16136436310700945478)
XLA Ops:
  1.3 0.0 copy-start.3
  1.3 0.7 copy-done.3
  2.0 0.0 copy-start.4
  2.0 0.8 copy-done.4
  2.8 0.0 copy-start
  2.8 3.9 %place.1 = (s32[8192]{0:T(1024)S(1)}, s32[1024]{0:T(1024)S(1)}, f32[128,128]{1,0:T(8,128)S(1)}, f32[128,128]{1,0:T(8,128)S(1)}) custom-call(s32[1]{0:T(128)S(6)} %copy.23.count_ref, s32[1,8192]{1,0:T(1,128)S(1)} %bitcast.15, s32[1,8192]{1,0:T(1,128)S(1)} %bitcast.16), custom_call_target="tpu_custom_call" | custom-call | flops 2147483648 | bytes 65536 | tf_op jit(solution)/shard_map/place/pallas_call | solution.py:323
  6.7 0.0 copy-done
  6.7 5.9 %pack.1 = bf16[128,88,128]{2,1,0:T(8,128)(2,1)S(1)} custom-call(s32[1]{0:T(128)S(6)} %copy.23.count_ref, s32[8192]{0:T(1024)S(1)} %get-tuple-element.31.pos_f, s32[1024]{0:T(1024)S(1)} %get-tuple-element.32.twin_f, f32[128,128]{1,0:T(8,128)S(1)} %get-tuple-element.33.high_ref, f32[128,128]{1,0:T(8,128)S(1)} %get-tuple-element.34.low_ref, ...), custom_call_target="tpu_custom_call" | custom-call | tf_op jit(solution)/shard_map/pack/pallas_call | solution.py:343
  12.7 48.4 %all_to_all.5.got_ref = bf16[128,88,128]{2,1,0:T(8,128)(2,1)S(1)} all-to-all(bf16[128,88,128]{2,1,0:T(8,128)(2,1)S(1)} %pack.1), channel_id=1, replica_groups=mesh['gx'=16,'gy'=8] {'gx','gy'}, dimensions={0} | all-to-all | bytes 5767168 | tf_op jit(solution)/shard_map/all_to_all | solution.py:431
  61.1 0.0 copy-start.1
  61.1 0.0 copy-start.2
  61.1 13.0 %add_up.1 = (bf16[4096,128]{1,0:T(8,128)(2,1)S(1)}, bf16[272,128]{1,0:T(8,128)(2,1)S(1)}, bf16[272,128]{1,0:T(8,128)(2,1)S(1)}, bf16[32,128]{1,0:T(8,128)(2,1)S(1)}, s32[1]{0:T(128)}) custom-call(bf16[128,88,128]{2,1,0:T(8,128)(2,1)S(1)} %all_to_all.5.got_ref), custom_call_target="tpu_custom_call" | custom-call | tf_op jit(solution)/shard_map/add_up/pallas_call | solution.py:365
  74.0 0.0 copy-start.5
  74.7 3.4 %collective-permute-start.2 = (bf16[272,128]{1,0:T(8,128)(2,1)S(1)}, bf16[272,128]{1,0:T(8,128)(2,1)S(1)}, u32[]{:S(2)}, u32[]{:S(2)}) collective-permute-start(bf16[272,128]{1,0:T(8,128)(2,1)S(1)} %get-tuple-element.42), channel_id=1, source_target_pairs={{0,8},{8,16},{16,24},{24,32},{32,40},{40,48},{48,56},{56,64},{64,7... | collective-permute-start | bytes 208904 | tf_op jit(solution)/shard_map/ppermute | solution.py:388
  78.1 2.4 %collective-permute-start.3 = (bf16[272,128]{1,0:T(8,128)(2,1)S(1)}, bf16[272,128]{1,0:T(8,128)(2,1)S(1)}, u32[]{:S(2)}, u32[]{:S(2)}) collective-permute-start(bf16[272,128]{1,0:T(8,128)(2,1)S(1)} %get-tuple-element.43), channel_id=1, source_target_pairs={{8,0},{16,8},{24,16},{32,24},{40,32},{48,40},{56,48},{64,56},{72,6... | collective-permute-start | bytes 208904 | tf_op jit(solution)/shard_map/ppermute | solution.py:388
  80.6 0.0 copy-done.1
  80.6 0.0 copy-done.2
  80.6 2.6 %inner.1 = (bf16[4096,128]{1,0:T(8,128)(2,1)}, bf16[512,768]{1,0:T(8,128)(2,1)S(1)}) custom-call(bf16[4096,128]{1,0:T(8,128)(2,1)S(1)} %get-tuple-element.35.bev_ref, bf16[32,128]{1,0:T(8,128)(2,1)S(1)} %get-tuple-element.40.sides_ref, bf16[3,3,128,128]{3,2,1,0:T(8,128)(2,1)S(1)} %copy-done.2, f32[1,128]{1,0:T(1,128)S(1)} %bitcast.13), custom_call_target="tpu_custom_call" | custom-call | flops 1207959552 | bytes 786432 | tf_op jit(solution)/shard_map/inner/pallas_call | solution.py:394
  83.2 0.0 collective-permute-done.2.up_ref
  83.2 3.2 %collective-permute-done.3.down_ref = bf16[272,128]{1,0:T(8,128)(2,1)S(1)} collective-permute-done((bf16[272,128]{1,0:T(8,128)(2,1)S(1)}, bf16[272,128]{1,0:T(8,128)(2,1)S(1)}, u32[]{:S(2)}, u32[]{:S(2)}) %collective-permute-start.3) | collective-permute-done | bytes 69664 | tf_op jit(solution)/shard_map/ppermute | solution.py:388
  86.4 1.4 %outer.1 = bf16[4096,128]{1,0:T(8,128)(2,1)} custom-call(bf16[4096,128]{1,0:T(8,128)(2,1)} %get-tuple-element.41.conv_ref, bf16[4096,128]{1,0:T(8,128)(2,1)S(1)} %get-tuple-element.35.bev_ref, bf16[272,128]{1,0:T(8,128)(2,1)S(1)} %collective-permute-done.2.up_ref, ...), custom_call_target="tpu_custom_call", output_to_operand_aliasing={{}: (0, {})} | custom-call | flops 301989888 | bytes 262144 | tf_op jit(solution)/shard_map/outer/pallas_call | solution.py:394
  87.9 0.0 copy-done.5
  (1 shorter events, 0.0 us)
Async XLA Ops:
  1.3 0.8 copy-start.3
  2.0 0.8 copy-start.4
  2.8 3.9 %copy-start = (bf16[8192,128]{1,0:T(8,128)(2,1)S(1)}, bf16[8192,128]{1,0:T(8,128)(2,1)}, u32[]{:S(2)}) copy-start(bf16[8192,128]{1,0:T(8,128)(2,1)} %feats_ref.1) | copy-start | bytes 6291460
  61.1 19.5 %copy-start.1 = (f32[128]{0:T(128)S(1)}, f32[128]{0:T(128)}, u32[]{:S(2)}) copy-start(f32[128]{0:T(128)} %param.13) | copy-start | bytes 1540
  61.1 19.5 %copy-start.2 = (bf16[3,3,128,128]{3,2,1,0:T(8,128)(2,1)S(1)}, bf16[3,3,128,128]{3,2,1,0:T(8,128)(2,1)}, u32[]{:S(2)}) copy-start(bf16[3,3,128,128]{3,2,1,0:T(8,128)(2,1)} %weight_ref.1) | copy-start | bytes 884740
  74.0 13.8 %copy-start.5 = (bf16[4096,128]{1,0:T(8,128)(2,1)}, bf16[4096,128]{1,0:T(8,128)(2,1)S(1)}, u32[]{:S(2)}) copy-start(bf16[4096,128]{1,0:T(8,128)(2,1)S(1)} %get-tuple-element.35.bev_ref) | copy-start | bytes 3145732
  74.7 8.5 %collective-permute-start.2 = (bf16[272,128]{1,0:T(8,128)(2,1)S(1)}, bf16[272,128]{1,0:T(8,128)(2,1)S(1)}, u32[]{:S(2)}, u32[]{:S(2)}) collective-permute-start(bf16[272,128]{1,0:T(8,128)(2,1)S(1)} %get-tuple-element.42), channel_id=1, source_target_pairs={{0,8},{8,16},{16,24},{24,32},{32,40},{40,48},{48,56},{56,64},{64,7... | collective-permute-start | bytes 208904 | tf_op jit(solution)/shard_map/ppermute | solution.py:388
  78.1 8.3 %collective-permute-start.3 = (bf16[272,128]{1,0:T(8,128)(2,1)S(1)}, bf16[272,128]{1,0:T(8,128)(2,1)S(1)}, u32[]{:S(2)}, u32[]{:S(2)}) collective-permute-start(bf16[272,128]{1,0:T(8,128)(2,1)S(1)} %get-tuple-element.43), channel_id=1, source_target_pairs={{8,0},{16,8},{24,16},{32,24},{40,32},{48,40},{56,48},{64,56},{72,6... | collective-permute-start | bytes 208904 | tf_op jit(solution)/shard_map/ppermute | solution.py:388
